TPU v7x, 32 devices: a whole 2x2x4 slice. The times are simulated.
32 devices in a mesh: row: 8 (over z, core), col: 4 (over y, x).
Axes of the slice: x: 2, y: 2, z: 4, core: 2. Of those that a mesh axis runs over, the one named last changes fastest.
Arguments:
- embedding: bfloat16 [256, 128], P('col'), may hold values from -6 to 6
- dilation: int32 [2], replicated, may hold values from 1 to 4, as said below
- kernel: bfloat16 [3, 3, 48, 128], replicated, may hold values from -0.1875 to 0.1875
- kernel_bias: float32 [48], replicated, may hold values from -3 to 3
- mixing: bfloat16 [5, 48], replicated, may hold values from -0.875 to 0.875
- mixing_bias: float32 [5], replicated, may hold values from -3 to 3
- cotangent: bfloat16 [5, 256, 256], P(None, 'row', 'col'), may hold values from -0.375 to 0.375
Outputs:
- contact: float32 [5, 256, 256], P(None, 'row', 'col')
- embedding_grad: float32 [256, 128], P('col')
- kernel_grad: float32 [3, 3, 48, 128], replicated
Inputs may be any that keep to these rules, and one draw needn't show every extreme that they name: `dilation`: the larger of the two rates is exactly 4.
All inputs are finite; a program needn't handle non-finite values.
Results may differ from a plain program's by a relative error of at most 0.019.
The roundings to bfloat16 on the way count: a program that leaves them out, or rounds other values in their place, can miss the bound.
Values may be sent and summed in bfloat16 or wider, within the bound.
No kernel may reach another device: no remote copies, remote signals or barrier semaphores. Data moves between devices by JAX's collectives and lax.ppermute only.
A program may use at most 64 MiB of HBM per device.

v0:
```python
import jax
import jax.numpy as jnp
from jax import lax
from jax.sharding import PartitionSpec as P

DMAX = 4


def shifted(value, axis, by):
    peers = lax.axis_size(axis)
    pairs = [(i, i + by) for i in range(peers) if 0 <= i + by < peers]
    return lax.ppermute(value, axis, pairs)


def tap_list():
    return [(tap_row, tap_col) for tap_row in (-1, 0, 1) for tap_col in (-1, 0, 1)]


def narrow(values):
    return values.astype(jnp.bfloat16)


def add_into(target, position, update):
    current = lax.dynamic_slice_in_dim(target, position, update.shape[0], 0)
    return lax.dynamic_update_slice_in_dim(target, current + update, position, 0)


def fold_edges(extended, margin, count, before, after):
    inner_rows = extended[margin : margin + count]
    inner_rows = inner_rows + jnp.pad(before, ((0, count - margin), (0, 0)))
    return inner_rows + jnp.pad(after, ((count - margin, 0), (0, 0)))


def per_device(embedding, dilation, kernel, kernel_bias, mixing, mixing_bias, cotangent):
    highest = lax.Precision.HIGHEST
    row_rate = dilation[0]
    col_rate = dilation[1]
    margin = DMAX
    channels = embedding.shape[1]
    filters = kernel.shape[2]
    row_count = cotangent.shape[1]
    col_count = cotangent.shape[2]
    col_devices = lax.axis_size("col")
    bins_total = col_count * col_devices
    row_index = lax.axis_index("row")
    col_index = lax.axis_index("col")
    row_start = row_index * row_count
    col_start = col_index * col_count
    every_bin = lax.all_gather(embedding, "col", axis=0, tiled=True)
    padded = jnp.pad(every_bin, ((margin, margin), (0, 0)))
    row_values = lax.dynamic_slice_in_dim(padded, row_start, row_count + 2 * margin, 0)
    col_values = lax.dynamic_slice_in_dim(padded, col_start, col_count + 2 * margin, 0)
    row_places = row_start - margin + jnp.arange(row_count + 2 * margin, dtype=jnp.int32)
    col_places = col_start - margin + jnp.arange(col_count + 2 * margin, dtype=jnp.int32)
    row_inside = ((row_places >= 0) & (row_places < bins_total)).astype(jnp.float32)
    col_inside = ((col_places >= 0) & (col_places < bins_total)).astype(jnp.float32)
    pairs = narrow(
        0.5
        * (row_values.astype(jnp.float32)[:, None, :] + col_values.astype(jnp.float32)[None, :, :])
    )
    keep_mask = (row_inside[:, None] * col_inside[None, :]).astype(jnp.bfloat16)
    pairs = pairs * keep_mask[:, :, None]
    zero_index = jnp.zeros((), jnp.int32)

    def slicer(tap_row, tap_col, mirrored):
        if mirrored:
            first_at, second_at = (margin + tap_col * col_rate, margin + tap_row * row_rate)
        else:
            first_at, second_at = (margin + tap_row * row_rate, margin + tap_col * col_rate)
        return lax.dynamic_slice(
            pairs, (first_at, second_at, zero_index), (row_count, col_count, channels)
        )

    def convolve(mirrored):
        running = jnp.zeros((filters, row_count, col_count), jnp.float32)
        for tap_row, tap_col in tap_list():
            tap_piece = slicer(tap_row, tap_col, mirrored)
            running = running + jnp.einsum(
                "ijc,fc->fij",
                tap_piece,
                kernel[tap_row + 1, tap_col + 1],
                preferred_element_type=jnp.float32,
            )
        return running + kernel_bias[:, None, None]

    direct = convolve(False)
    mirror = convolve(True)
    direct_act = narrow(jax.nn.relu(direct))
    mirror_act = narrow(jax.nn.relu(mirror))

    def mix_map(activation):
        return (
            jnp.einsum("tf,fij->tij", mixing, activation, preferred_element_type=jnp.float32)
            + mixing_bias[:, None, None]
        )

    contact = 0.5 * mix_map(direct_act) + 0.5 * mix_map(mirror_act)
    guide_grad = narrow(
        0.5 * jnp.einsum("tf,tij->fij", mixing, cotangent, preferred_element_type=jnp.float32)
    )
    grad_direct = jnp.where(direct > 0, guide_grad, jnp.zeros_like(guide_grad))
    grad_mirror = jnp.where(mirror > 0, guide_grad, jnp.zeros_like(guide_grad))
    updates = []
    for tap_row, tap_col in tap_list():
        tap_term = jnp.einsum(
            "fij,ijc->fc",
            grad_direct,
            slicer(tap_row, tap_col, False),
            preferred_element_type=jnp.float32,
        )
        tap_term = tap_term + jnp.einsum(
            "fij,ijc->fc",
            grad_mirror,
            slicer(tap_row, tap_col, True),
            preferred_element_type=jnp.float32,
        )
        updates.append(tap_term)
    kernel_terms = jnp.stack(updates).reshape(3, 3, filters, channels)
    kernel_grad = lax.psum(kernel_terms, ("row", "col"))

    def col_mask(shift):
        return lax.dynamic_slice_in_dim(col_inside, margin + shift, col_count, 0).astype(
            jnp.bfloat16
        )

    def row_mask(shift):
        return lax.dynamic_slice_in_dim(row_inside, margin + shift, row_count, 0).astype(
            jnp.bfloat16
        )

    direct_rows = [
        jnp.einsum(
            "fij,j->fi",
            grad_direct,
            col_mask(tap_step * col_rate),
            preferred_element_type=jnp.float32,
        )
        for tap_step in (-1, 0, 1)
    ]
    direct_cols = [
        jnp.einsum(
            "fij,i->fj",
            grad_direct,
            row_mask(tap_step * row_rate),
            preferred_element_type=jnp.float32,
        )
        for tap_step in (-1, 0, 1)
    ]
    mirror_rows = [
        jnp.einsum(
            "fij,j->fi",
            grad_mirror,
            col_mask(tap_step * row_rate),
            preferred_element_type=jnp.float32,
        )
        for tap_step in (-1, 0, 1)
    ]
    mirror_cols = [
        jnp.einsum(
            "fij,i->fj",
            grad_mirror,
            row_mask(tap_step * col_rate),
            preferred_element_type=jnp.float32,
        )
        for tap_step in (-1, 0, 1)
    ]
    row_grad = jnp.zeros((row_count + 2 * margin, channels), jnp.float32)
    col_grad = jnp.zeros((col_count + 2 * margin, channels), jnp.float32)
    for tap_row, tap_col in tap_list():
        tap_weight = kernel[tap_row + 1, tap_col + 1].astype(jnp.float32)
        row_grad = add_into(
            row_grad,
            margin + tap_row * row_rate,
            jnp.einsum("fi,fc->ic", direct_rows[tap_col + 1], tap_weight, precision=highest),
        )
        row_grad = add_into(
            row_grad,
            margin + tap_col * col_rate,
            jnp.einsum("fi,fc->ic", mirror_rows[tap_row + 1], tap_weight, precision=highest),
        )
        col_grad = add_into(
            col_grad,
            margin + tap_col * col_rate,
            jnp.einsum("fj,fc->jc", direct_cols[tap_row + 1], tap_weight, precision=highest),
        )
        col_grad = add_into(
            col_grad,
            margin + tap_row * row_rate,
            jnp.einsum("fj,fc->jc", mirror_cols[tap_col + 1], tap_weight, precision=highest),
        )
    upper_rows = shifted(row_grad[:margin], "row", -1)
    lower_rows = shifted(row_grad[row_count + margin :], "row", 1)
    inner_rows = fold_edges(row_grad, margin, row_count, lower_rows, upper_rows)
    row_total = lax.psum(inner_rows, "col")
    every_row = lax.all_gather(row_total, "row", axis=0, tiled=True)
    row_share = lax.dynamic_slice_in_dim(every_row, col_start, col_count, 0)
    left_cols = shifted(col_grad[:margin], "col", -1)
    right_cols = shifted(col_grad[col_count + margin :], "col", 1)
    inner_cols = fold_edges(col_grad, margin, col_count, right_cols, left_cols)
    col_total = lax.psum(inner_cols, "row")
    embedding_grad = 0.5 * row_share + 0.5 * col_total
    return (contact, embedding_grad, kernel_grad)


def solution(mesh):
    return jax.shard_map(
        per_device,
        mesh=mesh,
        in_specs=(P("col", None), P(), P(), P(), P(), P(), P(None, "row", "col")),
        out_specs=(P(None, "row", "col"), P("col", None), P()),
        check_vma=False,
    )
```

profile of v0, /device:TPU:0, one launch (start us, length us, event | category | flops | bytes accessed | tf_op | source)
XLA Modules:
  0.0 206.6 jit_solution(6077568537397466937)
XLA Ops:
  7.2 1.3 fusion.300
  13.8 9.9 %all_gather.6 = bf16[256,128]{1,0:T(8,128)(2,1)S(1)} all-gather(bf16[64,128]{1,0:T(8,128)(2,1)} %param.7), channel_id=1, replica_groups=mesh['row'=8,'col'=4] {'col'}, dimensions={0}, use_global_device_ids=true | all-gather | bytes 81920 | tf_op jit(solution)/shard_map/all_gather | solution.py:49
  24.3 0.6 fusion.72
  24.9 0.6 fusion.68
  25.5 0.6 convolution_add_fusion.13
  26.2 0.6 convolution_add_fusion.12
  26.8 0.6 fusion.3
  27.4 0.6 convolution_add_fusion.10
  28.1 0.6 convolution_add_fusion.9
  28.7 0.6 convolution_add_fusion.8
  29.4 0.6 fusion.59
  30.0 0.6 convolution_add_fusion.6
  30.6 0.6 convolution_add_fusion.5
  31.7 0.6 fusion.1
  32.4 0.6 convolution_add_fusion.3
  33.0 0.6 convolution_add_fusion.2
  33.6 0.6 convolution_add_fusion.1
  34.3 0.6 fusion.2
  34.9 0.6 fusion
  46.3 1.3 collective-permute-start.3
  47.6 4.7 %collective-permute-start.2 = (f32[4,128]{1,0:T(4,128)S(1)}, f32[4,128]{1,0:T(4,128)S(1)}, u32[]{:S(2)}, u32[]{:S(2)}) collective-permute-start(f32[4,128]{1,0:T(4,128)S(1)} %get-tuple-element.8), channel_id=1, source_target_pairs={{0,1},{1,2},{2,3},{4,5},{5,6},{6,7},{8,9},{9,10},{10,11},{12,13},{... | collective-permute-start | bytes 6152 | tf_op jit(solution)/shard_map/ppermute | solution.py:12
  52.9 0.5 fusion.270
  61.3 1.3 collective-permute-start.1
  62.6 3.0 %collective-permute-start = (f32[4,128]{1,0:T(4,128)S(1)}, f32[4,128]{1,0:T(4,128)S(1)}, u32[]{:S(2)}, u32[]{:S(2)}) collective-permute-start(f32[4,128]{1,0:T(4,128)S(1)} %get-tuple-element.10), channel_id=1, source_target_pairs={{0,4},{4,8},{8,12},{12,16},{16,20},{20,24},{24,28},{1,5},{5,9},{9,... | collective-permute-start | bytes 6152 | tf_op jit(solution)/shard_map/ppermute | solution.py:12
  71.6 0.7 copy-done.4
  72.6 0.7 copy.11
  73.3 28.4 %psum.22 = f32[64,128]{1,0:T(8,128)S(1)} all-reduce(f32[64,128]{1,0:T(8,128)S(1)} %fusion.93), channel_id=1, replica_groups=mesh['row'=8,'col'=4] {'row'}, use_global_device_ids=true, to_apply=%region_1.2 | all-reduce | flops 8192 | bytes 65536 | tf_op jit(solution)/shard_map/psum | solution.py:200
  101.7 15.8 %psum.21 = f32[32,128]{1,0:T(8,128)S(1)} all-reduce(f32[32,128]{1,0:T(8,128)S(1)} %fusion.95), channel_id=1, replica_groups=mesh['row'=8,'col'=4] {'col'}, use_global_device_ids=true, to_apply=%region_0.1 | all-reduce | flops 4096 | bytes 32768 | tf_op jit(solution)/shard_map/psum | solution.py:194
  117.5 14.0 %all_gather.7 = f32[256,128]{1,0:T(8,128)S(1)} all-gather(f32[32,128]{1,0:T(8,128)S(1)} %psum.21), channel_id=1, replica_groups=mesh['row'=8,'col'=4] {'row'}, dimensions={0}, use_global_device_ids=true | all-gather | bytes 147456 | tf_op jit(solution)/shard_map/all_gather | solution.py:195
  131.5 0.6 add_multiply_fusion
  132.1 66.0 %all-reduce.7.cloned.1.call-done = f32[3,3,48,128]{3,2,1,0:T(8,128)} async-done(((f32[3,3,48,128]{3,2,1,0:T(8,128)}), f32[3,3,48,128]{3,2,1,0:T(8,128)}) %all-reduce.7.cloned.1.call-update) | async-done | bytes 221200 | tf_op jit(solution)/shard_map/psum | solution.py:119
  198.2 1.6 copy.87
  (139 shorter events, 26.1 us)
Async XLA Ops:
  7.2 28.4 %copy-start = (bf16[5,32,64]{2,1,0:T(8,128)(2,1)S(1)}, bf16[5,32,64]{2,1,0:T(8,128)(2,1)}, u32[]{:S(2)}) copy-start(bf16[5,32,64]{2,1,0:T(8,128)(2,1)} %param.13) | copy-start | bytes 61444
  7.2 17.1 %copy-start.1 = (bf16[3,3,48,128]{3,2,1,0:T(8,128)(2,1)S(1)}, bf16[3,3,48,128]{3,2,1,0:T(8,128)(2,1)}, u32[]{:S(2)}) copy-start(bf16[3,3,48,128]{3,2,1,0:T(8,128)(2,1)} %param.9) | copy-start | bytes 331780
  7.2 191.0 %all-reduce.7.cloned.1.call-start = ((), (), s32[]{:S(2)}) async-start(), calls=%async_computation | async-start | bytes 442368 | tf_op jit(solution)/shard_map/psum | solution.py:119
  24.9 1.9 copy-start.2
  30.6 1.1 copy-start.3
  33.6 0.7 copy-start.6
  34.9 0.7 copy-start.5
  46.3 27.0 %collective-permute-start.3 = (f32[4,128]{1,0:T(4,128)S(1)}, f32[4,128]{1,0:T(4,128)S(1)}, u32[]{:S(2)}, u32[]{:S(2)}) collective-permute-start(f32[4,128]{1,0:T(4,128)S(1)} %get-tuple-element.9), channel_id=1, source_target_pairs={{1,0},{2,1},{3,2},{5,4},{6,5},{7,6},{9,8},{10,9},{11,10},{13,12},{... | collective-permute-start | bytes 6152 | tf_op jit(solution)/shard_map/ppermute | solution.py:12
  47.6 25.7 %collective-permute-start.2 = (f32[4,128]{1,0:T(4,128)S(1)}, f32[4,128]{1,0:T(4,128)S(1)}, u32[]{:S(2)}, u32[]{:S(2)}) collective-permute-start(f32[4,128]{1,0:T(4,128)S(1)} %get-tuple-element.8), channel_id=1, source_target_pairs={{0,1},{1,2},{2,3},{4,5},{5,6},{6,7},{8,9},{9,10},{10,11},{12,13},{... | collective-permute-start | bytes 6152 | tf_op jit(solution)/shard_map/ppermute | solution.py:12
  61.3 40.4 %collective-permute-start.1 = (f32[4,128]{1,0:T(4,128)S(1)}, f32[4,128]{1,0:T(4,128)S(1)}, u32[]{:S(2)}, u32[]{:S(2)}) collective-permute-start(f32[4,128]{1,0:T(4,128)S(1)} %get-tuple-element.11), channel_id=1, source_target_pairs={{4,0},{8,4},{12,8},{16,12},{20,16},{24,20},{28,24},{5,1},{9,5},{13... | collective-permute-start | bytes 6152 | tf_op jit(solution)/shard_map/ppermute | solution.py:12
  62.6 39.1 %collective-permute-start = (f32[4,128]{1,0:T(4,128)S(1)}, f32[4,128]{1,0:T(4,128)S(1)}, u32[]{:S(2)}, u32[]{:S(2)}) collective-permute-start(f32[4,128]{1,0:T(4,128)S(1)} %get-tuple-element.10), channel_id=1, source_target_pairs={{0,4},{4,8},{8,12},{12,16},{16,20},{20,24},{24,28},{1,5},{5,9},{9,... | collective-permute-start | bytes 6152 | tf_op jit(solution)/shard_map/ppermute | solution.py:12
  71.2 1.1 copy-start.7
  71.6 0.7 copy-start.4
Sparse Core Ops, SparseCore 0:
  72.4 125.7 all-reduce.6
where the time goes:
time: 207 us
  blocking collectives  68 us (33%)
  waiting for transfers between devices  66.1 us (32%)
  matrix products  27.7 us (13%)
  between operations  20.2 us (10%)
  local copies, waits for them, and re-layouts  13 us (6%)
  starting transfers between devices  10.4 us (5%)
    psum x1, waiting for transfers between devices, per_device(): kernel_grad = lax.psum(kernel_terms, ('row', 'col'))  66 us
    psum x1, blocking collectives, per_device(): col_total = lax.psum(inner_cols, 'row')  28.4 us
    psum x1, blocking collectives, per_device(): row_total = lax.psum(inner_rows, 'col')  15.8 us
    all_gather x1, blocking collectives, per_device(): every_row = lax.all_gather(row_total, 'row', axis=0, tiled=True)  14 us
    dot_general x17, matrix products, convolve(): jnp.einsum('ijc,fc->fij', tap_piece, kernel[tap_row + 1, tap_col + 1], pr...  10.5 us
    ppermute x4, starting transfers between devices, shifted(): return lax.ppermute(value, axis, pairs)  10.3 us
    all_gather x1, blocking collectives, per_device(): every_bin = lax.all_gather(embedding, 'col', axis=0, tiled=True)  9.88 us
    dynamic_update_slice x36, local copies, waits for them, and re-layouts, add_into(): lax.dynamic_update_slice_in_dim(target, current + update, position, 0)  8.11 us
  transfers between devices with their start and end apart: 5, of which 1 were waited for; matrix products, arithmetic and copies ran while one was open for 8% of the time, Pallas kernels for 0%

commit v1 on v0

v1 whole, which is shorter than its diff:
```python
import functools

import jax
import jax.numpy as jnp
from jax import lax
from jax.experimental import pallas as pl
from jax.experimental.pallas import tpu as pltpu
from jax.sharding import PartitionSpec as P

DMAX = 4
PAD = 8
STEPS = (-1, 0, 1)
LANES = 128


def contract(left, right, dims):
    return lax.dot_general(left, right, (dims, ((), ())), preferred_element_type=jnp.float32)


def local_kernel(
    sizes,
    dilation_ref,
    *refs,
):
    peers, rows, cols, bins, filters, half = sizes
    block_refs = refs[:peers]
    kernel_ref, bias_ref, mix_ref, mix_bias_ref, cot_ref = refs[peers : peers + 5]
    contact_ref, send_ref, keep_ref = refs[peers + 5 : peers + 8]
    bins_ref, x_ref, weight_ref, grad_ref, wide_ref, acc_ref, taps_ref = refs[peers + 8 :]
    row_rate = dilation_ref[0]
    col_rate = dilation_ref[1]
    row_index = lax.axis_index("row")
    col_index = lax.axis_index("col")
    row_start = row_index * rows
    col_start = col_index * cols
    core = lax.rem(row_index, 2)
    taps = [(a, b) for a in STEPS for b in STEPS]
    count = len(taps)
    mirror_lane = LANES // 2
    bf16 = jnp.bfloat16
    f32 = jnp.float32

    bins_ref[0:PAD, :] = jnp.zeros((PAD, LANES), f32)
    bins_ref[bins + PAD : bins + 2 * PAD, :] = jnp.zeros((PAD, LANES), f32)
    for step in range(peers):
        place = pl.multiple_of(jnp.bitwise_xor(col_index, step) * cols + PAD, 8)
        bins_ref[pl.ds(place, cols), :] = 0.5 * block_refs[step][...].astype(f32)

    weight_ref[...] = jnp.zeros_like(weight_ref)
    wide_ref[...] = jnp.zeros_like(wide_ref)
    for at, (a, b) in enumerate(taps):
        tap = kernel_ref[at]
        weight_ref[0:filters, at * LANES : (at + 1) * LANES] = tap
        weight_ref[mirror_lane : mirror_lane + filters, (count + at) * LANES : (count + at + 1) * LANES] = tap
        first = (b + 1) * LANES
        wide_ref[first : first + filters, (a + 1) * LANES : (a + 2) * LANES] = tap
        first = (a + 1) * LANES + mirror_lane
        wide_ref[first : first + filters, (b + 4) * LANES : (b + 5) * LANES] = tap

    col_lane = lax.broadcasted_iota(jnp.int32, (cols, LANES), 0) + col_start

    def col_values(shift):
        values = bins_ref[pl.ds(col_start + PAD + shift, cols), :]
        place = col_lane + shift
        keep = ((place >= 0) & (place < bins)).astype(f32)
        return values, keep

    for at in range(2 * count):
        mirrored = at >= count
        a, b = taps[at % count]
        row_shift = b * col_rate if mirrored else a * row_rate
        col_shift = a * row_rate if mirrored else b * col_rate
        values, keep = col_values(col_shift)
        for i in range(rows):
            row = bins_ref[pl.ds(row_start + PAD + row_shift + i, 1), :]
            piece = (row + values) * keep
            if i < DMAX or i >= rows - DMAX:
                place = row_start + row_shift + i
                inside = (place >= 0) & (place < bins)
                piece = piece * inside.astype(f32)
            x_ref[i * cols : (i + 1) * cols, at * LANES : (at + 1) * LANES] = piece.astype(bf16)

    conv = contract(x_ref[...], weight_ref[...], ((1,), (1,))) + bias_ref[...]
    guide = contract(cot_ref[...], mix_ref[...], ((0,), (0,))).astype(bf16)
    grad = jnp.where(conv > 0, guide.astype(f32), 0.0)
    grad_ref[...] = grad
    active = jnp.maximum(conv, 0.0).astype(bf16)
    mixed = contract(mix_ref[...], active, ((1,), (1,)))
    contact_ref[...] = mixed[0:8] + mix_bias_ref[...]

    grad16 = grad.astype(bf16)
    turned = grad16.T
    kernel_terms = contract(turned[0:filters], x_ref[:, : count * LANES], ((1,), (0,)))
    kernel_terms = kernel_terms + contract(
        turned[mirror_lane : mirror_lane + filters], x_ref[:, count * LANES :], ((1,), (0,))
    )
    for at in range(count):
        taps_ref[at * filters : (at + 1) * filters, :] = kernel_terms[:, at * LANES : (at + 1) * LANES]

    is_mirror = lax.broadcasted_iota(jnp.int32, (1, LANES), 1) >= mirror_lane
    row_sums = []
    col_sums = []
    for q in STEPS:
        place = col_lane + jnp.where(is_mirror, q * row_rate, q * col_rate)
        keep = ((place >= 0) & (place < bins)).astype(f32)
        sums = [
            jnp.sum(grad_ref[i * cols : (i + 1) * cols, :] * keep, axis=0, keepdims=True)
            for i in range(rows)
        ]
        row_sums.append(jnp.concatenate(sums, axis=0))
        total = None
        for i in range(rows):
            place = row_start + i + jnp.where(is_mirror, q * col_rate, q * row_rate)
            keep = ((place >= 0) & (place < bins)).astype(f32)
            term = grad_ref[i * cols : (i + 1) * cols, :] * keep
            total = term if total is None else total + term
        col_sums.append(pltpu.roll(total, mirror_lane, 1))
    sums = jnp.concatenate(
        [jnp.concatenate(row_sums, axis=1), jnp.concatenate(col_sums, axis=1)], axis=0
    ).astype(bf16)
    spread = contract(sums, wide_ref[...], ((1,), (0,)))
    acc_ref[...] = jnp.zeros_like(acc_ref)
    for group in range(6):
        shift = STEPS[group % 3] * (row_rate if group < 3 else col_rate)
        piece = spread[:, group * LANES : (group + 1) * LANES]
        where = pl.ds(row_start + PAD + shift, rows)
        acc_ref[where, :] = acc_ref[where, :] + piece[0:rows]
        where = pl.ds(col_start + PAD + shift, cols)
        acc_ref[where, :] = acc_ref[where, :] + piece[rows : rows + cols]

    total_rows = count * filters
    for target, which in ((keep_ref, core), (send_ref, 1 - core)):
        first = pl.multiple_of(which * (total_rows - half), 16)
        target[0:half, :] = taps_ref[pl.ds(first, half), :].astype(bf16)
        part = cols // 2
        for step in range(peers):
            first = pl.multiple_of(which * part + (step * cols + PAD), 8)
            target[half + step * part : half + (step + 1) * part, :] = (
                0.5 * acc_ref[pl.ds(first, part), :]
            ).astype(bf16)


def swap(value, axis, mask):
    peers = lax.axis_size(axis)
    return lax.ppermute(value, axis, [(i, i ^ mask) for i in range(peers)])


def per_device(embedding, dilation, kernel, kernel_bias, mixing, mixing_bias, cotangent):
    f32 = jnp.float32
    bf16 = jnp.bfloat16
    filters, channels = kernel.shape[2:]
    maps, rows, cols = cotangent.shape
    peers = lax.axis_size("col")
    row_peers = lax.axis_size("row")
    bins = cols * peers
    core = lax.rem(lax.axis_index("row"), 2)
    col_index = lax.axis_index("col")
    blocks = [embedding] + [swap(embedding, "col", mask) for mask in range(1, peers)]
    spare = LANES // 2 - filters
    taps = 9
    taps_rows = taps * filters
    half = (taps_rows // 2 + 15) // 16 * 16

    def twice(value):
        wide = jnp.pad(value, ((0, 0), (0, spare)))
        return jnp.concatenate([wide, wide], axis=1)

    bias = twice(kernel_bias[None, :])
    mix = jnp.pad(twice(0.5 * mixing), ((0, 16 - maps), (0, 0))).astype(bf16)
    mix_bias = jnp.pad(mixing_bias, (0, 8 - maps))[:, None]
    cot = jnp.pad(cotangent.reshape(maps, rows * cols), ((0, 16 - maps), (0, 0)))
    packed = half + peers * cols // 2
    vmem = pl.BlockSpec(memory_space=pltpu.VMEM)
    contact, send, keep = pl.pallas_call(
        functools.partial(local_kernel, (peers, rows, cols, bins, filters, half)),
        out_shape=(
            jax.ShapeDtypeStruct((8, rows * cols), f32),
            jax.ShapeDtypeStruct((packed, LANES), bf16),
            jax.ShapeDtypeStruct((packed, LANES), bf16),
        ),
        in_specs=[pl.BlockSpec(memory_space=pltpu.SMEM)] + [vmem] * (peers + 5),
        out_specs=(vmem, vmem, vmem),
        scratch_shapes=[
            pltpu.VMEM((bins + 2 * PAD, LANES), f32),
            pltpu.VMEM((rows * cols, 2 * taps * LANES), bf16),
            pltpu.VMEM((LANES, 2 * taps * LANES), bf16),
            pltpu.VMEM((rows * cols, LANES), f32),
            pltpu.VMEM((3 * LANES, 6 * LANES), bf16),
            pltpu.VMEM((bins + 2 * PAD, LANES), f32),
            pltpu.VMEM((taps_rows, LANES), f32),
        ],
        name="contact_head",
    )(dilation, *blocks, kernel.reshape(taps, filters, channels), bias, mix, mix_bias, cot)

    total = keep + swap(send, "row", 1)
    mask = 1
    while mask < peers:
        total = total + swap(total, "col", mask)
        mask *= 2
    mask = 2
    while mask < row_peers:
        total = total + swap(total, "row", mask)
        mask *= 2
    part = cols // 2
    mine = lax.dynamic_slice_in_dim(total[half:], col_index * part, part, 0)
    mine = jnp.concatenate([total[:half], mine], axis=0)
    other = swap(mine, "row", 1)
    low = jnp.where(core == 0, mine, other).astype(f32)
    high = jnp.where(core == 0, other, mine).astype(f32)
    kernel_grad = jnp.concatenate([low[: taps_rows - half], high[:half]], axis=0)
    embedding_grad = jnp.concatenate([low[half:], high[half:]], axis=0)
    return (
        contact[:maps].reshape(maps, rows, cols),
        embedding_grad,
        kernel_grad.reshape(kernel.shape),
    )


def solution(mesh):
    return jax.shard_map(
        per_device,
        mesh=mesh,
        in_specs=(P("col", None), P(), P(), P(), P(), P(), P(None, "row", "col")),
        out_specs=(P(None, "row", "col"), P("col", None), P()),
        check_vma=False,
    )
```

time: 207 us -> 45.5 us (0.22)
  blocking collectives: 68 us -> 0 us
  waiting for transfers between devices: 66.1 us -> 15.9 us
  matrix products: 27.7 us -> 0 us
  between operations: 20.2 us -> 0.79 us
  Pallas kernels: 0 us -> 9.45 us
  local copies, waits for them, and re-layouts: 13 us -> 4.31 us
  other arithmetic: 1.24 us -> 3.71 us
    psum x1 -> x0, waiting for transfers between devices: 66 us -> none  [per_device(): kernel_grad = lax.psum(kernel_terms, ('row', 'col'))]
    psum x2 -> x0, blocking collectives: 44.2 us -> none  [the longest x1 28.4 us: per_device(): col_total = lax.psum(inner_cols, 'row')]
    dot_general x86 -> x0, matrix products: 27.7 us -> none  [the longest x17 10.5 us: convolve(): jnp.einsum('ijc,fc->fij', tap_piece, kernel[tap_row + 1, tap_col + 1], pr...]
    all_gather x2 -> x0, blocking collectives: 23.8 us -> none  [the longest x1 14 us: per_device(): every_row = lax.all_gather(row_total, 'row', axis=0, tiled=True)]
    ppermute x4 -> x9, waiting for transfers between devices: 0.01 us -> 15.9 us  [swap(): return lax.ppermute(value, axis, [(i, i ^ mask) for i in range(peers)])]
    pallas_call x0 -> x1, Pallas kernels: none -> 9.45 us  [per_device(): pl.pallas_call(functools.partial(local_kernel, (peers, rows, cols, bins,...]
    dynamic_update_slice x36 -> x0, local copies, waits for them, and re-layouts: 8.11 us -> none  [add_into(): lax.dynamic_update_slice_in_dim(target, current + update, position, 0)]
    concatenate x0 -> x5, other arithmetic: none -> 2.66 us  [the longest x2 1.34 us: twice(): return jnp.concatenate([wide, wide], axis=1)]
  transfers between devices with their start and end apart: 5 -> 9, of which waited for: 1 -> 6; matrix products, arithmetic and copies ran while one was open for 8% -> 9% of each run, Pallas kernels for 0% -> 0%
where the time goes in v1:
time: 45.5 us; the launch traced here: 45.2 us
  waiting for transfers between devices  15.9 us (35%)
  starting transfers between devices  11 us (24%)
  Pallas kernels  9.45 us (21%)
  local copies, waits for them, and re-layouts  4.31 us (9%)
  other arithmetic  3.71 us (8%)
  between operations  0.79 us (2%)
    ppermute x9, waiting for transfers between devices, swap(): return lax.ppermute(value, axis, [(i, i ^ mask) for i in range(peers)])  15.9 us
    ppermute x9, starting transfers between devices, swap(): return lax.ppermute(value, axis, [(i, i ^ mask) for i in range(peers)])  11 us
    pallas_call x1, Pallas kernels, per_device(): pl.pallas_call(functools.partial(local_kernel, (peers, rows, cols, bins,...  9.45 us
    unnamed x14, local copies, waits for them, and re-layouts  1.35 us
    concatenate x2, other arithmetic, twice(): return jnp.concatenate([wide, wide], axis=1)  1.34 us
    add x1, other arithmetic, per_device(): total = keep + swap(send, 'row', 1)  0.92 us
  transfers between devices with their start and end apart: 9, of which 6 were waited for; matrix products, arithmetic and copies ran while one was open for 9% of the time, Pallas kernels for 0%

profile of v1, /device:TPU:0, one launch (start us, length us, event | category | flops | bytes accessed | tf_op | source)
XLA Modules:
  0.0 45.2 jit_solution(5933350917967172654)
XLA Ops:
  0.6 3.1 %collective-permute-start.1 = (bf16[64,128]{1,0:T(8,128)(2,1)}, bf16[64,128]{1,0:T(8,128)(2,1)S(1)}, u32[]{:S(2)}, u32[]{:S(2)}) collective-permute-start(bf16[64,128]{1,0:T(8,128)(2,1)} %refs_0_.1), channel_id=1, source_target_pairs={{0,2},{1,3},{2,0},{3,1},{4,6},{5,7},{6,4},{7,5},{8,10},{9,11},{10,... | collective-permute-start | bytes 49160 | tf_op jit(solution)/shard_map/ppermute | solution.py:145
  3.7 1.5 %collective-permute-start = (bf16[64,128]{1,0:T(8,128)(2,1)}, bf16[64,128]{1,0:T(8,128)(2,1)S(1)}, u32[]{:S(2)}, u32[]{:S(2)}) collective-permute-start(bf16[64,128]{1,0:T(8,128)(2,1)} %refs_0_.1), channel_id=1, source_target_pairs={{0,1},{1,0},{2,3},{3,2},{4,5},{5,4},{6,7},{7,6},{8,9},{9,8},{10,11... | collective-permute-start | bytes 49160 | tf_op jit(solution)/shard_map/ppermute | solution.py:145
  5.2 0.1 collective-permute-start.2
  5.3 0.7 %pad_maximum_fusion.3.refs_5_ = f32[1,128]{1,0:T(1,128)} fusion(f32[1,64]{1,0:T(1,128)S(1)} %pad.20), kind=kLoop, calls=%fused_computation.10 | loop fusion | flops 128 | bytes 768 | tf_op jit(solution)/shard_map/concatenate | solution.py:166
  5.9 0.0 copy-done.4
  6.0 0.7 %fusion.2.refs_6_ = bf16[16,128]{1,0:T(8,128)(2,1)} fusion(bf16[5,64]{1,0:T(8,128)(2,1)S(1)} %pad.21), kind=kLoop, calls=%fused_computation.8 | loop fusion | flops 14336 | bytes 4736 | tf_op jit(solution)/shard_map/concatenate | solution.py:166
  6.6 0.7 %copy.10.refs_7_ = f32[8,1]{1,0:T(8,128)} copy(f32[8,1]{0,1:T(1,128)S(1)} %pad_bitcast_fusion) | data formatting | bytes 64 | tf_op jit(solution)/shard_map/broadcast_in_dim | solution.py:170
  7.3 0.9 %reshape.19 = bf16[5,2048]{1,0:T(8,128)(2,1)S(1)} reshape(bf16[5,32,64]{2,1,0:T(8,128)(2,1)} %param.13) | data formatting | bytes 40960 | tf_op jit(solution)/shard_map/reshape | solution.py:171
  8.2 0.6 %pad.24.refs_8_ = bf16[16,2048]{1,0:T(8,128)(2,1)} pad(bf16[5,2048]{1,0:T(8,128)(2,1)S(1)} %reshape.19, bf16[]{:T(256)} %constant.17.clone.1), padding=0_11x0_0 | pad | bytes 86018 | tf_op jit(solution)/shard_map/jit(_pad)/pad | solution.py:171
  8.8 0.0 collective-permute-done.1.refs_2_
  8.8 0.0 collective-permute-done.refs_1_
  8.8 0.0 copy-start.2
  8.8 1.2 %collective-permute-done.2.refs_3_ = bf16[64,128]{1,0:T(8,128)(2,1)S(1)} collective-permute-done((bf16[64,128]{1,0:T(8,128)(2,1)}, bf16[64,128]{1,0:T(8,128)(2,1)S(1)}, u32[]{:S(2)}, u32[]{:S(2)}) %collective-permute-start.2) | collective-permute-done | bytes 16416 | tf_op jit(solution)/shard_map/ppermute | solution.py:145
  10.0 0.6 %copy-done.3 = bf16[64,128]{1,0:T(8,128)(2,1)} copy-done((bf16[64,128]{1,0:T(8,128)(2,1)}, bf16[64,128]{1,0:T(8,128)(2,1)S(1)}, u32[]{:S(2)}) %copy-start.3) | copy-done | bytes 16408
  10.6 9.5 %contact_head.1 = (f32[8,2048]{1,0:T(8,128)}, bf16[352,128]{1,0:T(8,128)(2,1)}, bf16[352,128]{1,0:T(8,128)(2,1)}) custom-call(s32[2]{0:T(128)} %dilation_ref.1, bf16[64,128]{1,0:T(8,128)(2,1)} %refs_0_.1, bf16[64,128]{1,0:T(8,128)(2,1)} %copy-done.2, bf16[64,128]{1,0:T(8,128)(2,1)} %copy-done.1, bf16[64,128]{1,0:T(8,128)(2,1)} %copy-done.3, ...), custom_call_target="tpu_custom_call" | custom-call | tf_op jit(solution)/shard_map/contact_head/pallas_call | solution.py:174
  20.1 0.0 collective-permute-start.3
  20.1 1.5 %collective-permute-done.3 = bf16[352,128]{1,0:T(8,128)(2,1)S(1)} collective-permute-done((bf16[352,128]{1,0:T(8,128)(2,1)}, bf16[352,128]{1,0:T(8,128)(2,1)S(1)}, u32[]{:S(2)}, u32[]{:S(2)}) %collective-permute-start.3) | collective-permute-done | bytes 90144 | tf_op jit(solution)/shard_map/ppermute | solution.py:145
  21.6 0.9 %add.28 = bf16[352,128]{1,0:T(8,128)(2,1)S(1)} add(bf16[352,128]{1,0:T(8,128)(2,1)} %get-tuple-element.7, bf16[352,128]{1,0:T(8,128)(2,1)S(1)} %collective-permute-done.3) | non-fusion elementwise | flops 45056 | bytes 270336 | tf_op jit(solution)/shard_map/add | solution.py:195
  22.5 0.8 %collective-permute-start.4 = (bf16[352,128]{1,0:T(8,128)(2,1)S(1)}, bf16[352,128]{1,0:T(8,128)(2,1)S(1)}, u32[]{:S(2)}, u32[]{:S(2)}) collective-permute-start(bf16[352,128]{1,0:T(8,128)(2,1)S(1)} %add.28), channel_id=1, source_target_pairs={{0,1},{1,0},{2,3},{3,2},{4,5},{5,4},{6,7},{7,6},{8,9},{9,8},{10,11... | collective-permute-start | bytes 270344 | tf_op jit(solution)/shard_map/ppermute | solution.py:145
  23.3 3.9 %collective-permute-done.4 = bf16[352,128]{1,0:T(8,128)(2,1)S(1)} collective-permute-done((bf16[352,128]{1,0:T(8,128)(2,1)S(1)}, bf16[352,128]{1,0:T(8,128)(2,1)S(1)}, u32[]{:S(2)}, u32[]{:S(2)}) %collective-permute-start.4) | collective-permute-done | bytes 90144 | tf_op jit(solution)/shard_map/ppermute | solution.py:145
  27.3 0.8 %collective-permute-start.5 = (bf16[352,128]{1,0:T(8,128)(2,1)S(1)}, bf16[352,128]{1,0:T(8,128)(2,1)S(1)}, u32[]{:S(2)}, u32[]{:S(2)}) collective-permute-start(bf16[352,128]{1,0:T(8,128)(2,1)S(1)} %add.29), channel_id=1, source_target_pairs={{0,2},{1,3},{2,0},{3,1},{4,6},{5,7},{6,4},{7,5},{8,10},{9,11},{10,... | collective-permute-start | bytes 270344 | tf_op jit(solution)/shard_map/ppermute | solution.py:145
  28.1 3.8 %collective-permute-done.5 = bf16[352,128]{1,0:T(8,128)(2,1)S(1)} collective-permute-done((bf16[352,128]{1,0:T(8,128)(2,1)S(1)}, bf16[352,128]{1,0:T(8,128)(2,1)S(1)}, u32[]{:S(2)}, u32[]{:S(2)}) %collective-permute-start.5) | collective-permute-done | bytes 90144 | tf_op jit(solution)/shard_map/ppermute | solution.py:145
  31.9 1.6 %collective-permute-start.6 = (bf16[352,128]{1,0:T(8,128)(2,1)S(1)}, bf16[352,128]{1,0:T(8,128)(2,1)S(1)}, u32[]{:S(2)}, u32[]{:S(2)}) collective-permute-start(bf16[352,128]{1,0:T(8,128)(2,1)S(1)} %add.30), channel_id=1, source_target_pairs={{0,8},{4,12},{8,0},{12,4},{16,24},{20,28},{24,16},{28,20},{1,9},{5... | collective-permute-start | bytes 270344 | tf_op jit(solution)/shard_map/ppermute | solution.py:145
  33.5 3.0 %collective-permute-done.6 = bf16[352,128]{1,0:T(8,128)(2,1)S(1)} collective-permute-done((bf16[352,128]{1,0:T(8,128)(2,1)S(1)}, bf16[352,128]{1,0:T(8,128)(2,1)S(1)}, u32[]{:S(2)}, u32[]{:S(2)}) %collective-permute-start.6) | collective-permute-done | bytes 90144 | tf_op jit(solution)/shard_map/ppermute | solution.py:145
  36.5 3.1 %collective-permute-start.7 = (bf16[352,128]{1,0:T(8,128)(2,1)S(1)}, bf16[352,128]{1,0:T(8,128)(2,1)S(1)}, u32[]{:S(2)}, u32[]{:S(2)}) collective-permute-start(bf16[352,128]{1,0:T(8,128)(2,1)S(1)} %add.31), channel_id=1, source_target_pairs={{0,16},{4,20},{8,24},{12,28},{16,0},{20,4},{24,8},{28,12},{1,17},{... | collective-permute-start | bytes 270344 | tf_op jit(solution)/shard_map/ppermute | solution.py:145
  39.6 2.5 %collective-permute-done.7 = bf16[352,128]{1,0:T(8,128)(2,1)S(1)} collective-permute-done((bf16[352,128]{1,0:T(8,128)(2,1)S(1)}, bf16[352,128]{1,0:T(8,128)(2,1)S(1)}, u32[]{:S(2)}, u32[]{:S(2)}) %collective-permute-start.7) | collective-permute-done | bytes 90144 | tf_op jit(solution)/shard_map/ppermute | solution.py:145
  42.2 0.1 collective-permute-start.8
  42.3 0.7 %copy-done = f32[8,2048]{1,0:T(8,128)S(1)} copy-done((f32[8,2048]{1,0:T(8,128)S(1)}, f32[8,2048]{1,0:T(8,128)}, u32[]{:S(2)}) %copy-start) | copy-done | bytes 65560
  43.0 0.7 %reshape.20 = f32[5,32,64]{2,1,0:T(8,128)} reshape(f32[5,2048]{1,0:T(8,128)S(1)} %bitcast.8) | data formatting | bytes 81920 | tf_op jit(solution)/shard_map/reshape | solution.py:213
  43.8 0.0 collective-permute-done.8
  43.8 0.7 %pad_maximum_fusion = f32[432,128]{1,0:T(8,128)} fusion(f32[224,128]{1,0:T(8,128)S(1)} %slice.33, f32[208,128]{1,0:T(8,128)S(1)} %slice.32), kind=kLoop, calls=%fused_computation | loop fusion | flops 55296 | bytes 442368 | tf_op jit(solution)/shard_map/concatenate | solution.py:210
  44.5 0.6 %pad_maximum_fusion.2 = f32[64,128]{1,0:T(8,128)} fusion(f32[32,128]{1,0:T(8,128)S(1)} %slice.31, f32[32,128]{1,0:T(8,128)S(1)} %slice.30), kind=kLoop, calls=%fused_computation.4 | loop fusion | flops 8192 | bytes 65536 | tf_op jit(solution)/shard_map/concatenate | solution.py:211
  (27 shorter events, 0.2 us)
Async XLA Ops:
  0.6 4.6 %copy-start.5 = (f32[48]{0:T(128)S(1)}, f32[48]{0:T(128)}, u32[]{:S(2)}) copy-start(f32[48]{0:T(128)} %param.10) | copy-start | bytes 580
  0.6 8.2 %collective-permute-start.1 = (bf16[64,128]{1,0:T(8,128)(2,1)}, bf16[64,128]{1,0:T(8,128)(2,1)S(1)}, u32[]{:S(2)}, u32[]{:S(2)}) collective-permute-start(bf16[64,128]{1,0:T(8,128)(2,1)} %refs_0_.1), channel_id=1, source_target_pairs={{0,2},{1,3},{2,0},{3,1},{4,6},{5,7},{6,4},{7,5},{8,10},{9,11},{10,... | collective-permute-start | bytes 49160 | tf_op jit(solution)/shard_map/ppermute | solution.py:145
  3.7 5.1 %collective-permute-start = (bf16[64,128]{1,0:T(8,128)(2,1)}, bf16[64,128]{1,0:T(8,128)(2,1)S(1)}, u32[]{:S(2)}, u32[]{:S(2)}) collective-permute-start(bf16[64,128]{1,0:T(8,128)(2,1)} %refs_0_.1), channel_id=1, source_target_pairs={{0,1},{1,0},{2,3},{3,2},{4,5},{5,4},{6,7},{7,6},{8,9},{9,8},{10,11... | collective-permute-start | bytes 49160 | tf_op jit(solution)/shard_map/ppermute | solution.py:145
  5.2 4.8 %collective-permute-start.2 = (bf16[64,128]{1,0:T(8,128)(2,1)}, bf16[64,128]{1,0:T(8,128)(2,1)S(1)}, u32[]{:S(2)}, u32[]{:S(2)}) collective-permute-start(bf16[64,128]{1,0:T(8,128)(2,1)} %refs_0_.1), channel_id=1, source_target_pairs={{0,3},{1,2},{2,1},{3,0},{4,7},{5,6},{6,5},{7,4},{8,11},{9,10},{10,... | collective-permute-start | bytes 49160 | tf_op jit(solution)/shard_map/ppermute | solution.py:145
  5.2 0.7 %copy-start.4 = (bf16[5,48]{1,0:T(8,128)(2,1)S(1)}, bf16[5,48]{1,0:T(8,128)(2,1)}, u32[]{:S(2)}) copy-start(bf16[5,48]{1,0:T(8,128)(2,1)} %param.11) | copy-start | bytes 1444
  5.9 0.7 %copy-start.6 = (f32[5]{0:T(128)S(1)}, f32[5]{0:T(128)}, u32[]{:S(2)}) copy-start(f32[5]{0:T(128)} %param.12) | copy-start | bytes 64
  8.8 1.2 %copy-start.1 = (bf16[64,128]{1,0:T(8,128)(2,1)}, bf16[64,128]{1,0:T(8,128)(2,1)S(1)}, u32[]{:S(2)}) copy-start(bf16[64,128]{1,0:T(8,128)(2,1)S(1)} %collective-permute-done.1.refs_2_) | copy-start | bytes 49156
  8.8 1.2 %copy-start.2 = (bf16[64,128]{1,0:T(8,128)(2,1)}, bf16[64,128]{1,0:T(8,128)(2,1)S(1)}, u32[]{:S(2)}) copy-start(bf16[64,128]{1,0:T(8,128)(2,1)S(1)} %collective-permute-done.refs_1_) | copy-start | bytes 49156
  10.0 0.6 %copy-start.3 = (bf16[64,128]{1,0:T(8,128)(2,1)}, bf16[64,128]{1,0:T(8,128)(2,1)S(1)}, u32[]{:S(2)}) copy-start(bf16[64,128]{1,0:T(8,128)(2,1)S(1)} %collective-permute-done.2.refs_3_) | copy-start | bytes 49156
  20.1 1.5 %collective-permute-start.3 = (bf16[352,128]{1,0:T(8,128)(2,1)}, bf16[352,128]{1,0:T(8,128)(2,1)S(1)}, u32[]{:S(2)}, u32[]{:S(2)}) collective-permute-start(bf16[352,128]{1,0:T(8,128)(2,1)} %get-tuple-element.8), channel_id=1, source_target_pairs={{0,4},{4,0},{8,12},{12,8},{16,20},{20,16},{24,28},{28,24},{1,5},{5... | collective-permute-start | bytes 270344 | tf_op jit(solution)/shard_map/ppermute | solution.py:145
  22.5 4.7 %collective-permute-start.4 = (bf16[352,128]{1,0:T(8,128)(2,1)S(1)}, bf16[352,128]{1,0:T(8,128)(2,1)S(1)}, u32[]{:S(2)}, u32[]{:S(2)}) collective-permute-start(bf16[352,128]{1,0:T(8,128)(2,1)S(1)} %add.28), channel_id=1, source_target_pairs={{0,1},{1,0},{2,3},{3,2},{4,5},{5,4},{6,7},{7,6},{8,9},{9,8},{10,11... | collective-permute-start | bytes 270344 | tf_op jit(solution)/shard_map/ppermute | solution.py:145
  27.3 4.6 %collective-permute-start.5 = (bf16[352,128]{1,0:T(8,128)(2,1)S(1)}, bf16[352,128]{1,0:T(8,128)(2,1)S(1)}, u32[]{:S(2)}, u32[]{:S(2)}) collective-permute-start(bf16[352,128]{1,0:T(8,128)(2,1)S(1)} %add.29), channel_id=1, source_target_pairs={{0,2},{1,3},{2,0},{3,1},{4,6},{5,7},{6,4},{7,5},{8,10},{9,11},{10,... | collective-permute-start | bytes 270344 | tf_op jit(solution)/shard_map/ppermute | solution.py:145
  31.9 4.6 %collective-permute-start.6 = (bf16[352,128]{1,0:T(8,128)(2,1)S(1)}, bf16[352,128]{1,0:T(8,128)(2,1)S(1)}, u32[]{:S(2)}, u32[]{:S(2)}) collective-permute-start(bf16[352,128]{1,0:T(8,128)(2,1)S(1)} %add.30), channel_id=1, source_target_pairs={{0,8},{4,12},{8,0},{12,4},{16,24},{20,28},{24,16},{28,20},{1,9},{5... | collective-permute-start | bytes 270344 | tf_op jit(solution)/shard_map/ppermute | solution.py:145
  36.5 5.6 %collective-permute-start.7 = (bf16[352,128]{1,0:T(8,128)(2,1)S(1)}, bf16[352,128]{1,0:T(8,128)(2,1)S(1)}, u32[]{:S(2)}, u32[]{:S(2)}) collective-permute-start(bf16[352,128]{1,0:T(8,128)(2,1)S(1)} %add.31), channel_id=1, source_target_pairs={{0,16},{4,20},{8,24},{12,28},{16,0},{20,4},{24,8},{28,12},{1,17},{... | collective-permute-start | bytes 270344 | tf_op jit(solution)/shard_map/ppermute | solution.py:145
  42.2 0.8 %copy-start = (f32[8,2048]{1,0:T(8,128)S(1)}, f32[8,2048]{1,0:T(8,128)}, u32[]{:S(2)}) copy-start(f32[8,2048]{1,0:T(8,128)} %get-tuple-element.6) | copy-start | bytes 196612
  42.2 1.5 %collective-permute-start.8 = (bf16[256,128]{1,0:T(8,128)(2,1)S(1)}, bf16[256,128]{1,0:T(8,128)(2,1)S(1)}, u32[]{:S(2)}, u32[]{:S(2)}) collective-permute-start(bf16[256,128]{1,0:T(8,128)(2,1)S(1)} %pad_maximum_fusion.1), channel_id=1, source_target_pairs={{0,4},{4,0},{8,12},{12,8},{16,20},{20,16},{24,28},{28,24},{1,5},{5... | collective-permute-start | bytes 196616 | tf_op jit(solution)/shard_map/ppermute | solution.py:145

commit v2 on v1

--- a/solution.py
+++ b/solution.py
@@ -140,6 +140,20 @@
             ).astype(bf16)
 
 
+def join_kernel(half, mine_ref, other_ref, embedding_ref, taps_ref):
+    core = lax.rem(lax.axis_index("row"), 2)
+    total_rows = taps_ref.shape[0]
+    part = embedding_ref.shape[0] // 2
+    mine = mine_ref[...].astype(jnp.float32)
+    other = other_ref[...].astype(jnp.float32)
+    low = jnp.where(core == 0, mine, other)
+    high = jnp.where(core == 0, other, mine)
+    taps_ref[0 : total_rows - half, :] = low[0 : total_rows - half]
+    taps_ref[total_rows - half : total_rows, :] = high[0:half]
+    embedding_ref[0:part, :] = low[half : half + part]
+    embedding_ref[part : 2 * part, :] = high[half : half + part]
+
+
 def swap(value, axis, mask):
     peers = lax.axis_size(axis)
     return lax.ppermute(value, axis, [(i, i ^ mask) for i in range(peers)])
@@ -153,7 +167,6 @@
     peers = lax.axis_size("col")
     row_peers = lax.axis_size("row")
     bins = cols * peers
-    core = lax.rem(lax.axis_index("row"), 2)
     col_index = lax.axis_index("col")
     blocks = [embedding] + [swap(embedding, "col", mask) for mask in range(1, peers)]
     spare = LANES // 2 - filters
@@ -189,6 +202,7 @@
             pltpu.VMEM((bins + 2 * PAD, LANES), f32),
             pltpu.VMEM((taps_rows, LANES), f32),
         ],
+        compiler_params=pltpu.CompilerParams(vmem_limit_bytes=24 * 1024 * 1024),
         name="contact_head",
     )(dilation, *blocks, kernel.reshape(taps, filters, channels), bias, mix, mix_bias, cot)
 
@@ -197,6 +211,8 @@
     while mask < peers:
         total = total + swap(total, "col", mask)
         mask *= 2
+    contact = contact[:maps].reshape(maps, rows, cols)
+    total, contact = lax.optimization_barrier((total, contact))
     mask = 2
     while mask < row_peers:
         total = total + swap(total, "row", mask)
@@ -205,15 +221,18 @@
     mine = lax.dynamic_slice_in_dim(total[half:], col_index * part, part, 0)
     mine = jnp.concatenate([total[:half], mine], axis=0)
     other = swap(mine, "row", 1)
-    low = jnp.where(core == 0, mine, other).astype(f32)
-    high = jnp.where(core == 0, other, mine).astype(f32)
-    kernel_grad = jnp.concatenate([low[: taps_rows - half], high[:half]], axis=0)
-    embedding_grad = jnp.concatenate([low[half:], high[half:]], axis=0)
-    return (
-        contact[:maps].reshape(maps, rows, cols),
-        embedding_grad,
-        kernel_grad.reshape(kernel.shape),
-    )
+    embedding_grad, kernel_grad = pl.pallas_call(
+        functools.partial(join_kernel, half),
+        out_shape=(
+            jax.ShapeDtypeStruct((cols, channels), f32),
+            jax.ShapeDtypeStruct((taps_rows, channels), f32),
+        ),
+        in_specs=[vmem, vmem],
+        out_specs=(vmem, vmem),
+        compiler_params=pltpu.CompilerParams(vmem_limit_bytes=4 * 1024 * 1024),
+        name="join",
+    )(mine, other)
+    return contact, embedding_grad, kernel_grad.reshape(kernel.shape)
 
 
 def solution(mesh):

time: 45.5 us -> 41.8 us (0.919)
  other arithmetic: 3.71 us -> 0.99 us
  local copies, waits for them, and re-layouts: 4.31 us -> 2.4 us
  waiting for transfers between devices: 15.9 us -> 17.7 us
    ppermute x9, waiting for transfers between devices: 15.9 us -> 17.7 us  [swap(): return lax.ppermute(value, axis, [(i, i ^ mask) for i in range(peers)])]
    unnamed x14 -> x8, local copies, waits for them, and re-layouts: 1.35 us -> 0.02 us
    concatenate x2 -> x0, other arithmetic: 1.32 us -> none  [the longest x1 0.7 us: per_device(): kernel_grad = jnp.concatenate([low[:taps_rows - half], high[:half]], axis=0)]
    concatenate x2, other arithmetic: 1.34 us -> 0.16 us  [twice(): return jnp.concatenate([wide, wide], axis=1)]
    pallas_call x1, Pallas kernels: 9.45 us -> 8.33 us  [per_device(): pl.pallas_call(functools.partial(local_kernel, (peers, rows, cols, bins,...]
    add x1, other arithmetic: 0.92 us -> 0.03 us  [per_device(): total = keep + swap(send, 'row', 1)]
    pallas_call x0 -> x1, Pallas kernels: none -> 0.71 us  [per_device(): pl.pallas_call(functools.partial(join_kernel, half), out_shape=(jax.Shape...]
    mul x1, other arithmetic: 0.01 us -> 0.69 us  [per_device(): mix = jnp.pad(twice(0.5 * mixing), ((0, 16 - maps), (0, 0))).astype(bf16)]
  transfers between devices with their start and end apart: 9 -> 9, of which waited for: 6 -> 7; matrix products, arithmetic and copies ran while one was open for 9% -> 8% of each run, Pallas kernels for 0% -> 0%
where the time goes in v2:
time: 41.8 us; the launch traced here: 41.5 us
  waiting for transfers between devices  17.7 us (42%)
  starting transfers between devices  10.6 us (25%)
  Pallas kernels  9.04 us (22%)
  local copies, waits for them, and re-layouts  2.4 us (6%)
  other arithmetic  0.99 us (2%)
  between operations  0.78 us (2%)
    ppermute x9, waiting for transfers between devices, swap(): return lax.ppermute(value, axis, [(i, i ^ mask) for i in range(peers)])  17.7 us
    ppermute x9, starting transfers between devices, swap(): return lax.ppermute(value, axis, [(i, i ^ mask) for i in range(peers)])  10.6 us
    pallas_call x1, Pallas kernels, per_device(): pl.pallas_call(functools.partial(local_kernel, (peers, rows, cols, bins,...  8.33 us
    reshape x1, local copies, waits for them, and re-layouts, per_device(): cotangent.reshape(maps, rows * cols)  0.88 us
  transfers between devices with their start and end apart: 9, of which 7 were waited for; matrix products, arithmetic and copies ran while one was open for 8% of the time, Pallas kernels for 0%

profile of v2, /device:TPU:0, one launch (start us, length us, event | category | flops | bytes accessed | tf_op | source)
XLA Modules:
  0.0 41.5 jit_solution(7492047361085400882)
XLA Ops:
  0.6 0.0 copy-start.3
  0.6 0.0 copy-start
  0.7 3.1 %collective-permute-start.1 = (bf16[64,128]{1,0:T(8,128)(2,1)}, bf16[64,128]{1,0:T(8,128)(2,1)S(1)}, u32[]{:S(2)}, u32[]{:S(2)}) collective-permute-start(bf16[64,128]{1,0:T(8,128)(2,1)} %refs_0_.1), channel_id=1, source_target_pairs={{0,2},{1,3},{2,0},{3,1},{4,6},{5,7},{6,4},{7,5},{8,10},{9,11},{10,... | collective-permute-start | bytes 49160 | tf_op jit(solution)/shard_map/ppermute | solution.py:159
  3.7 1.5 %collective-permute-start = (bf16[64,128]{1,0:T(8,128)(2,1)}, bf16[64,128]{1,0:T(8,128)(2,1)S(1)}, u32[]{:S(2)}, u32[]{:S(2)}) collective-permute-start(bf16[64,128]{1,0:T(8,128)(2,1)} %refs_0_.1), channel_id=1, source_target_pairs={{0,1},{1,0},{2,3},{3,2},{4,5},{5,4},{6,7},{7,6},{8,9},{9,8},{10,11... | collective-permute-start | bytes 49160 | tf_op jit(solution)/shard_map/ppermute | solution.py:159
  5.2 0.1 collective-permute-start.2
  5.3 0.0 copy-done.3
  5.3 0.1 pad_maximum_fusion.1.refs_5_
  5.3 0.7 %broadcast_multiply_fusion = bf16[5,48]{1,0:T(8,128)(2,1)S(1)} fusion(bf16[5,48]{1,0:T(8,128)(2,1)} %param.11), kind=kLoop, calls=%fused_computation.5 | loop fusion | flops 240 | bytes 960 | tf_op jit(solution)/shard_map/mul | solution.py:182
  6.0 0.1 fusion.2.refs_6_
  6.1 0.7 %pad_bitcast_fusion = f32[8,1]{0,1:T(1,128)S(1)} fusion(f32[5]{0:T(128)} %param.12), kind=kLoop, calls=%fused_computation.7 | loop fusion | bytes 52 | tf_op jit(solution)/shard_map/broadcast_in_dim | solution.py:183
  6.8 0.1 copy.10.refs_7_
  6.9 0.9 %reshape.19 = bf16[5,2048]{1,0:T(8,128)(2,1)S(1)} reshape(bf16[5,32,64]{2,1,0:T(8,128)(2,1)} %param.13) | data formatting | bytes 40960 | tf_op jit(solution)/shard_map/reshape | solution.py:184
  7.7 0.0 copy-start.1
  7.8 0.0 copy-start.2
  7.8 0.0 collective-permute-done.1.refs_2_
  7.8 0.0 collective-permute-done.refs_1_
  7.8 2.2 %collective-permute-done.2.refs_3_ = bf16[64,128]{1,0:T(8,128)(2,1)S(1)} collective-permute-done((bf16[64,128]{1,0:T(8,128)(2,1)}, bf16[64,128]{1,0:T(8,128)(2,1)S(1)}, u32[]{:S(2)}, u32[]{:S(2)}) %collective-permute-start.2) | collective-permute-done | bytes 16416 | tf_op jit(solution)/shard_map/ppermute | solution.py:159
  10.1 8.3 %contact_head.1 = (f32[8,2048]{1,0:T(8,128)S(1)}, bf16[352,128]{1,0:T(8,128)(2,1)S(1)}, bf16[352,128]{1,0:T(8,128)(2,1)S(1)}) custom-call(s32[2]{0:T(128)S(1)} %copy-done.2, bf16[64,128]{1,0:T(8,128)(2,1)S(1)} %copy-done.1, bf16[64,128]{1,0:T(8,128)(2,1)S(1)} %collective-permute-done.refs_1_, bf16[64,128]{1,0:T(8,128)(2,1)S(1)} %collective-permute-done.1.refs_2_, ...), custom_call_target="tpu_custom_call" | custom-call | tf_op jit(solution)/shard_map/contact_head/pallas_call | solution.py:187
  18.4 0.1 collective-permute-start.3
  18.5 1.3 %collective-permute-done.3 = bf16[352,128]{1,0:T(8,128)(2,1)S(1)} collective-permute-done((bf16[352,128]{1,0:T(8,128)(2,1)S(1)}, bf16[352,128]{1,0:T(8,128)(2,1)S(1)}, u32[]{:S(2)}, u32[]{:S(2)}) %collective-permute-start.3) | collective-permute-done | bytes 90144 | tf_op jit(solution)/shard_map/ppermute | solution.py:159
  19.8 0.6 %collective-permute-start.4 = (bf16[352,128]{1,0:T(8,128)(2,1)S(1)}, bf16[352,128]{1,0:T(8,128)(2,1)S(1)}, u32[]{:S(2)}, u32[]{:S(2)}) collective-permute-start(bf16[352,128]{1,0:T(8,128)(2,1)S(1)} %add.28), channel_id=1, source_target_pairs={{0,1},{1,0},{2,3},{3,2},{4,5},{5,4},{6,7},{7,6},{8,9},{9,8},{10,11... | collective-permute-start | bytes 270344 | tf_op jit(solution)/shard_map/ppermute | solution.py:159
  20.4 4.1 %collective-permute-done.4 = bf16[352,128]{1,0:T(8,128)(2,1)S(1)} collective-permute-done((bf16[352,128]{1,0:T(8,128)(2,1)S(1)}, bf16[352,128]{1,0:T(8,128)(2,1)S(1)}, u32[]{:S(2)}, u32[]{:S(2)}) %collective-permute-start.4) | collective-permute-done | bytes 90144 | tf_op jit(solution)/shard_map/ppermute | solution.py:159
  24.6 0.6 %collective-permute-start.5 = (bf16[352,128]{1,0:T(8,128)(2,1)S(1)}, bf16[352,128]{1,0:T(8,128)(2,1)S(1)}, u32[]{:S(2)}, u32[]{:S(2)}) collective-permute-start(bf16[352,128]{1,0:T(8,128)(2,1)S(1)} %add.29), channel_id=1, source_target_pairs={{0,2},{1,3},{2,0},{3,1},{4,6},{5,7},{6,4},{7,5},{8,10},{9,11},{10,... | collective-permute-start | bytes 270344 | tf_op jit(solution)/shard_map/ppermute | solution.py:159
  25.1 0.7 %reshape.20 = f32[5,32,64]{2,1,0:T(8,128)} reshape(f32[5,2048]{1,0:T(8,128)S(1)} %bitcast.7) | data formatting | bytes 81920 | tf_op jit(solution)/shard_map/reshape | solution.py:214
  25.8 3.3 %collective-permute-done.5 = bf16[352,128]{1,0:T(8,128)(2,1)S(1)} collective-permute-done((bf16[352,128]{1,0:T(8,128)(2,1)S(1)}, bf16[352,128]{1,0:T(8,128)(2,1)S(1)}, u32[]{:S(2)}, u32[]{:S(2)}) %collective-permute-start.5) | collective-permute-done | bytes 90144 | tf_op jit(solution)/shard_map/ppermute | solution.py:159
  29.2 1.6 %collective-permute-start.6 = (bf16[352,128]{1,0:T(8,128)(2,1)S(1)}, bf16[352,128]{1,0:T(8,128)(2,1)S(1)}, u32[]{:S(2)}, u32[]{:S(2)}) collective-permute-start(bf16[352,128]{1,0:T(8,128)(2,1)S(1)} %add.30), channel_id=1, source_target_pairs={{0,8},{4,12},{8,0},{12,4},{16,24},{20,28},{24,16},{28,20},{1,9},{5... | collective-permute-start | bytes 270344 | tf_op jit(solution)/shard_map/ppermute | solution.py:159
  30.8 3.0 %collective-permute-done.6 = bf16[352,128]{1,0:T(8,128)(2,1)S(1)} collective-permute-done((bf16[352,128]{1,0:T(8,128)(2,1)S(1)}, bf16[352,128]{1,0:T(8,128)(2,1)S(1)}, u32[]{:S(2)}, u32[]{:S(2)}) %collective-permute-start.6) | collective-permute-done | bytes 90144 | tf_op jit(solution)/shard_map/ppermute | solution.py:159
  33.8 3.1 %collective-permute-start.7 = (bf16[352,128]{1,0:T(8,128)(2,1)S(1)}, bf16[352,128]{1,0:T(8,128)(2,1)S(1)}, u32[]{:S(2)}, u32[]{:S(2)}) collective-permute-start(bf16[352,128]{1,0:T(8,128)(2,1)S(1)} %add.31), channel_id=1, source_target_pairs={{0,16},{4,20},{8,24},{12,28},{16,0},{20,4},{24,8},{28,12},{1,17},{... | collective-permute-start | bytes 270344 | tf_op jit(solution)/shard_map/ppermute | solution.py:159
  36.9 2.5 %collective-permute-done.7 = bf16[352,128]{1,0:T(8,128)(2,1)S(1)} collective-permute-done((bf16[352,128]{1,0:T(8,128)(2,1)S(1)}, bf16[352,128]{1,0:T(8,128)(2,1)S(1)}, u32[]{:S(2)}, u32[]{:S(2)}) %collective-permute-start.7) | collective-permute-done | bytes 90144 | tf_op jit(solution)/shard_map/ppermute | solution.py:159
  39.5 0.1 collective-permute-start.8
  39.6 1.2 %collective-permute-done.8.other_ref = bf16[256,128]{1,0:T(8,128)(2,1)S(1)} collective-permute-done((bf16[256,128]{1,0:T(8,128)(2,1)S(1)}, bf16[256,128]{1,0:T(8,128)(2,1)S(1)}, u32[]{:S(2)}, u32[]{:S(2)}) %collective-permute-start.8) | collective-permute-done | bytes 65568 | tf_op jit(solution)/shard_map/ppermute | solution.py:159
  40.8 0.7 %join.1 = (f32[64,128]{1,0:T(8,128)}, f32[432,128]{1,0:T(8,128)}) custom-call(bf16[256,128]{1,0:T(8,128)(2,1)S(1)} %pad_maximum_fusion.mine_ref, bf16[256,128]{1,0:T(8,128)(2,1)S(1)} %collective-permute-done.8.other_ref), custom_call_target="tpu_custom_call" | custom-call | tf_op jit(solution)/shard_map/join/pallas_call | solution.py:224
  (15 shorter events, 0.2 us)
Async XLA Ops:
  0.6 4.6 %copy-start.3 = (f32[48]{0:T(128)S(1)}, f32[48]{0:T(128)}, u32[]{:S(2)}) copy-start(f32[48]{0:T(128)} %param.10) | copy-start | bytes 580
  0.6 9.4 %copy-start = (bf16[3,3,48,128]{3,2,1,0:T(8,128)(2,1)S(1)}, bf16[3,3,48,128]{3,2,1,0:T(8,128)(2,1)}, u32[]{:S(2)}) copy-start(bf16[3,3,48,128]{3,2,1,0:T(8,128)(2,1)} %param.9) | copy-start | bytes 331780
  0.7 7.1 %collective-permute-start.1 = (bf16[64,128]{1,0:T(8,128)(2,1)}, bf16[64,128]{1,0:T(8,128)(2,1)S(1)}, u32[]{:S(2)}, u32[]{:S(2)}) collective-permute-start(bf16[64,128]{1,0:T(8,128)(2,1)} %refs_0_.1), channel_id=1, source_target_pairs={{0,2},{1,3},{2,0},{3,1},{4,6},{5,7},{6,4},{7,5},{8,10},{9,11},{10,... | collective-permute-start | bytes 49160 | tf_op jit(solution)/shard_map/ppermute | solution.py:159
  3.7 4.1 %collective-permute-start = (bf16[64,128]{1,0:T(8,128)(2,1)}, bf16[64,128]{1,0:T(8,128)(2,1)S(1)}, u32[]{:S(2)}, u32[]{:S(2)}) collective-permute-start(bf16[64,128]{1,0:T(8,128)(2,1)} %refs_0_.1), channel_id=1, source_target_pairs={{0,1},{1,0},{2,3},{3,2},{4,5},{5,4},{6,7},{7,6},{8,9},{9,8},{10,11... | collective-permute-start | bytes 49160 | tf_op jit(solution)/shard_map/ppermute | solution.py:159
  5.2 4.8 %collective-permute-start.2 = (bf16[64,128]{1,0:T(8,128)(2,1)}, bf16[64,128]{1,0:T(8,128)(2,1)S(1)}, u32[]{:S(2)}, u32[]{:S(2)}) collective-permute-start(bf16[64,128]{1,0:T(8,128)(2,1)} %refs_0_.1), channel_id=1, source_target_pairs={{0,3},{1,2},{2,1},{3,0},{4,7},{5,6},{6,5},{7,4},{8,11},{9,10},{10,... | collective-permute-start | bytes 49160 | tf_op jit(solution)/shard_map/ppermute | solution.py:159
  7.7 2.3 %copy-start.1 = (bf16[64,128]{1,0:T(8,128)(2,1)S(1)}, bf16[64,128]{1,0:T(8,128)(2,1)}, u32[]{:S(2)}) copy-start(bf16[64,128]{1,0:T(8,128)(2,1)} %refs_0_.1) | copy-start | bytes 49156
  7.8 2.3 %copy-start.2 = (s32[2]{0:T(128)S(1)}, s32[2]{0:T(128)}, u32[]{:S(2)}) copy-start(s32[2]{0:T(128)} %dilation_ref.1) | copy-start | bytes 28
  18.4 1.4 %collective-permute-start.3 = (bf16[352,128]{1,0:T(8,128)(2,1)S(1)}, bf16[352,128]{1,0:T(8,128)(2,1)S(1)}, u32[]{:S(2)}, u32[]{:S(2)}) collective-permute-start(bf16[352,128]{1,0:T(8,128)(2,1)S(1)} %get-tuple-element.11), channel_id=1, source_target_pairs={{0,4},{4,0},{8,12},{12,8},{16,20},{20,16},{24,28},{28,24},{1,5},{5... | collective-permute-start | bytes 270344 | tf_op jit(solution)/shard_map/ppermute | solution.py:159
  19.8 4.7 %collective-permute-start.4 = (bf16[352,128]{1,0:T(8,128)(2,1)S(1)}, bf16[352,128]{1,0:T(8,128)(2,1)S(1)}, u32[]{:S(2)}, u32[]{:S(2)}) collective-permute-start(bf16[352,128]{1,0:T(8,128)(2,1)S(1)} %add.28), channel_id=1, source_target_pairs={{0,1},{1,0},{2,3},{3,2},{4,5},{5,4},{6,7},{7,6},{8,9},{9,8},{10,11... | collective-permute-start | bytes 270344 | tf_op jit(solution)/shard_map/ppermute | solution.py:159
  24.6 4.6 %collective-permute-start.5 = (bf16[352,128]{1,0:T(8,128)(2,1)S(1)}, bf16[352,128]{1,0:T(8,128)(2,1)S(1)}, u32[]{:S(2)}, u32[]{:S(2)}) collective-permute-start(bf16[352,128]{1,0:T(8,128)(2,1)S(1)} %add.29), channel_id=1, source_target_pairs={{0,2},{1,3},{2,0},{3,1},{4,6},{5,7},{6,4},{7,5},{8,10},{9,11},{10,... | collective-permute-start | bytes 270344 | tf_op jit(solution)/shard_map/ppermute | solution.py:159
  29.2 4.6 %collective-permute-start.6 = (bf16[352,128]{1,0:T(8,128)(2,1)S(1)}, bf16[352,128]{1,0:T(8,128)(2,1)S(1)}, u32[]{:S(2)}, u32[]{:S(2)}) collective-permute-start(bf16[352,128]{1,0:T(8,128)(2,1)S(1)} %add.30), channel_id=1, source_target_pairs={{0,8},{4,12},{8,0},{12,4},{16,24},{20,28},{24,16},{28,20},{1,9},{5... | collective-permute-start | bytes 270344 | tf_op jit(solution)/shard_map/ppermute | solution.py:159
  33.8 5.6 %collective-permute-start.7 = (bf16[352,128]{1,0:T(8,128)(2,1)S(1)}, bf16[352,128]{1,0:T(8,128)(2,1)S(1)}, u32[]{:S(2)}, u32[]{:S(2)}) collective-permute-start(bf16[352,128]{1,0:T(8,128)(2,1)S(1)} %add.31), channel_id=1, source_target_pairs={{0,16},{4,20},{8,24},{12,28},{16,0},{20,4},{24,8},{28,12},{1,17},{... | collective-permute-start | bytes 270344 | tf_op jit(solution)/shard_map/ppermute | solution.py:159
  39.5 1.3 %collective-permute-start.8 = (bf16[256,128]{1,0:T(8,128)(2,1)S(1)}, bf16[256,128]{1,0:T(8,128)(2,1)S(1)}, u32[]{:S(2)}, u32[]{:S(2)}) collective-permute-start(bf16[256,128]{1,0:T(8,128)(2,1)S(1)} %pad_maximum_fusion.mine_ref), channel_id=1, source_target_pairs={{0,4},{4,0},{8,12},{12,8},{16,20},{20,16},{24,28},{28,24},{1,5},{5... | collective-permute-start | bytes 196616 | tf_op jit(solution)/shard_map/ppermute | solution.py:159

commit v3 on v2

v3 whole, which is shorter than its diff:
```python
import functools

import jax
import jax.numpy as jnp
from jax import lax
from jax.experimental import pallas as pl
from jax.experimental.pallas import tpu as pltpu
from jax.sharding import PartitionSpec as P

DMAX = 4
PAD = 8
STEPS = (-1, 0, 1)
TAPS = [(a, b) for a in STEPS for b in STEPS]
LANES = 128
HALF = LANES // 2


def contract(left, right, dims):
    return lax.dot_general(left, right, (dims, ((), ())), preferred_element_type=jnp.float32)


def prepare_kernel(
    embedding_hbm,
    dilation_hbm,
    kernel_hbm,
    bias_hbm,
    mixing_hbm,
    cot_hbm,
    own_ref,
    rate_ref,
    weight_ref,
    wide_ref,
    guide_ref,
    mix_ref,
    wide_bias_ref,
    rates,
    kernel_ref,
    bias_ref,
    mixing_ref,
    cot_ref,
    flat_ref,
    semaphores,
):
    pairs = (
        (kernel_hbm, kernel_ref),
        (cot_hbm, cot_ref),
        (mixing_hbm, mixing_ref),
        (bias_hbm, bias_ref),
        (dilation_hbm, rates),
        (embedding_hbm, own_ref),
    )
    copies = [pltpu.make_async_copy(*pair, semaphores.at[at]) for at, pair in enumerate(pairs)]
    for copy in copies:
        copy.start()
    filters = kernel_ref.shape[1]
    maps, rows, cols = cot_ref.shape
    weight_ref[...] = jnp.zeros_like(weight_ref)
    wide_ref[...] = jnp.zeros_like(wide_ref)
    wide_bias_ref[...] = jnp.zeros_like(wide_bias_ref)
    for copy in copies:
        copy.wait()
    lead = (0, HALF, 2 * HALF)
    side = (HALF, 0, 3 * HALF)
    for at, (a, b) in enumerate(TAPS):
        tap = kernel_ref[at]
        first = lead[a + 1]
        weight_ref[0, first : first + filters, (b + 1) * LANES : (b + 2) * LANES] = tap
        first = side[b + 1]
        weight_ref[1, first : first + filters, (a + 1) * LANES : (a + 2) * LANES] = tap
        first = (b + 1) * LANES
        wide_ref[first : first + filters, (a + 1) * LANES : (a + 2) * LANES] = tap
        first = (a + 1) * LANES + HALF
        wide_ref[first : first + filters, (b + 4) * LANES : (b + 5) * LANES] = tap
    rate_ref[0:8, :] = jnp.full((8, LANES), rates[0], jnp.int32)
    rate_ref[8:16, :] = jnp.full((8, LANES), rates[1], jnp.int32)
    wide_bias_ref[0:1, 0:filters] = bias_ref[...]
    wide_bias_ref[0:1, HALF : HALF + filters] = bias_ref[...]
    mix = 0.5 * mixing_ref[...].astype(jnp.float32)
    spare = jnp.zeros((maps, HALF - filters), jnp.float32)
    mix = jnp.concatenate([mix, spare, mix, spare], axis=1)
    mix_ref[0:maps, :] = mix
    mix_ref[maps:16, :] = jnp.zeros((16 - maps, LANES), jnp.float32)
    for t in range(maps):
        flat_ref[t * rows : (t + 1) * rows, :] = cot_ref[t].astype(jnp.float32)
    lines = [flat_ref[pl.ds(i, maps, stride=rows), :] for i in range(rows)]
    cot = jnp.concatenate(lines, axis=1).astype(jnp.bfloat16)
    mix = mix.astype(jnp.bfloat16)
    guide_ref[...] = contract(cot, mix, ((0,), (0,))).astype(jnp.bfloat16)


def contact_kernel(mix_bias_ref, mix_ref, active_ref, contact_ref):
    mix = mix_ref[...].astype(jnp.bfloat16)
    mixed = contract(mix, active_ref[...], ((1,), (1,)))
    maps = contact_ref.shape[0]
    which = lax.broadcasted_iota(jnp.int32, (8, 1), 0)
    offset = jnp.zeros((8, 1), jnp.float32)
    for t in range(maps):
        offset = jnp.where(which == t, mix_bias_ref[t], offset)
    contact_ref[...] = (mixed[0:8] + offset)[0:maps]


def local_kernel(sizes, *refs):
    peers, rows, cols, bins, filters, half = sizes
    block_refs = refs[:peers]
    rate_ref, weight_ref, wide_ref, guide_ref, bias_ref = refs[peers : peers + 5]
    active_ref, send_ref, keep_ref = refs[peers + 5 : peers + 8]
    bins_ref, pair_ref, conv_ref, grad_ref, turned_ref, acc_ref, taps_ref = refs[peers + 8 :]
    row_rate = jnp.max(rate_ref[0:8, :])
    col_rate = jnp.max(rate_ref[8:16, :])
    row_index = lax.axis_index("row")
    col_index = lax.axis_index("col")
    row_start = row_index * rows
    col_start = col_index * cols
    core = lax.rem(row_index, 2)
    count = len(TAPS)
    bf16 = jnp.bfloat16
    f32 = jnp.float32
    extended = rows + 2 * DMAX

    bins_ref[0:PAD, :] = jnp.zeros((PAD, LANES), f32)
    bins_ref[bins + PAD : bins + 2 * PAD, :] = jnp.zeros((PAD, LANES), f32)
    for step in range(peers):
        place = pl.multiple_of(jnp.bitwise_xor(col_index, step) * cols + PAD, 8)
        bins_ref[pl.ds(place, cols), :] = 0.5 * block_refs[step][...].astype(f32)

    col_place = lax.broadcasted_iota(jnp.int32, (cols, LANES), 0) + col_start
    edge = 16
    values = []
    keeps = []
    for shift in (0, -col_rate, col_rate, -row_rate, row_rate):
        values.append(bins_ref[pl.ds(col_start + PAD + shift, cols), :].astype(bf16))
        place = col_place + shift
        keeps.append(((place >= 0) & (place < bins)).astype(f32).astype(bf16))
    for m in range(extended):
        row = bins_ref[pl.ds(row_start + PAD - DMAX + m, 1), :]
        row = jnp.broadcast_to(row, (edge, LANES)).astype(bf16)
        place = row_start - DMAX + m
        inside = ((place >= 0) & (place < bins)).astype(f32).astype(bf16)
        for slot in range(5):
            for j in range(0, cols, edge):
                piece = row + values[slot][j : j + edge]
                if slot > 0 and (j == 0 or j + edge == cols):
                    piece = piece * keeps[slot][j : j + edge]
                if m < DMAX or m >= rows + DMAX:
                    piece = piece * inside
                pair_ref[slot, m * cols + j : m * cols + j + edge, :] = piece

    def shifted_columns(first, last):
        return jnp.concatenate([pair_ref[first], pair_ref[0], pair_ref[last]], axis=1)

    conv_ref[0] = contract(shifted_columns(1, 2), weight_ref[0], ((1,), (1,)))
    conv_ref[1] = contract(shifted_columns(3, 4), weight_ref[1], ((1,), (1,)))

    lane = lax.broadcasted_iota(jnp.int32, (1, LANES), 1)
    is_mirror = lane >= HALF
    bias = bias_ref[0:1, :]
    row_keeps = []
    for q in STEPS:
        place = col_place + jnp.where(is_mirror, q * row_rate, q * col_rate)
        row_keeps.append(((place >= 0) & (place < bins)).astype(f32))
    margin = PAD * cols
    grad_ref[0:margin, :] = jnp.zeros((margin, LANES), bf16)
    grad_ref[margin + rows * cols : 2 * margin + rows * cols, :] = jnp.zeros((margin, LANES), bf16)
    row_sums = [[], [], []]
    col_middle = None
    col_edges = [None, None, None]

    def add(total, term):
        return term if total is None else total + term

    for i in range(rows):
        def part(mirrored, shift, group):
            first = pl.multiple_of((DMAX + i + shift) * cols, cols)
            return conv_ref[mirrored, pl.ds(first, cols), group * LANES : (group + 1) * LANES]

        swapped = jnp.where(is_mirror, part(0, 0, 0), part(1, 0, 0))
        conv = jnp.where(is_mirror, part(1, -col_rate, 0), part(0, -row_rate, 0))
        conv = conv + pltpu.roll(swapped, HALF, 1)
        conv = conv + (part(0, row_rate, 1) + part(1, col_rate, 1))
        conv = conv + bias
        here = slice(i * cols, (i + 1) * cols)
        grad = jnp.where(conv > 0, guide_ref[here, :].astype(f32), 0.0)
        active_ref[here, :] = jnp.maximum(conv, 0.0).astype(bf16)
        grad_ref[margin + i * cols : margin + (i + 1) * cols, :] = grad.astype(bf16)
        last = cols - 8
        inner = grad[8:16]
        for j in range(16, last, 8):
            inner = inner + grad[j : j + 8]
        for q in range(3):
            keep = row_keeps[q]
            eight = inner + grad[0:8] * keep[0:8] + grad[last:cols] * keep[last:cols]
            row_sums[q].append(jnp.sum(eight, axis=0, keepdims=True))
            if i < DMAX or i >= rows - DMAX:
                step = STEPS[q]
                place = row_start + i + jnp.where(is_mirror, step * col_rate, step * row_rate)
                keep = ((place >= 0) & (place < bins)).astype(f32)
                col_edges[q] = add(col_edges[q], grad * keep)
        if DMAX <= i < rows - DMAX:
            col_middle = add(col_middle, grad)

    chunks = (2 * margin + rows * cols) // LANES
    first_chunk = margin // LANES
    last_chunk = chunks - first_chunk
    blank = jnp.zeros((LANES, LANES), bf16)
    for odd in range(2):
        for chunk in range(chunks):
            at = slice(chunk * LANES, (chunk + 1) * LANES)
            if first_chunk <= chunk < last_chunk + odd:
                begin = chunk * LANES - odd * cols
                turned_ref[odd, :, at] = grad_ref[begin : begin + LANES, :].T
            else:
                turned_ref[odd, :, at] = blank

    def shifted_rows(first, rate):
        pieces = []
        for q in STEPS:
            start = (DMAX - q * rate) * cols
            odd = lax.rem(lax.rem(q * rate, 2) + 2, 2)
            start = pl.multiple_of(start + odd * cols, LANES)
            pieces.append(turned_ref[odd, first : first + filters, pl.ds(start, extended * cols)])
        return jnp.concatenate(pieces, axis=0)

    direct = contract(shifted_rows(0, row_rate), shifted_columns(1, 2), ((1,), (0,)))
    mirror = contract(shifted_rows(HALF, col_rate), shifted_columns(3, 4), ((1,), (0,)))
    for at, (a, b) in enumerate(TAPS):
        a, b = a + 1, b + 1
        taps_ref[at * filters : (at + 1) * filters, :] = (
            direct[a * filters : (a + 1) * filters, b * LANES : (b + 1) * LANES]
            + mirror[b * filters : (b + 1) * filters, a * LANES : (a + 1) * LANES]
        )

    row_sums = [jnp.concatenate(sums, axis=0) for sums in row_sums]
    col_sums = [pltpu.roll(col_middle + edges, HALF, 1) for edges in col_edges]
    sums = jnp.concatenate(
        [jnp.concatenate(row_sums, axis=1), jnp.concatenate(col_sums, axis=1)], axis=0
    ).astype(bf16)
    spread = contract(sums, wide_ref[...], ((1,), (0,)))
    acc_ref[...] = jnp.zeros_like(acc_ref)
    for group in range(6):
        shift = STEPS[group % 3] * (row_rate if group < 3 else col_rate)
        piece = spread[:, group * LANES : (group + 1) * LANES]
        where = pl.ds(row_start + PAD + shift, rows)
        acc_ref[where, :] = acc_ref[where, :] + piece[0:rows]
        where = pl.ds(col_start + PAD + shift, cols)
        acc_ref[where, :] = acc_ref[where, :] + piece[rows : rows + cols]

    total_rows = count * filters
    for target, which in ((keep_ref, core), (send_ref, 1 - core)):
        first = pl.multiple_of(which * (total_rows - half), 16)
        target[0:half, :] = taps_ref[pl.ds(first, half), :].astype(bf16)
        part = cols // 2
        for step in range(peers):
            first = pl.multiple_of(which * part + (step * cols + PAD), 8)
            target[half + step * part : half + (step + 1) * part, :] = (
                0.5 * acc_ref[pl.ds(first, part), :]
            ).astype(bf16)


def join_kernel(half, mine_ref, other_ref, embedding_ref, taps_ref):
    core = lax.rem(lax.axis_index("row"), 2)
    total_rows = taps_ref.shape[0]
    part = embedding_ref.shape[0] // 2
    mine = mine_ref[...].astype(jnp.float32)
    other = other_ref[...].astype(jnp.float32)
    low = jnp.where(core == 0, mine, other)
    high = jnp.where(core == 0, other, mine)
    taps_ref[0 : total_rows - half, :] = low[0 : total_rows - half]
    taps_ref[total_rows - half : total_rows, :] = high[0:half]
    embedding_ref[0:part, :] = low[half : half + part]
    embedding_ref[part : 2 * part, :] = high[half : half + part]


def swap(value, axis, mask):
    peers = lax.axis_size(axis)
    return lax.ppermute(value, axis, [(i, i ^ mask) for i in range(peers)])


def per_device(embedding, dilation, kernel, kernel_bias, mixing, mixing_bias, cotangent):
    f32 = jnp.float32
    bf16 = jnp.bfloat16
    filters, channels = kernel.shape[2:]
    maps, rows, cols = cotangent.shape
    peers = lax.axis_size("col")
    row_peers = lax.axis_size("row")
    bins = cols * peers
    col_index = lax.axis_index("col")
    blocks = [embedding] + [swap(embedding, "col", mask) for mask in range(1, peers)]
    taps = len(TAPS)
    taps_rows = taps * filters
    half = (taps_rows // 2 + 15) // 16 * 16
    spots = rows * cols
    packed = half + peers * cols // 2
    vmem = pl.BlockSpec(memory_space=pltpu.VMEM)
    mib = 1024 * 1024

    def call(body, name, out_shape, inputs, scratch=(), limit=16, specs=None, flops=1000):
        return pl.pallas_call(
            body,
            out_shape=out_shape,
            in_specs=specs or [vmem] * len(inputs),
            out_specs=jax.tree.map(lambda _: vmem, out_shape),
            scratch_shapes=list(scratch),
            compiler_params=pltpu.CompilerParams(vmem_limit_bytes=limit * mib),
            cost_estimate=pl.CostEstimate(flops=flops, bytes_accessed=1000, transcendentals=0),
            name=name,
        )(*inputs)

    shape = jax.ShapeDtypeStruct
    kernels = kernel.reshape(taps, filters, channels)
    own, rates, weight, wide, guide, mix, bias = call(
        prepare_kernel,
        "prepare",
        (
            shape(embedding.shape, bf16),
            shape((16, LANES), jnp.int32),
            shape((2, 2 * LANES, 3 * LANES), bf16),
            shape((3 * LANES, 6 * LANES), bf16),
            shape((spots, LANES), bf16),
            shape((16, LANES), f32),
            shape((8, LANES), f32),
        ),
        (embedding, dilation, kernels, kernel_bias[None, :], mixing, cotangent),
        scratch=(
            pltpu.SMEM((2,), jnp.int32),
            pltpu.VMEM(kernels.shape, bf16),
            pltpu.VMEM((1, filters), f32),
            pltpu.VMEM(mixing.shape, bf16),
            pltpu.VMEM(cotangent.shape, bf16),
            pltpu.VMEM((maps * rows, cols), f32),
            pltpu.SemaphoreType.DMA((6,)),
        ),
        specs=[pl.BlockSpec(memory_space=pltpu.HBM)] * 6,
        flops=4_000_000_000,
    )
    blocks[0] = own
    extended = (rows + 2 * DMAX) * cols
    padded = spots + 2 * PAD * cols
    active, send, keep = call(
        functools.partial(local_kernel, (peers, rows, cols, bins, filters, half)),
        "contact_head",
        (shape((spots, LANES), bf16), shape((packed, LANES), bf16), shape((packed, LANES), bf16)),
        (*blocks, rates, weight, wide, guide, bias),
        scratch=(
            pltpu.VMEM((bins + 2 * PAD, LANES), f32),
            pltpu.VMEM((5, extended, LANES), bf16),
            pltpu.VMEM((2, extended, 2 * LANES), f32),
            pltpu.VMEM((padded, LANES), bf16),
            pltpu.VMEM((2, LANES, padded), bf16),
            pltpu.VMEM((bins + 2 * PAD, LANES), f32),
            pltpu.VMEM((taps_rows, LANES), f32),
        ),
        limit=24,
        flops=20_000_000_000,
    )

    total = keep + swap(send, "row", 1)
    mask = 1
    while mask < peers:
        total = total + swap(total, "col", mask)
        mask *= 2
    contact = call(
        contact_kernel,
        "contact",
        shape((maps, spots), f32),
        (mixing_bias, mix, active),
        specs=[pl.BlockSpec(memory_space=pltpu.SMEM), vmem, vmem],
        flops=1_000_000_000,
    ).reshape(maps, rows, cols)
    total, contact = lax.optimization_barrier((total, contact))
    mask = 2
    while mask < row_peers:
        total = total + swap(total, "row", mask)
        mask *= 2
    part = cols // 2
    mine = lax.dynamic_slice_in_dim(total[half:], col_index * part, part, 0)
    mine = jnp.concatenate([total[:half], mine], axis=0)
    other = swap(mine, "row", 1)
    embedding_grad, kernel_grad = call(
        functools.partial(join_kernel, half),
        "join",
        (shape((cols, channels), f32), shape((taps_rows, channels), f32)),
        (mine, other),
        limit=4,
    )
    return contact, embedding_grad, kernel_grad.reshape(kernel.shape)


def solution(mesh):
    return jax.shard_map(
        per_device,
        mesh=mesh,
        in_specs=(P("col", None), P(), P(), P(), P(), P(), P(None, "row", "col")),
        out_specs=(P(None, "row", "col"), P("col", None), P()),
        check_vma=False,
    )
```

time: 41.8 us -> 37.6 us (0.90)
  waiting for transfers between devices: 17.7 us -> 12.5 us
  Pallas kernels: 9.04 us -> 6.94 us
  local copies, waits for them, and re-layouts: 2.4 us -> 4.47 us
  starting transfers between devices: 10.6 us -> 12.6 us
  other arithmetic: 0.99 us -> 0.14 us
    ppermute x9, waiting for transfers between devices: 17.7 us -> 12.5 us  [swap(): return lax.ppermute(value, axis, [(i, i ^ mask) for i in range(peers)])]
    unnamed x8 -> x14, local copies, waits for them, and re-layouts: 0.02 us -> 3.72 us
    pallas_call x2 -> x4, Pallas kernels: 9.04 us -> 6.94 us  [call(): pl.pallas_call(body, out_shape=out_shape, in_specs=specs or [vmem] * len(...]
    ppermute x9, starting transfers between devices: 10.6 us -> 12.6 us  [swap(): return lax.ppermute(value, axis, [(i, i ^ mask) for i in range(peers)])]
    reshape x2 -> x1, local copies, waits for them, and re-layouts: 1.59 us -> 0.73 us  [per_device(): contact = call(contact_kernel, 'contact', shape((maps, spots), f32), (mix...]
    broadcast_in_dim x2 -> x0, local copies, waits for them, and re-layouts: 0.74 us -> none  [per_device(): mix_bias = jnp.pad(mixing_bias, (0, 8 - maps))[:, None]]
    mul x1 -> x0, other arithmetic: 0.69 us -> none  [per_device(): mix = jnp.pad(twice(0.5 * mixing), ((0, 16 - maps), (0, 0))).astype(bf16)]
  transfers between devices with their start and end apart: 9 -> 9, of which waited for: 7 -> 7; matrix products, arithmetic and copies ran while one was open for 8% -> 2% of each run, Pallas kernels for 0% -> 6%
where the time goes in v3:
time: 37.6 us; the launch traced here: 37.3 us
  starting transfers between devices  12.6 us (34%)
  waiting for transfers between devices  12.5 us (33%)
  Pallas kernels  6.94 us (18%)
  local copies, waits for them, and re-layouts  4.47 us (12%)
  between operations  0.75 us (2%)
    ppermute x9, starting transfers between devices, swap(): return lax.ppermute(value, axis, [(i, i ^ mask) for i in range(peers)])  12.6 us
    ppermute x9, waiting for transfers between devices, swap(): return lax.ppermute(value, axis, [(i, i ^ mask) for i in range(peers)])  12.5 us
    pallas_call x4, Pallas kernels, call(): pl.pallas_call(body, out_shape=out_shape, in_specs=specs or [vmem] * len(...  6.94 us
    unnamed x14, local copies, waits for them, and re-layouts  3.72 us
  transfers between devices with their start and end apart: 9, of which 7 were waited for; matrix products, arithmetic and copies ran while one was open for 2% of the time, Pallas kernels for 6%

profile of v3, /device:TPU:0, one launch (start us, length us, event | category | flops | bytes accessed | tf_op | source)
XLA Modules:
  0.0 37.3 jit_solution(5435099908214958396)
XLA Ops:
  0.6 0.0 copy-start.3
  0.6 3.0 %collective-permute-start = (bf16[64,128]{1,0:T(8,128)(2,1)}, bf16[64,128]{1,0:T(8,128)(2,1)S(1)}, u32[]{:S(2)}, u32[]{:S(2)}) collective-permute-start(bf16[64,128]{1,0:T(8,128)(2,1)} %embedding_hbm.1), channel_id=1, source_target_pairs={{0,1},{1,0},{2,3},{3,2},{4,5},{5,4},{6,7},{7,6},{8,9},{9,8},{10,11... | collective-permute-start | bytes 49160 | tf_op jit(solution)/shard_map/ppermute | solution.py:275
  3.7 1.5 %collective-permute-start.1 = (bf16[64,128]{1,0:T(8,128)(2,1)}, bf16[64,128]{1,0:T(8,128)(2,1)S(1)}, u32[]{:S(2)}, u32[]{:S(2)}) collective-permute-start(bf16[64,128]{1,0:T(8,128)(2,1)} %embedding_hbm.1), channel_id=1, source_target_pairs={{0,2},{1,3},{2,0},{3,1},{4,6},{5,7},{6,4},{7,5},{8,10},{9,11},{10,... | collective-permute-start | bytes 49160 | tf_op jit(solution)/shard_map/ppermute | solution.py:275
  5.2 0.0 collective-permute-start.2
  5.2 0.0 copy-start.4
  5.2 0.0 copy-done.3
  5.2 0.6 %copy-done.4 = s32[2]{0:T(128)S(1)} copy-done((s32[2]{0:T(128)S(1)}, s32[2]{0:T(128)}, u32[]{:S(2)}) %copy-start.4) | copy-done | bytes 32
  5.9 0.0 copy-done.5
  5.9 0.9 %copy-done = bf16[3,3,48,128]{3,2,1,0:T(8,128)(2,1)S(1)} copy-done((bf16[3,3,48,128]{3,2,1,0:T(8,128)(2,1)S(1)}, bf16[3,3,48,128]{3,2,1,0:T(8,128)(2,1)}, u32[]{:S(2)}) %copy-start) | copy-done | bytes 110616
  6.8 0.8 %copy-done.1 = bf16[5,32,64]{2,1,0:T(8,128)(2,1)S(1)} copy-done((bf16[5,32,64]{2,1,0:T(8,128)(2,1)S(1)}, bf16[5,32,64]{2,1,0:T(8,128)(2,1)}, u32[]{:S(2)}) %copy-start.1) | copy-done | bytes 20504
  7.6 0.7 %copy-done.2 = bf16[64,128]{1,0:T(8,128)(2,1)S(1)} copy-done((bf16[64,128]{1,0:T(8,128)(2,1)S(1)}, bf16[64,128]{1,0:T(8,128)(2,1)}, u32[]{:S(2)}) %copy-start.2) | copy-done | bytes 16408
  8.3 1.3 %prepare.1 = (bf16[64,128]{1,0:T(8,128)(2,1)S(1)}, s32[16,128]{1,0:T(8,128)S(1)}, bf16[2,256,384]{2,1,0:T(8,128)(2,1)S(1)}, bf16[384,768]{1,0:T(8,128)(2,1)S(1)}...) custom-call(bf16[64,128]{1,0:T(8,128)(2,1)S(1)} %copy-done.2, s32[2]{0:T(128)S(1)} %copy-done.4, ...), custom_call_target="tpu_custom_call" | custom-call | flops 4000000000 | bytes 1000 | tf_op jit(solution)/shard_map/prepare/pallas_call | solution.py:297
  9.6 0.0 collective-permute-done.refs_1_
  9.6 0.0 collective-permute-done.1.refs_2_
  9.6 0.4 %collective-permute-done.2.refs_3_ = bf16[64,128]{1,0:T(8,128)(2,1)S(1)} collective-permute-done((bf16[64,128]{1,0:T(8,128)(2,1)}, bf16[64,128]{1,0:T(8,128)(2,1)S(1)}, u32[]{:S(2)}, u32[]{:S(2)}) %collective-permute-start.2) | collective-permute-done | bytes 16416 | tf_op jit(solution)/shard_map/ppermute | solution.py:275
  10.0 4.2 %contact_head.1 = (bf16[2048,128]{1,0:T(8,128)(2,1)S(1)}, bf16[352,128]{1,0:T(8,128)(2,1)S(1)}, bf16[352,128]{1,0:T(8,128)(2,1)S(1)}) custom-call(bf16[64,128]{1,0:T(8,128)(2,1)S(1)} %get-tuple-element.17.refs_0_, bf16[64,128]{1,0:T(8,128)(2,1)S(1)} %collective-permute-done.refs_1_, bf16[64,128]{1,0:T(8,128)(2,1)S(1)} %collective-permute-done.1.refs_2_, ...), custom_call_target="tpu_custom_call" | custom-call | flops 20000000000 | bytes 1000 | tf_op jit(solution)/shard_map/contact_head/pallas_call | solution.py:297
  14.2 0.1 collective-permute-start.3
  14.3 1.3 %collective-permute-done.3 = bf16[352,128]{1,0:T(8,128)(2,1)S(1)} collective-permute-done((bf16[352,128]{1,0:T(8,128)(2,1)S(1)}, bf16[352,128]{1,0:T(8,128)(2,1)S(1)}, u32[]{:S(2)}, u32[]{:S(2)}) %collective-permute-start.3) | collective-permute-done | bytes 90144 | tf_op jit(solution)/shard_map/ppermute | solution.py:275
  15.6 1.6 %collective-permute-start.4 = (bf16[352,128]{1,0:T(8,128)(2,1)S(1)}, bf16[352,128]{1,0:T(8,128)(2,1)S(1)}, u32[]{:S(2)}, u32[]{:S(2)}) collective-permute-start(bf16[352,128]{1,0:T(8,128)(2,1)S(1)} %add.18), channel_id=1, source_target_pairs={{0,1},{1,0},{2,3},{3,2},{4,5},{5,4},{6,7},{7,6},{8,9},{9,8},{10,11... | collective-permute-start | bytes 270344 | tf_op jit(solution)/shard_map/ppermute | solution.py:275
  17.2 3.2 %collective-permute-done.4 = bf16[352,128]{1,0:T(8,128)(2,1)S(1)} collective-permute-done((bf16[352,128]{1,0:T(8,128)(2,1)S(1)}, bf16[352,128]{1,0:T(8,128)(2,1)S(1)}, u32[]{:S(2)}, u32[]{:S(2)}) %collective-permute-start.4) | collective-permute-done | bytes 90144 | tf_op jit(solution)/shard_map/ppermute | solution.py:275
  20.4 1.6 %collective-permute-start.5 = (bf16[352,128]{1,0:T(8,128)(2,1)S(1)}, bf16[352,128]{1,0:T(8,128)(2,1)S(1)}, u32[]{:S(2)}, u32[]{:S(2)}) collective-permute-start(bf16[352,128]{1,0:T(8,128)(2,1)S(1)} %add.19), channel_id=1, source_target_pairs={{0,2},{1,3},{2,0},{3,1},{4,6},{5,7},{6,4},{7,5},{8,10},{9,11},{10,... | collective-permute-start | bytes 270344 | tf_op jit(solution)/shard_map/ppermute | solution.py:275
  22.0 0.7 %copy-done.6 = f32[5]{0:T(128)S(1)} copy-done((f32[5]{0:T(128)S(1)}, f32[5]{0:T(128)}, u32[]{:S(2)}) %copy-start.6) | copy-done | bytes 44
  22.6 0.8 %contact.1 = f32[5,2048]{1,0:T(8,128)S(1)} custom-call(f32[5]{0:T(128)S(1)} %copy-done.6, f32[16,128]{1,0:T(8,128)S(1)} %get-tuple-element.25.mix_ref, bf16[2048,128]{1,0:T(8,128)(2,1)S(1)} %get-tuple-element.26.active_ref), custom_call_target="tpu_custom_call" | custom-call | flops 1000000000 | bytes 1000 | tf_op jit(solution)/shard_map/contact/pallas_call | solution.py:297
  23.4 0.7 %reshape.16 = f32[5,32,64]{2,1,0:T(8,128)} reshape(f32[5,2048]{1,0:T(8,128)S(1)} %contact.1) | data formatting | bytes 81920 | tf_op jit(solution)/shard_map/reshape | solution.py:368
  24.1 0.8 %collective-permute-done.5 = bf16[352,128]{1,0:T(8,128)(2,1)S(1)} collective-permute-done((bf16[352,128]{1,0:T(8,128)(2,1)S(1)}, bf16[352,128]{1,0:T(8,128)(2,1)S(1)}, u32[]{:S(2)}, u32[]{:S(2)}) %collective-permute-start.5) | collective-permute-done | bytes 90144 | tf_op jit(solution)/shard_map/ppermute | solution.py:275
  25.0 1.7 %collective-permute-start.6 = (bf16[352,128]{1,0:T(8,128)(2,1)S(1)}, bf16[352,128]{1,0:T(8,128)(2,1)S(1)}, u32[]{:S(2)}, u32[]{:S(2)}) collective-permute-start(bf16[352,128]{1,0:T(8,128)(2,1)S(1)} %add.20), channel_id=1, source_target_pairs={{0,8},{4,12},{8,0},{12,4},{16,24},{20,28},{24,16},{28,20},{1,9},{5... | collective-permute-start | bytes 270344 | tf_op jit(solution)/shard_map/ppermute | solution.py:275
  26.7 2.9 %collective-permute-done.6 = bf16[352,128]{1,0:T(8,128)(2,1)S(1)} collective-permute-done((bf16[352,128]{1,0:T(8,128)(2,1)S(1)}, bf16[352,128]{1,0:T(8,128)(2,1)S(1)}, u32[]{:S(2)}, u32[]{:S(2)}) %collective-permute-start.6) | collective-permute-done | bytes 90144 | tf_op jit(solution)/shard_map/ppermute | solution.py:275
  29.6 3.1 %collective-permute-start.7 = (bf16[352,128]{1,0:T(8,128)(2,1)S(1)}, bf16[352,128]{1,0:T(8,128)(2,1)S(1)}, u32[]{:S(2)}, u32[]{:S(2)}) collective-permute-start(bf16[352,128]{1,0:T(8,128)(2,1)S(1)} %add.21), channel_id=1, source_target_pairs={{0,16},{4,20},{8,24},{12,28},{16,0},{20,4},{24,8},{28,12},{1,17},{... | collective-permute-start | bytes 270344 | tf_op jit(solution)/shard_map/ppermute | solution.py:275
  32.7 2.5 %collective-permute-done.7 = bf16[352,128]{1,0:T(8,128)(2,1)S(1)} collective-permute-done((bf16[352,128]{1,0:T(8,128)(2,1)S(1)}, bf16[352,128]{1,0:T(8,128)(2,1)S(1)}, u32[]{:S(2)}, u32[]{:S(2)}) %collective-permute-start.7) | collective-permute-done | bytes 90144 | tf_op jit(solution)/shard_map/ppermute | solution.py:275
  35.3 0.1 collective-permute-start.8
  35.4 1.2 %collective-permute-done.8.other_ref = bf16[256,128]{1,0:T(8,128)(2,1)S(1)} collective-permute-done((bf16[256,128]{1,0:T(8,128)(2,1)S(1)}, bf16[256,128]{1,0:T(8,128)(2,1)S(1)}, u32[]{:S(2)}, u32[]{:S(2)}) %collective-permute-start.8) | collective-permute-done | bytes 65568 | tf_op jit(solution)/shard_map/ppermute | solution.py:275
  36.6 0.7 %join.1 = (f32[64,128]{1,0:T(8,128)}, f32[432,128]{1,0:T(8,128)}) custom-call(bf16[256,128]{1,0:T(8,128)(2,1)S(1)} %pad_maximum_fusion.mine_ref, bf16[256,128]{1,0:T(8,128)(2,1)S(1)} %collective-permute-done.8.other_ref), custom_call_target="tpu_custom_call" | custom-call | flops 1000 | bytes 1000 | tf_op jit(solution)/shard_map/join/pallas_call | solution.py:297
  (14 shorter events, 0.2 us)
Async XLA Ops:
  0.6 4.6 %copy-start.3 = (bf16[5,48]{1,0:T(8,128)(2,1)S(1)}, bf16[5,48]{1,0:T(8,128)(2,1)}, u32[]{:S(2)}) copy-start(bf16[5,48]{1,0:T(8,128)(2,1)} %mixing_hbm.1) | copy-start | bytes 1444
  0.6 8.9 %collective-permute-start = (bf16[64,128]{1,0:T(8,128)(2,1)}, bf16[64,128]{1,0:T(8,128)(2,1)S(1)}, u32[]{:S(2)}, u32[]{:S(2)}) collective-permute-start(bf16[64,128]{1,0:T(8,128)(2,1)} %embedding_hbm.1), channel_id=1, source_target_pairs={{0,1},{1,0},{2,3},{3,2},{4,5},{5,4},{6,7},{7,6},{8,9},{9,8},{10,11... | collective-permute-start | bytes 49160 | tf_op jit(solution)/shard_map/ppermute | solution.py:275
  3.7 5.9 %collective-permute-start.1 = (bf16[64,128]{1,0:T(8,128)(2,1)}, bf16[64,128]{1,0:T(8,128)(2,1)S(1)}, u32[]{:S(2)}, u32[]{:S(2)}) collective-permute-start(bf16[64,128]{1,0:T(8,128)(2,1)} %embedding_hbm.1), channel_id=1, source_target_pairs={{0,2},{1,3},{2,0},{3,1},{4,6},{5,7},{6,4},{7,5},{8,10},{9,11},{10,... | collective-permute-start | bytes 49160 | tf_op jit(solution)/shard_map/ppermute | solution.py:275
  5.2 4.8 %collective-permute-start.2 = (bf16[64,128]{1,0:T(8,128)(2,1)}, bf16[64,128]{1,0:T(8,128)(2,1)S(1)}, u32[]{:S(2)}, u32[]{:S(2)}) collective-permute-start(bf16[64,128]{1,0:T(8,128)(2,1)} %embedding_hbm.1), channel_id=1, source_target_pairs={{0,3},{1,2},{2,1},{3,0},{4,7},{5,6},{6,5},{7,4},{8,11},{9,10},{10,... | collective-permute-start | bytes 49160 | tf_op jit(solution)/shard_map/ppermute | solution.py:275
  5.2 0.7 %copy-start.4 = (s32[2]{0:T(128)S(1)}, s32[2]{0:T(128)}, u32[]{:S(2)}) copy-start(s32[2]{0:T(128)} %dilation_hbm.1) | copy-start | bytes 28
  5.2 0.7 %copy-start.5 = (f32[48]{0:T(128)S(1)}, f32[48]{0:T(128)}, u32[]{:S(2)}) copy-start(f32[48]{0:T(128)} %param.10) | copy-start | bytes 580
  5.9 0.9 %copy-start = (bf16[3,3,48,128]{3,2,1,0:T(8,128)(2,1)S(1)}, bf16[3,3,48,128]{3,2,1,0:T(8,128)(2,1)}, u32[]{:S(2)}) copy-start(bf16[3,3,48,128]{3,2,1,0:T(8,128)(2,1)} %param.9) | copy-start | bytes 331780
  6.8 0.8 %copy-start.1 = (bf16[5,32,64]{2,1,0:T(8,128)(2,1)S(1)}, bf16[5,32,64]{2,1,0:T(8,128)(2,1)}, u32[]{:S(2)}) copy-start(bf16[5,32,64]{2,1,0:T(8,128)(2,1)} %cot_hbm.1) | copy-start | bytes 61444
  7.6 0.7 %copy-start.2 = (bf16[64,128]{1,0:T(8,128)(2,1)S(1)}, bf16[64,128]{1,0:T(8,128)(2,1)}, u32[]{:S(2)}) copy-start(bf16[64,128]{1,0:T(8,128)(2,1)} %embedding_hbm.1) | copy-start | bytes 49156
  14.2 1.4 %collective-permute-start.3 = (bf16[352,128]{1,0:T(8,128)(2,1)S(1)}, bf16[352,128]{1,0:T(8,128)(2,1)S(1)}, u32[]{:S(2)}, u32[]{:S(2)}) collective-permute-start(bf16[352,128]{1,0:T(8,128)(2,1)S(1)} %get-tuple-element.24), channel_id=1, source_target_pairs={{0,4},{4,0},{8,12},{12,8},{16,20},{20,16},{24,28},{28,24},{1,5},{5... | collective-permute-start | bytes 270344 | tf_op jit(solution)/shard_map/ppermute | solution.py:275
  15.6 4.7 %collective-permute-start.4 = (bf16[352,128]{1,0:T(8,128)(2,1)S(1)}, bf16[352,128]{1,0:T(8,128)(2,1)S(1)}, u32[]{:S(2)}, u32[]{:S(2)}) collective-permute-start(bf16[352,128]{1,0:T(8,128)(2,1)S(1)} %add.18), channel_id=1, source_target_pairs={{0,1},{1,0},{2,3},{3,2},{4,5},{5,4},{6,7},{7,6},{8,9},{9,8},{10,11... | collective-permute-start | bytes 270344 | tf_op jit(solution)/shard_map/ppermute | solution.py:275
  20.4 4.6 %collective-permute-start.5 = (bf16[352,128]{1,0:T(8,128)(2,1)S(1)}, bf16[352,128]{1,0:T(8,128)(2,1)S(1)}, u32[]{:S(2)}, u32[]{:S(2)}) collective-permute-start(bf16[352,128]{1,0:T(8,128)(2,1)S(1)} %add.19), channel_id=1, source_target_pairs={{0,2},{1,3},{2,0},{3,1},{4,6},{5,7},{6,4},{7,5},{8,10},{9,11},{10,... | collective-permute-start | bytes 270344 | tf_op jit(solution)/shard_map/ppermute | solution.py:275
  22.0 0.7 %copy-start.6 = (f32[5]{0:T(128)S(1)}, f32[5]{0:T(128)}, u32[]{:S(2)}) copy-start(f32[5]{0:T(128)} %mix_bias_ref.1) | copy-start | bytes 64
  25.0 4.6 %collective-permute-start.6 = (bf16[352,128]{1,0:T(8,128)(2,1)S(1)}, bf16[352,128]{1,0:T(8,128)(2,1)S(1)}, u32[]{:S(2)}, u32[]{:S(2)}) collective-permute-start(bf16[352,128]{1,0:T(8,128)(2,1)S(1)} %add.20), channel_id=1, source_target_pairs={{0,8},{4,12},{8,0},{12,4},{16,24},{20,28},{24,16},{28,20},{1,9},{5... | collective-permute-start | bytes 270344 | tf_op jit(solution)/shard_map/ppermute | solution.py:275
  29.6 5.6 %collective-permute-start.7 = (bf16[352,128]{1,0:T(8,128)(2,1)S(1)}, bf16[352,128]{1,0:T(8,128)(2,1)S(1)}, u32[]{:S(2)}, u32[]{:S(2)}) collective-permute-start(bf16[352,128]{1,0:T(8,128)(2,1)S(1)} %add.21), channel_id=1, source_target_pairs={{0,16},{4,20},{8,24},{12,28},{16,0},{20,4},{24,8},{28,12},{1,17},{... | collective-permute-start | bytes 270344 | tf_op jit(solution)/shard_map/ppermute | solution.py:275
  35.3 1.3 %collective-permute-start.8 = (bf16[256,128]{1,0:T(8,128)(2,1)S(1)}, bf16[256,128]{1,0:T(8,128)(2,1)S(1)}, u32[]{:S(2)}, u32[]{:S(2)}) collective-permute-start(bf16[256,128]{1,0:T(8,128)(2,1)S(1)} %pad_maximum_fusion.mine_ref), channel_id=1, source_target_pairs={{0,4},{4,0},{8,12},{12,8},{16,20},{20,16},{24,28},{28,24},{1,5},{5... | collective-permute-start | bytes 196616 | tf_op jit(solution)/shard_map/ppermute | solution.py:275

commit v4 on v3

--- a/solution.py
+++ b/solution.py
@@ -13,6 +13,15 @@
 TAPS = [(a, b) for a in STEPS for b in STEPS]
 LANES = 128
 HALF = LANES // 2
+
+
+def slot_order(peers):
+    order = [0]
+    mask = peers // 2
+    while mask:
+        order = order + [slot | mask for slot in order]
+        mask //= 2
+    return order
 
 
 def contract(left, right, dims):
@@ -104,7 +113,9 @@
     block_refs = refs[:peers]
     rate_ref, weight_ref, wide_ref, guide_ref, bias_ref = refs[peers : peers + 5]
     active_ref, send_ref, keep_ref = refs[peers + 5 : peers + 8]
-    bins_ref, pair_ref, conv_ref, grad_ref, turned_ref, acc_ref, taps_ref = refs[peers + 8 :]
+    bins_ref, pair_ref, conv_ref, center_ref, eights_ref, grad_ref, turned_ref, acc_ref, taps_ref = (
+        refs[peers + 8 :]
+    )
     row_rate = jnp.max(rate_ref[0:8, :])
     col_rate = jnp.max(rate_ref[8:16, :])
     row_index = lax.axis_index("row")
@@ -148,12 +159,16 @@
     def shifted_columns(first, last):
         return jnp.concatenate([pair_ref[first], pair_ref[0], pair_ref[last]], axis=1)
 
-    conv_ref[0] = contract(shifted_columns(1, 2), weight_ref[0], ((1,), (1,)))
-    conv_ref[1] = contract(shifted_columns(3, 4), weight_ref[1], ((1,), (1,)))
-
     lane = lax.broadcasted_iota(jnp.int32, (1, LANES), 1)
     is_mirror = lane >= HALF
-    bias = bias_ref[0:1, :]
+    center = slice(DMAX * cols, (DMAX + rows) * cols)
+    direct = contract(shifted_columns(1, 2), weight_ref[0], ((1,), (1,)))
+    conv_ref[0] = direct
+    mirror = contract(shifted_columns(3, 4), weight_ref[1], ((1,), (1,)))
+    conv_ref[1] = mirror
+    swapped = jnp.where(is_mirror, direct[center, :LANES], mirror[center, :LANES])
+    center_ref[...] = pltpu.roll(swapped, HALF, 1) + bias_ref[0:1, :]
+
     row_keeps = []
     for q in STEPS:
         place = col_place + jnp.where(is_mirror, q * row_rate, q * col_rate)
@@ -161,42 +176,41 @@
     margin = PAD * cols
     grad_ref[0:margin, :] = jnp.zeros((margin, LANES), bf16)
     grad_ref[margin + rows * cols : 2 * margin + rows * cols, :] = jnp.zeros((margin, LANES), bf16)
-    row_sums = [[], [], []]
-    col_middle = None
-    col_edges = [None, None, None]
-
-    def add(total, term):
-        return term if total is None else total + term
-
-    for i in range(rows):
+    last = cols - 8
+
+    def row_step(i, col_total):
         def part(mirrored, shift, group):
             first = pl.multiple_of((DMAX + i + shift) * cols, cols)
             return conv_ref[mirrored, pl.ds(first, cols), group * LANES : (group + 1) * LANES]
 
-        swapped = jnp.where(is_mirror, part(0, 0, 0), part(1, 0, 0))
+        here = pl.ds(pl.multiple_of(i * cols, cols), cols)
         conv = jnp.where(is_mirror, part(1, -col_rate, 0), part(0, -row_rate, 0))
-        conv = conv + pltpu.roll(swapped, HALF, 1)
+        conv = conv + center_ref[here, :]
         conv = conv + (part(0, row_rate, 1) + part(1, col_rate, 1))
-        conv = conv + bias
-        here = slice(i * cols, (i + 1) * cols)
         grad = jnp.where(conv > 0, guide_ref[here, :].astype(f32), 0.0)
         active_ref[here, :] = jnp.maximum(conv, 0.0).astype(bf16)
-        grad_ref[margin + i * cols : margin + (i + 1) * cols, :] = grad.astype(bf16)
-        last = cols - 8
+        grad_ref[pl.ds(pl.multiple_of(margin + i * cols, cols), cols), :] = grad.astype(bf16)
         inner = grad[8:16]
         for j in range(16, last, 8):
             inner = inner + grad[j : j + 8]
         for q in range(3):
             keep = row_keeps[q]
             eight = inner + grad[0:8] * keep[0:8] + grad[last:cols] * keep[last:cols]
-            row_sums[q].append(jnp.sum(eight, axis=0, keepdims=True))
-            if i < DMAX or i >= rows - DMAX:
-                step = STEPS[q]
-                place = row_start + i + jnp.where(is_mirror, step * col_rate, step * row_rate)
-                keep = ((place >= 0) & (place < bins)).astype(f32)
-                col_edges[q] = add(col_edges[q], grad * keep)
-        if DMAX <= i < rows - DMAX:
-            col_middle = add(col_middle, grad)
+            eights_ref[q, pl.ds(pl.multiple_of(i * 8, 8), 8), :] = eight
+        return col_total + grad
+
+    col_total = lax.fori_loop(0, rows, row_step, jnp.zeros((cols, LANES), f32), unroll=4)
+    row_sums = []
+    col_sums = []
+    for q in range(3):
+        row_sums.append(jnp.sum(eights_ref[q].reshape(rows, 8, LANES), axis=1))
+        total = col_total
+        for i in [*range(DMAX), *range(rows - DMAX, rows)]:
+            step = STEPS[q]
+            place = row_start + i + jnp.where(is_mirror, step * col_rate, step * row_rate)
+            drop = ((place < 0) | (place >= bins)).astype(f32)
+            total = total - grad_ref[margin + i * cols : margin + (i + 1) * cols, :].astype(f32) * drop
+        col_sums.append(pltpu.roll(total, HALF, 1))
 
     chunks = (2 * margin + rows * cols) // LANES
     first_chunk = margin // LANES
@@ -229,8 +243,6 @@
             + mirror[b * filters : (b + 1) * filters, a * LANES : (a + 1) * LANES]
         )
 
-    row_sums = [jnp.concatenate(sums, axis=0) for sums in row_sums]
-    col_sums = [pltpu.roll(col_middle + edges, HALF, 1) for edges in col_edges]
     sums = jnp.concatenate(
         [jnp.concatenate(row_sums, axis=1), jnp.concatenate(col_sums, axis=1)], axis=0
     ).astype(bf16)
@@ -246,14 +258,15 @@
 
     total_rows = count * filters
     for target, which in ((keep_ref, core), (send_ref, 1 - core)):
-        first = pl.multiple_of(which * (total_rows - half), 16)
-        target[0:half, :] = taps_ref[pl.ds(first, half), :].astype(bf16)
         part = cols // 2
-        for step in range(peers):
-            first = pl.multiple_of(which * part + (step * cols + PAD), 8)
-            target[half + step * part : half + (step + 1) * part, :] = (
+        for slot, step in enumerate(slot_order(peers)):
+            block = jnp.bitwise_xor(col_index, step)
+            first = pl.multiple_of(block * cols + which * part + PAD, 8)
+            target[slot * part : (slot + 1) * part, :] = (
                 0.5 * acc_ref[pl.ds(first, part), :]
             ).astype(bf16)
+        first = pl.multiple_of(which * (total_rows - half), 16)
+        target[peers * part : peers * part + half, :] = taps_ref[pl.ds(first, half), :].astype(bf16)
 
 
 def join_kernel(half, mine_ref, other_ref, embedding_ref, taps_ref):
@@ -264,10 +277,10 @@
     other = other_ref[...].astype(jnp.float32)
     low = jnp.where(core == 0, mine, other)
     high = jnp.where(core == 0, other, mine)
-    taps_ref[0 : total_rows - half, :] = low[0 : total_rows - half]
-    taps_ref[total_rows - half : total_rows, :] = high[0:half]
-    embedding_ref[0:part, :] = low[half : half + part]
-    embedding_ref[part : 2 * part, :] = high[half : half + part]
+    taps_ref[0 : total_rows - half, :] = low[part : part + total_rows - half]
+    taps_ref[total_rows - half : total_rows, :] = high[part : part + half]
+    embedding_ref[0:part, :] = low[0:part]
+    embedding_ref[part : 2 * part, :] = high[0:part]
 
 
 def swap(value, axis, mask):
@@ -283,8 +296,7 @@
     peers = lax.axis_size("col")
     row_peers = lax.axis_size("row")
     bins = cols * peers
-    col_index = lax.axis_index("col")
-    blocks = [embedding] + [swap(embedding, "col", mask) for mask in range(1, peers)]
+    blocks = [swap(embedding, "col", mask) for mask in range(peers - 1, 0, -1)]
     taps = len(TAPS)
     taps_rows = taps * filters
     half = (taps_rows // 2 + 15) // 16 * 16
@@ -319,7 +331,10 @@
             shape((16, LANES), f32),
             shape((8, LANES), f32),
         ),
-        (embedding, dilation, kernels, kernel_bias[None, :], mixing, cotangent),
+        [
+            pltpu.with_memory_space_constraint(value, pltpu.HBM)
+            for value in (embedding, dilation, kernels, kernel_bias[None, :], mixing, cotangent)
+        ],
         scratch=(
             pltpu.SMEM((2,), jnp.int32),
             pltpu.VMEM(kernels.shape, bf16),
@@ -332,7 +347,7 @@
         specs=[pl.BlockSpec(memory_space=pltpu.HBM)] * 6,
         flops=4_000_000_000,
     )
-    blocks[0] = own
+    blocks = [own] + blocks[::-1]
     extended = (rows + 2 * DMAX) * cols
     padded = spots + 2 * PAD * cols
     active, send, keep = call(
@@ -344,6 +359,8 @@
             pltpu.VMEM((bins + 2 * PAD, LANES), f32),
             pltpu.VMEM((5, extended, LANES), bf16),
             pltpu.VMEM((2, extended, 2 * LANES), f32),
+            pltpu.VMEM((spots, LANES), f32),
+            pltpu.VMEM((3, rows * 8, LANES), f32),
             pltpu.VMEM((padded, LANES), bf16),
             pltpu.VMEM((2, LANES, padded), bf16),
             pltpu.VMEM((bins + 2 * PAD, LANES), f32),
@@ -356,7 +373,9 @@
     total = keep + swap(send, "row", 1)
     mask = 1
     while mask < peers:
-        total = total + swap(total, "col", mask)
+        kept = peers * (cols // 2) // (2 * mask)
+        got = swap(total[kept:], "col", mask)
+        total = jnp.concatenate([total[:kept] + got[:kept], total[2 * kept :] + got[kept:]], axis=0)
         mask *= 2
     contact = call(
         contact_kernel,
@@ -371,15 +390,12 @@
     while mask < row_peers:
         total = total + swap(total, "row", mask)
         mask *= 2
-    part = cols // 2
-    mine = lax.dynamic_slice_in_dim(total[half:], col_index * part, part, 0)
-    mine = jnp.concatenate([total[:half], mine], axis=0)
-    other = swap(mine, "row", 1)
+    other = swap(total, "row", 1)
     embedding_grad, kernel_grad = call(
         functools.partial(join_kernel, half),
         "join",
         (shape((cols, channels), f32), shape((taps_rows, channels), f32)),
-        (mine, other),
+        (total, other),
         limit=4,
     )
     return contact, embedding_grad, kernel_grad.reshape(kernel.shape)

time: 37.6 us -> 35.3 us (0.939)
  local copies, waits for them, and re-layouts: 4.47 us -> 1.39 us
  waiting for transfers between devices: 12.5 us -> 13.9 us
  starting transfers between devices: 12.6 us -> 12.2 us
    unnamed x14 -> x2, local copies, waits for them, and re-layouts: 3.72 us -> 0.65 us
    ppermute x9, waiting for transfers between devices: 12.5 us -> 13.9 us  [swap(): return lax.ppermute(value, axis, [(i, i ^ mask) for i in range(peers)])]
    ppermute x9, starting transfers between devices: 12.6 us -> 12.2 us  [swap(): return lax.ppermute(value, axis, [(i, i ^ mask) for i in range(peers)])]
  transfers between devices with their start and end apart: 9 -> 9, of which waited for: 7 -> 8; matrix products, arithmetic and copies ran while one was open for 2% -> 2% of each run, Pallas kernels for 6% -> 6%
where the time goes in v4:
time: 35.3 us; the launch traced here: 35.2 us
  waiting for transfers between devices  13.9 us (39%)
  starting transfers between devices  12.2 us (35%)
  Pallas kernels  6.83 us (19%)
  local copies, waits for them, and re-layouts  1.39 us (4%)
  between operations  0.72 us (2%)
    ppermute x9, waiting for transfers between devices, swap(): return lax.ppermute(value, axis, [(i, i ^ mask) for i in range(peers)])  13.9 us
    ppermute x9, starting transfers between devices, swap(): return lax.ppermute(value, axis, [(i, i ^ mask) for i in range(peers)])  12.2 us
    pallas_call x4, Pallas kernels, call(): pl.pallas_call(body, out_shape=out_shape, in_specs=specs or [vmem] * len(...  6.83 us
    reshape x1, local copies, waits for them, and re-layouts, per_device(): contact = call(contact_kernel, 'contact', shape((maps, spots), f32), (mix...  0.73 us
  transfers between devices with their start and end apart: 9, of which 8 were waited for; matrix products, arithmetic and copies ran while one was open for 2% of the time, Pallas kernels for 6%

profile of v4, /device:TPU:0, one launch (start us, length us, event | category | flops | bytes accessed | tf_op | source)
XLA Modules:
  0.0 35.2 jit_solution(1890107197411507414)
XLA Ops:
  0.6 3.0 %collective-permute-start = (bf16[64,128]{1,0:T(8,128)(2,1)}, bf16[64,128]{1,0:T(8,128)(2,1)S(1)}, u32[]{:S(2)}, u32[]{:S(2)}) collective-permute-start(bf16[64,128]{1,0:T(8,128)(2,1)} %embedding_hbm.1), channel_id=1, source_target_pairs={{0,1},{1,0},{2,3},{3,2},{4,5},{5,4},{6,7},{7,6},{8,9},{9,8},{10,11... | collective-permute-start | bytes 49160 | tf_op jit(solution)/shard_map/ppermute | solution.py:288
  3.7 1.5 %collective-permute-start.2 = (bf16[64,128]{1,0:T(8,128)(2,1)}, bf16[64,128]{1,0:T(8,128)(2,1)S(1)}, u32[]{:S(2)}, u32[]{:S(2)}) collective-permute-start(bf16[64,128]{1,0:T(8,128)(2,1)} %embedding_hbm.1), channel_id=1, source_target_pairs={{0,3},{1,2},{2,1},{3,0},{4,7},{5,6},{6,5},{7,4},{8,11},{9,10},{10,... | collective-permute-start | bytes 49160 | tf_op jit(solution)/shard_map/ppermute | solution.py:288
  5.2 0.0 collective-permute-start.1
  5.2 1.5 %prepare.1 = (bf16[64,128]{1,0:T(8,128)(2,1)S(1)}, s32[16,128]{1,0:T(8,128)S(1)}, bf16[2,256,384]{2,1,0:T(8,128)(2,1)S(1)}, bf16[384,768]{1,0:T(8,128)(2,1)S(1)}...) custom-call(bf16[64,128]{1,0:T(8,128)(2,1)} %embedding_hbm.1, s32[2]{0:T(128)} %dilation_hbm.1, ...), custom_call_target="tpu_custom_call" | custom-call | flops 4000000000 | bytes 1000 | tf_op jit(solution)/shard_map/prepare/pallas_call | solution.py:309
  6.7 0.0 collective-permute-done.refs_1_
  6.7 1.8 %collective-permute-done.2.refs_3_ = bf16[64,128]{1,0:T(8,128)(2,1)S(1)} collective-permute-done((bf16[64,128]{1,0:T(8,128)(2,1)}, bf16[64,128]{1,0:T(8,128)(2,1)S(1)}, u32[]{:S(2)}, u32[]{:S(2)}) %collective-permute-start.2) | collective-permute-done | bytes 16416 | tf_op jit(solution)/shard_map/ppermute | solution.py:288
  8.5 0.6 %collective-permute-done.1.refs_2_ = bf16[64,128]{1,0:T(8,128)(2,1)S(1)} collective-permute-done((bf16[64,128]{1,0:T(8,128)(2,1)}, bf16[64,128]{1,0:T(8,128)(2,1)S(1)}, u32[]{:S(2)}, u32[]{:S(2)}) %collective-permute-start.1) | collective-permute-done | bytes 16416 | tf_op jit(solution)/shard_map/ppermute | solution.py:288
  9.1 3.8 %contact_head.1 = (bf16[2048,128]{1,0:T(8,128)(2,1)S(1)}, bf16[352,128]{1,0:T(8,128)(2,1)S(1)}, bf16[352,128]{1,0:T(8,128)(2,1)S(1)}) custom-call(bf16[64,128]{1,0:T(8,128)(2,1)S(1)} %get-tuple-element.17.refs_0_, bf16[64,128]{1,0:T(8,128)(2,1)S(1)} %collective-permute-done.refs_1_, bf16[64,128]{1,0:T(8,128)(2,1)S(1)} %collective-permute-done.1.refs_2_, ...), custom_call_target="tpu_custom_call" | custom-call | flops 20000000000 | bytes 1000 | tf_op jit(solution)/shard_map/contact_head/pallas_call | solution.py:309
  13.0 0.1 collective-permute-start.3
  13.0 1.3 %collective-permute-done.3 = bf16[352,128]{1,0:T(8,128)(2,1)S(1)} collective-permute-done((bf16[352,128]{1,0:T(8,128)(2,1)S(1)}, bf16[352,128]{1,0:T(8,128)(2,1)S(1)}, u32[]{:S(2)}, u32[]{:S(2)}) %collective-permute-start.3) | collective-permute-done | bytes 90144 | tf_op jit(solution)/shard_map/ppermute | solution.py:288
  14.4 1.5 %collective-permute-start.4 = (bf16[288,128]{1,0:T(8,128)(2,1)S(1)}, bf16[288,128]{1,0:T(8,128)(2,1)S(1)}, u32[]{:S(2)}, u32[]{:S(2)}) collective-permute-start(bf16[288,128]{1,0:T(8,128)(2,1)S(1)} %slice.37), channel_id=1, source_target_pairs={{0,1},{1,0},{2,3},{3,2},{4,5},{5,4},{6,7},{7,6},{8,9},{9,8},{10,11... | collective-permute-start | bytes 221192 | tf_op jit(solution)/shard_map/ppermute | solution.py:288
  15.9 2.9 %collective-permute-done.4 = bf16[288,128]{1,0:T(8,128)(2,1)S(1)} collective-permute-done((bf16[288,128]{1,0:T(8,128)(2,1)S(1)}, bf16[288,128]{1,0:T(8,128)(2,1)S(1)}, u32[]{:S(2)}, u32[]{:S(2)}) %collective-permute-start.4) | collective-permute-done | bytes 73760 | tf_op jit(solution)/shard_map/ppermute | solution.py:288
  18.8 1.0 %collective-permute-start.5 = (bf16[256,128]{1,0:T(8,128)(2,1)S(1)}, bf16[256,128]{1,0:T(8,128)(2,1)S(1)}, u32[]{:S(2)}, u32[]{:S(2)}) collective-permute-start(bf16[256,128]{1,0:T(8,128)(2,1)S(1)} %pad_maximum_fusion), channel_id=1, source_target_pairs={{0,2},{1,3},{2,0},{3,1},{4,6},{5,7},{6,4},{7,5},{8,10},{9,11},{10,... | collective-permute-start | bytes 196616 | tf_op jit(solution)/shard_map/ppermute | solution.py:288
  19.8 0.0 copy-start
  19.8 0.7 %copy-done = f32[5]{0:T(128)S(1)} copy-done((f32[5]{0:T(128)S(1)}, f32[5]{0:T(128)}, u32[]{:S(2)}) %copy-start) | copy-done | bytes 44
  20.4 0.8 %contact.1 = f32[5,2048]{1,0:T(8,128)S(1)} custom-call(f32[5]{0:T(128)S(1)} %copy-done, f32[16,128]{1,0:T(8,128)S(1)} %get-tuple-element.25.mix_ref, bf16[2048,128]{1,0:T(8,128)(2,1)S(1)} %get-tuple-element.26.active_ref), custom_call_target="tpu_custom_call" | custom-call | flops 1000000000 | bytes 1000 | tf_op jit(solution)/shard_map/contact/pallas_call | solution.py:309
  21.2 0.7 %reshape.16 = f32[5,32,64]{2,1,0:T(8,128)} reshape(f32[5,2048]{1,0:T(8,128)S(1)} %contact.1) | data formatting | bytes 81920 | tf_op jit(solution)/shard_map/reshape | solution.py:387
  21.9 1.2 %collective-permute-done.5 = bf16[256,128]{1,0:T(8,128)(2,1)S(1)} collective-permute-done((bf16[256,128]{1,0:T(8,128)(2,1)S(1)}, bf16[256,128]{1,0:T(8,128)(2,1)S(1)}, u32[]{:S(2)}, u32[]{:S(2)}) %collective-permute-start.5) | collective-permute-done | bytes 65568 | tf_op jit(solution)/shard_map/ppermute | solution.py:288
  23.2 1.6 %collective-permute-start.6 = (bf16[256,128]{1,0:T(8,128)(2,1)S(1)}, bf16[256,128]{1,0:T(8,128)(2,1)S(1)}, u32[]{:S(2)}, u32[]{:S(2)}) collective-permute-start(bf16[256,128]{1,0:T(8,128)(2,1)S(1)} %pad_maximum_fusion.1), channel_id=1, source_target_pairs={{0,8},{4,12},{8,0},{12,4},{16,24},{20,28},{24,16},{28,20},{1,9},{5... | collective-permute-start | bytes 196616 | tf_op jit(solution)/shard_map/ppermute | solution.py:288
  24.8 2.7 %collective-permute-done.6 = bf16[256,128]{1,0:T(8,128)(2,1)S(1)} collective-permute-done((bf16[256,128]{1,0:T(8,128)(2,1)S(1)}, bf16[256,128]{1,0:T(8,128)(2,1)S(1)}, u32[]{:S(2)}, u32[]{:S(2)}) %collective-permute-start.6) | collective-permute-done | bytes 65568 | tf_op jit(solution)/shard_map/ppermute | solution.py:288
  27.5 3.3 %collective-permute-start.7 = (bf16[256,128]{1,0:T(8,128)(2,1)S(1)}, bf16[256,128]{1,0:T(8,128)(2,1)S(1)}, u32[]{:S(2)}, u32[]{:S(2)}) collective-permute-start(bf16[256,128]{1,0:T(8,128)(2,1)S(1)} %add.26), channel_id=1, source_target_pairs={{0,16},{4,20},{8,24},{12,28},{16,0},{20,4},{24,8},{28,12},{1,17},{... | collective-permute-start | bytes 196616 | tf_op jit(solution)/shard_map/ppermute | solution.py:288
  30.8 2.3 %collective-permute-done.7 = bf16[256,128]{1,0:T(8,128)(2,1)S(1)} collective-permute-done((bf16[256,128]{1,0:T(8,128)(2,1)S(1)}, bf16[256,128]{1,0:T(8,128)(2,1)S(1)}, u32[]{:S(2)}, u32[]{:S(2)}) %collective-permute-start.7) | collective-permute-done | bytes 65568 | tf_op jit(solution)/shard_map/ppermute | solution.py:288
  33.1 0.1 collective-permute-start.8
  33.2 1.2 %collective-permute-done.8.other_ref = bf16[256,128]{1,0:T(8,128)(2,1)S(1)} collective-permute-done((bf16[256,128]{1,0:T(8,128)(2,1)S(1)}, bf16[256,128]{1,0:T(8,128)(2,1)S(1)}, u32[]{:S(2)}, u32[]{:S(2)}) %collective-permute-start.8) | collective-permute-done | bytes 65568 | tf_op jit(solution)/shard_map/ppermute | solution.py:288
  34.5 0.7 %join.1 = (f32[64,128]{1,0:T(8,128)}, f32[432,128]{1,0:T(8,128)}) custom-call(bf16[256,128]{1,0:T(8,128)(2,1)S(1)} %add.27.mine_ref, bf16[256,128]{1,0:T(8,128)(2,1)S(1)} %collective-permute-done.8.other_ref), custom_call_target="tpu_custom_call" | custom-call | flops 1000 | bytes 1000 | tf_op jit(solution)/shard_map/join/pallas_call | solution.py:309
  (10 shorter events, 0.1 us)
Async XLA Ops:
  0.6 6.1 %collective-permute-start = (bf16[64,128]{1,0:T(8,128)(2,1)}, bf16[64,128]{1,0:T(8,128)(2,1)S(1)}, u32[]{:S(2)}, u32[]{:S(2)}) collective-permute-start(bf16[64,128]{1,0:T(8,128)(2,1)} %embedding_hbm.1), channel_id=1, source_target_pairs={{0,1},{1,0},{2,3},{3,2},{4,5},{5,4},{6,7},{7,6},{8,9},{9,8},{10,11... | collective-permute-start | bytes 49160 | tf_op jit(solution)/shard_map/ppermute | solution.py:288
  3.7 4.8 %collective-permute-start.2 = (bf16[64,128]{1,0:T(8,128)(2,1)}, bf16[64,128]{1,0:T(8,128)(2,1)S(1)}, u32[]{:S(2)}, u32[]{:S(2)}) collective-permute-start(bf16[64,128]{1,0:T(8,128)(2,1)} %embedding_hbm.1), channel_id=1, source_target_pairs={{0,3},{1,2},{2,1},{3,0},{4,7},{5,6},{6,5},{7,4},{8,11},{9,10},{10,... | collective-permute-start | bytes 49160 | tf_op jit(solution)/shard_map/ppermute | solution.py:288
  5.2 3.9 %collective-permute-start.1 = (bf16[64,128]{1,0:T(8,128)(2,1)}, bf16[64,128]{1,0:T(8,128)(2,1)S(1)}, u32[]{:S(2)}, u32[]{:S(2)}) collective-permute-start(bf16[64,128]{1,0:T(8,128)(2,1)} %embedding_hbm.1), channel_id=1, source_target_pairs={{0,2},{1,3},{2,0},{3,1},{4,6},{5,7},{6,4},{7,5},{8,10},{9,11},{10,... | collective-permute-start | bytes 49160 | tf_op jit(solution)/shard_map/ppermute | solution.py:288
  13.0 1.4 %collective-permute-start.3 = (bf16[352,128]{1,0:T(8,128)(2,1)S(1)}, bf16[352,128]{1,0:T(8,128)(2,1)S(1)}, u32[]{:S(2)}, u32[]{:S(2)}) collective-permute-start(bf16[352,128]{1,0:T(8,128)(2,1)S(1)} %get-tuple-element.24), channel_id=1, source_target_pairs={{0,4},{4,0},{8,12},{12,8},{16,20},{20,16},{24,28},{28,24},{1,5},{5... | collective-permute-start | bytes 270344 | tf_op jit(solution)/shard_map/ppermute | solution.py:288
  14.4 4.4 %collective-permute-start.4 = (bf16[288,128]{1,0:T(8,128)(2,1)S(1)}, bf16[288,128]{1,0:T(8,128)(2,1)S(1)}, u32[]{:S(2)}, u32[]{:S(2)}) collective-permute-start(bf16[288,128]{1,0:T(8,128)(2,1)S(1)} %slice.37), channel_id=1, source_target_pairs={{0,1},{1,0},{2,3},{3,2},{4,5},{5,4},{6,7},{7,6},{8,9},{9,8},{10,11... | collective-permute-start | bytes 221192 | tf_op jit(solution)/shard_map/ppermute | solution.py:288
  18.8 4.3 %collective-permute-start.5 = (bf16[256,128]{1,0:T(8,128)(2,1)S(1)}, bf16[256,128]{1,0:T(8,128)(2,1)S(1)}, u32[]{:S(2)}, u32[]{:S(2)}) collective-permute-start(bf16[256,128]{1,0:T(8,128)(2,1)S(1)} %pad_maximum_fusion), channel_id=1, source_target_pairs={{0,2},{1,3},{2,0},{3,1},{4,6},{5,7},{6,4},{7,5},{8,10},{9,11},{10,... | collective-permute-start | bytes 196616 | tf_op jit(solution)/shard_map/ppermute | solution.py:288
  19.8 0.7 %copy-start = (f32[5]{0:T(128)S(1)}, f32[5]{0:T(128)}, u32[]{:S(2)}) copy-start(f32[5]{0:T(128)} %mix_bias_ref.1) | copy-start | bytes 64
  23.2 4.3 %collective-permute-start.6 = (bf16[256,128]{1,0:T(8,128)(2,1)S(1)}, bf16[256,128]{1,0:T(8,128)(2,1)S(1)}, u32[]{:S(2)}, u32[]{:S(2)}) collective-permute-start(bf16[256,128]{1,0:T(8,128)(2,1)S(1)} %pad_maximum_fusion.1), channel_id=1, source_target_pairs={{0,8},{4,12},{8,0},{12,4},{16,24},{20,28},{24,16},{28,20},{1,9},{5... | collective-permute-start | bytes 196616 | tf_op jit(solution)/shard_map/ppermute | solution.py:288
  27.5 5.6 %collective-permute-start.7 = (bf16[256,128]{1,0:T(8,128)(2,1)S(1)}, bf16[256,128]{1,0:T(8,128)(2,1)S(1)}, u32[]{:S(2)}, u32[]{:S(2)}) collective-permute-start(bf16[256,128]{1,0:T(8,128)(2,1)S(1)} %add.26), channel_id=1, source_target_pairs={{0,16},{4,20},{8,24},{12,28},{16,0},{20,4},{24,8},{28,12},{1,17},{... | collective-permute-start | bytes 196616 | tf_op jit(solution)/shard_map/ppermute | solution.py:288
  33.1 1.3 %collective-permute-start.8 = (bf16[256,128]{1,0:T(8,128)(2,1)S(1)}, bf16[256,128]{1,0:T(8,128)(2,1)S(1)}, u32[]{:S(2)}, u32[]{:S(2)}) collective-permute-start(bf16[256,128]{1,0:T(8,128)(2,1)S(1)} %add.27.mine_ref), channel_id=1, source_target_pairs={{0,4},{4,0},{8,12},{12,8},{16,20},{20,16},{24,28},{28,24},{1,5},{5... | collective-permute-start | bytes 196616 | tf_op jit(solution)/shard_map/ppermute | solution.py:288

commit v5 on v4

--- a/solution.py
+++ b/solution.py
@@ -15,17 +15,34 @@
 HALF = LANES // 2
 
 
+def digit_groups(peers):
+    groups = []
+    low = 1
+    while low < peers:
+        size = min(4, peers // low)
+        groups.append([digit * low for digit in range(size)])
+        low *= size
+    return groups
+
+
 def slot_order(peers):
     order = [0]
-    mask = peers // 2
-    while mask:
-        order = order + [slot | mask for slot in order]
-        mask //= 2
+    for group in digit_groups(peers)[::-1]:
+        order = [digit | slot for digit in group for slot in order]
     return order
 
 
 def contract(left, right, dims):
     return lax.dot_general(left, right, (dims, ((), ())), preferred_element_type=jnp.float32)
+
+
+def guide_of(cot_ref, flat_ref, mix):
+    maps, rows, cols = cot_ref.shape
+    for t in range(maps):
+        flat_ref[t * rows : (t + 1) * rows, :] = cot_ref[t].astype(jnp.float32)
+    lines = [flat_ref[pl.ds(i, maps, stride=rows), :] for i in range(rows)]
+    cot = jnp.concatenate(lines, axis=1).astype(jnp.bfloat16)
+    return contract(cot, mix.astype(jnp.bfloat16), ((0,), (0,))).astype(jnp.bfloat16)
 
 
 def prepare_kernel(
@@ -62,7 +79,7 @@
     for copy in copies:
         copy.start()
     filters = kernel_ref.shape[1]
-    maps, rows, cols = cot_ref.shape
+    maps = cot_ref.shape[0]
     weight_ref[...] = jnp.zeros_like(weight_ref)
     wide_ref[...] = jnp.zeros_like(wide_ref)
     wide_bias_ref[...] = jnp.zeros_like(wide_bias_ref)
@@ -89,18 +106,15 @@
     mix = jnp.concatenate([mix, spare, mix, spare], axis=1)
     mix_ref[0:maps, :] = mix
     mix_ref[maps:16, :] = jnp.zeros((16 - maps, LANES), jnp.float32)
-    for t in range(maps):
-        flat_ref[t * rows : (t + 1) * rows, :] = cot_ref[t].astype(jnp.float32)
-    lines = [flat_ref[pl.ds(i, maps, stride=rows), :] for i in range(rows)]
-    cot = jnp.concatenate(lines, axis=1).astype(jnp.bfloat16)
-    mix = mix.astype(jnp.bfloat16)
-    guide_ref[...] = contract(cot, mix, ((0,), (0,))).astype(jnp.bfloat16)
+    guide_ref[...] = guide_of(cot_ref, flat_ref, mix)
 
 
 def contact_kernel(mix_bias_ref, mix_ref, active_ref, contact_ref):
     mix = mix_ref[...].astype(jnp.bfloat16)
-    mixed = contract(mix, active_ref[...], ((1,), (1,)))
-    maps = contact_ref.shape[0]
+    maps, spots = contact_ref.shape
+    upper = lax.axis_index("row") // (lax.axis_size("row") // 2)
+    mine = pl.ds(pl.multiple_of(upper * spots, spots), spots)
+    mixed = contract(mix, active_ref[mine, :], ((1,), (1,)))
     which = lax.broadcasted_iota(jnp.int32, (8, 1), 0)
     offset = jnp.zeros((8, 1), jnp.float32)
     for t in range(maps):
@@ -111,22 +125,26 @@
 def local_kernel(sizes, *refs):
     peers, rows, cols, bins, filters, half = sizes
     block_refs = refs[:peers]
-    rate_ref, weight_ref, wide_ref, guide_ref, bias_ref = refs[peers : peers + 5]
-    active_ref, send_ref, keep_ref = refs[peers + 5 : peers + 8]
-    bins_ref, pair_ref, conv_ref, center_ref, eights_ref, grad_ref, turned_ref, acc_ref, taps_ref = (
-        refs[peers + 8 :]
-    )
+    rate_ref, weight_ref, wide_ref, own_guide_ref, mix_ref, bias_ref, twin_cot_ref = refs[peers : peers + 7]
+    active_ref, send_ref, keep_ref = refs[peers + 7 : peers + 10]
+    bins_ref, pair_ref, conv_ref, center_ref, guide_ref, eights_ref = refs[peers + 10 : peers + 16]
+    grad_ref, turned_ref, acc_ref, taps_ref, flat_ref = refs[peers + 16 :]
     row_rate = jnp.max(rate_ref[0:8, :])
     col_rate = jnp.max(rate_ref[8:16, :])
     row_index = lax.axis_index("row")
     col_index = lax.axis_index("col")
-    row_start = row_index * rows
+    split = lax.axis_size("row") // 2
+    upper = row_index // split
+    lower_index = lax.rem(row_index, split)
+    row_starts = [lower_index * rows, (lower_index + split) * rows]
     col_start = col_index * cols
     core = lax.rem(row_index, 2)
     count = len(TAPS)
     bf16 = jnp.bfloat16
     f32 = jnp.float32
     extended = rows + 2 * DMAX
+    spots = rows * cols
+    blocks = range(2)
 
     bins_ref[0:PAD, :] = jnp.zeros((PAD, LANES), f32)
     bins_ref[bins + PAD : bins + 2 * PAD, :] = jnp.zeros((PAD, LANES), f32)
@@ -142,96 +160,122 @@
         values.append(bins_ref[pl.ds(col_start + PAD + shift, cols), :].astype(bf16))
         place = col_place + shift
         keeps.append(((place >= 0) & (place < bins)).astype(f32).astype(bf16))
-    for m in range(extended):
-        row = bins_ref[pl.ds(row_start + PAD - DMAX + m, 1), :]
-        row = jnp.broadcast_to(row, (edge, LANES)).astype(bf16)
-        place = row_start - DMAX + m
-        inside = ((place >= 0) & (place < bins)).astype(f32).astype(bf16)
-        for slot in range(5):
-            for j in range(0, cols, edge):
-                piece = row + values[slot][j : j + edge]
-                if slot > 0 and (j == 0 or j + edge == cols):
-                    piece = piece * keeps[slot][j : j + edge]
-                if m < DMAX or m >= rows + DMAX:
-                    piece = piece * inside
-                pair_ref[slot, m * cols + j : m * cols + j + edge, :] = piece
-
-    def shifted_columns(first, last):
-        return jnp.concatenate([pair_ref[first], pair_ref[0], pair_ref[last]], axis=1)
+    for block in blocks:
+        for m in range(extended):
+            place = row_starts[block] - DMAX + m
+            row = bins_ref[pl.ds(place + PAD, 1), :]
+            row = jnp.broadcast_to(row, (edge, LANES)).astype(bf16)
+            inside = ((place >= 0) & (place < bins)).astype(f32).astype(bf16)
+            first = (block * extended + m) * cols
+            for slot in range(5):
+                for j in range(0, cols, edge):
+                    piece = row + values[slot][j : j + edge]
+                    if slot > 0 and (j == 0 or j + edge == cols):
+                        piece = piece * keeps[slot][j : j + edge]
+                    if m < DMAX or m >= rows + DMAX:
+                        piece = piece * inside
+                    pair_ref[slot, first + j : first + j + edge, :] = piece
+
+    own = pl.ds(pl.multiple_of(upper * spots, spots), spots)
+    guide_ref[own, :] = own_guide_ref[...]
+    twin = pl.ds(pl.multiple_of((1 - upper) * spots, spots), spots)
+    guide_ref[twin, :] = guide_of(twin_cot_ref, flat_ref, mix_ref[0 : twin_cot_ref.shape[0], :])
+
+    def shifted_columns(first, last, block=None):
+        at = slice(None) if block is None else slice(block * extended * cols, (block + 1) * extended * cols)
+        return jnp.concatenate([pair_ref[first, at], pair_ref[0, at], pair_ref[last, at]], axis=1)
 
     lane = lax.broadcasted_iota(jnp.int32, (1, LANES), 1)
     is_mirror = lane >= HALF
     center = slice(DMAX * cols, (DMAX + rows) * cols)
-    direct = contract(shifted_columns(1, 2), weight_ref[0], ((1,), (1,)))
-    conv_ref[0] = direct
-    mirror = contract(shifted_columns(3, 4), weight_ref[1], ((1,), (1,)))
-    conv_ref[1] = mirror
-    swapped = jnp.where(is_mirror, direct[center, :LANES], mirror[center, :LANES])
-    center_ref[...] = pltpu.roll(swapped, HALF, 1) + bias_ref[0:1, :]
+    for block in blocks:
+        here = slice(block * extended * cols, (block + 1) * extended * cols)
+        direct = contract(shifted_columns(1, 2, block), weight_ref[0], ((1,), (1,)))
+        conv_ref[0, here, :] = direct
+        mirror = contract(shifted_columns(3, 4, block), weight_ref[1], ((1,), (1,)))
+        conv_ref[1, here, :] = mirror
+        swapped = jnp.where(is_mirror, direct[center, :LANES], mirror[center, :LANES])
+        center_ref[block * spots : (block + 1) * spots, :] = pltpu.roll(swapped, HALF, 1) + bias_ref[0:1, :]
 
     row_keeps = []
     for q in STEPS:
         place = col_place + jnp.where(is_mirror, q * row_rate, q * col_rate)
         row_keeps.append(((place >= 0) & (place < bins)).astype(f32))
     margin = PAD * cols
-    grad_ref[0:margin, :] = jnp.zeros((margin, LANES), bf16)
-    grad_ref[margin + rows * cols : 2 * margin + rows * cols, :] = jnp.zeros((margin, LANES), bf16)
+    padded = 2 * margin + spots
+    for block in blocks:
+        for first in (block * padded, block * padded + margin + spots):
+            grad_ref[first : first + margin, :] = jnp.zeros((margin, LANES), bf16)
     last = cols - 8
 
-    def row_step(i, col_total):
+    def row_step(block, i, col_total):
         def part(mirrored, shift, group):
-            first = pl.multiple_of((DMAX + i + shift) * cols, cols)
+            first = pl.multiple_of((block * extended + DMAX + i + shift) * cols, cols)
             return conv_ref[mirrored, pl.ds(first, cols), group * LANES : (group + 1) * LANES]
 
-        here = pl.ds(pl.multiple_of(i * cols, cols), cols)
+        here = pl.ds(pl.multiple_of(block * spots + i * cols, cols), cols)
         conv = jnp.where(is_mirror, part(1, -col_rate, 0), part(0, -row_rate, 0))
         conv = conv + center_ref[here, :]
         conv = conv + (part(0, row_rate, 1) + part(1, col_rate, 1))
         grad = jnp.where(conv > 0, guide_ref[here, :].astype(f32), 0.0)
         active_ref[here, :] = jnp.maximum(conv, 0.0).astype(bf16)
-        grad_ref[pl.ds(pl.multiple_of(margin + i * cols, cols), cols), :] = grad.astype(bf16)
+        first = pl.multiple_of(block * padded + margin + i * cols, cols)
+        grad_ref[pl.ds(first, cols), :] = grad.astype(bf16)
         inner = grad[8:16]
         for j in range(16, last, 8):
             inner = inner + grad[j : j + 8]
         for q in range(3):
             keep = row_keeps[q]
             eight = inner + grad[0:8] * keep[0:8] + grad[last:cols] * keep[last:cols]
-            eights_ref[q, pl.ds(pl.multiple_of(i * 8, 8), 8), :] = eight
+            eights_ref[q, pl.ds(pl.multiple_of((block * rows + i) * 8, 8), 8), :] = eight
         return col_total + grad
 
-    col_total = lax.fori_loop(0, rows, row_step, jnp.zeros((cols, LANES), f32), unroll=4)
+    col_total = jnp.zeros((cols, LANES), f32)
+    for block in blocks:
+        col_total = lax.fori_loop(0, rows, functools.partial(row_step, block), col_total, unroll=4)
     row_sums = []
     col_sums = []
     for q in range(3):
-        row_sums.append(jnp.sum(eights_ref[q].reshape(rows, 8, LANES), axis=1))
+        row_sums.append(jnp.sum(eights_ref[q].reshape(2 * rows, 8, LANES), axis=1))
         total = col_total
-        for i in [*range(DMAX), *range(rows - DMAX, rows)]:
-            step = STEPS[q]
-            place = row_start + i + jnp.where(is_mirror, step * col_rate, step * row_rate)
-            drop = ((place < 0) | (place >= bins)).astype(f32)
-            total = total - grad_ref[margin + i * cols : margin + (i + 1) * cols, :].astype(f32) * drop
+        for block in blocks:
+            for i in [*range(DMAX), *range(rows - DMAX, rows)]:
+                step = STEPS[q]
+                place = row_starts[block] + i + jnp.where(is_mirror, step * col_rate, step * row_rate)
+                drop = ((place < 0) | (place >= bins)).astype(f32)
+                first = block * padded + margin + i * cols
+                total = total - grad_ref[first : first + cols, :].astype(f32) * drop
         col_sums.append(pltpu.roll(total, HALF, 1))
 
-    chunks = (2 * margin + rows * cols) // LANES
+    chunks = padded // LANES
     first_chunk = margin // LANES
     last_chunk = chunks - first_chunk
     blank = jnp.zeros((LANES, LANES), bf16)
-    for odd in range(2):
-        for chunk in range(chunks):
-            at = slice(chunk * LANES, (chunk + 1) * LANES)
-            if first_chunk <= chunk < last_chunk + odd:
-                begin = chunk * LANES - odd * cols
-                turned_ref[odd, :, at] = grad_ref[begin : begin + LANES, :].T
-            else:
-                turned_ref[odd, :, at] = blank
+    for block in blocks:
+        for odd in range(2):
+            for chunk in range(chunks):
+                at = slice(block * padded + chunk * LANES, block * padded + (chunk + 1) * LANES)
+                if first_chunk <= chunk < last_chunk + odd:
+                    begin = block * padded + chunk * LANES - odd * cols
+                    turned_ref[odd, :, at] = grad_ref[begin : begin + LANES, :].T
+                else:
+                    turned_ref[odd, :, at] = blank
 
     def shifted_rows(first, rate):
         pieces = []
         for q in STEPS:
             start = (DMAX - q * rate) * cols
             odd = lax.rem(lax.rem(q * rate, 2) + 2, 2)
-            start = pl.multiple_of(start + odd * cols, LANES)
-            pieces.append(turned_ref[odd, first : first + filters, pl.ds(start, extended * cols)])
+            start = start + odd * cols
+            wide = [
+                turned_ref[
+                    odd,
+                    first : first + filters,
+                    pl.ds(pl.multiple_of(start + block * padded, LANES), extended * cols),
+                ]
+                for block in blocks
+            ]
+            pieces.append(jnp.concatenate(wide, axis=1))
         return jnp.concatenate(pieces, axis=0)
 
     direct = contract(shifted_rows(0, row_rate), shifted_columns(1, 2), ((1,), (0,)))
@@ -251,10 +295,11 @@
     for group in range(6):
         shift = STEPS[group % 3] * (row_rate if group < 3 else col_rate)
         piece = spread[:, group * LANES : (group + 1) * LANES]
-        where = pl.ds(row_start + PAD + shift, rows)
-        acc_ref[where, :] = acc_ref[where, :] + piece[0:rows]
+        for block in blocks:
+            where = pl.ds(row_starts[block] + PAD + shift, rows)
+            acc_ref[where, :] = acc_ref[where, :] + piece[block * rows : (block + 1) * rows]
         where = pl.ds(col_start + PAD + shift, cols)
-        acc_ref[where, :] = acc_ref[where, :] + piece[rows : rows + cols]
+        acc_ref[where, :] = acc_ref[where, :] + piece[2 * rows : 2 * rows + cols]
 
     total_rows = count * filters
     for target, which in ((keep_ref, core), (send_ref, 1 - core)):
@@ -296,6 +341,7 @@
     peers = lax.axis_size("col")
     row_peers = lax.axis_size("row")
     bins = cols * peers
+    twin_cot = swap(cotangent, "row", row_peers // 2)
     blocks = [swap(embedding, "col", mask) for mask in range(peers - 1, 0, -1)]
     taps = len(TAPS)
     taps_rows = taps * filters
@@ -353,30 +399,43 @@
     active, send, keep = call(
         functools.partial(local_kernel, (peers, rows, cols, bins, filters, half)),
         "contact_head",
-        (shape((spots, LANES), bf16), shape((packed, LANES), bf16), shape((packed, LANES), bf16)),
-        (*blocks, rates, weight, wide, guide, bias),
+        (shape((2 * spots, LANES), bf16), shape((packed, LANES), bf16), shape((packed, LANES), bf16)),
+        (*blocks, rates, weight, wide, guide, mix, bias, twin_cot),
         scratch=(
             pltpu.VMEM((bins + 2 * PAD, LANES), f32),
-            pltpu.VMEM((5, extended, LANES), bf16),
-            pltpu.VMEM((2, extended, 2 * LANES), f32),
-            pltpu.VMEM((spots, LANES), f32),
-            pltpu.VMEM((3, rows * 8, LANES), f32),
-            pltpu.VMEM((padded, LANES), bf16),
-            pltpu.VMEM((2, LANES, padded), bf16),
+            pltpu.VMEM((5, 2 * extended, LANES), bf16),
+            pltpu.VMEM((2, 2 * extended, 2 * LANES), f32),
+            pltpu.VMEM((2 * spots, LANES), f32),
+            pltpu.VMEM((2 * spots, LANES), bf16),
+            pltpu.VMEM((3, 2 * rows * 8, LANES), f32),
+            pltpu.VMEM((2 * padded, LANES), bf16),
+            pltpu.VMEM((2, LANES, 2 * padded), bf16),
             pltpu.VMEM((bins + 2 * PAD, LANES), f32),
             pltpu.VMEM((taps_rows, LANES), f32),
+            pltpu.VMEM((maps * rows, cols), f32),
         ),
-        limit=24,
+        limit=44,
         flops=20_000_000_000,
     )
 
     total = keep + swap(send, "row", 1)
-    mask = 1
-    while mask < peers:
-        kept = peers * (cols // 2) // (2 * mask)
-        got = swap(total[kept:], "col", mask)
-        total = jnp.concatenate([total[:kept] + got[:kept], total[2 * kept :] + got[kept:]], axis=0)
-        mask *= 2
+    bins_left = peers * (cols // 2)
+    for group in digit_groups(peers):
+        each = bins_left // len(group)
+
+        def portion(digit):
+            return jnp.concatenate(
+                [total[digit * each : (digit + 1) * each], total[bins_left:]], axis=0
+            )
+
+        terms = [portion(0)] + [
+            swap(portion(digit), "col", group[digit]) for digit in range(1, len(group))
+        ]
+        terms = [term.astype(f32) for term in terms]
+        while len(terms) > 1:
+            terms = [left + right for left, right in zip(terms[0::2], terms[1::2])]
+        total = terms[0].astype(bf16)
+        bins_left = each
     contact = call(
         contact_kernel,
         "contact",
@@ -387,7 +446,7 @@
     ).reshape(maps, rows, cols)
     total, contact = lax.optimization_barrier((total, contact))
     mask = 2
-    while mask < row_peers:
+    while mask < row_peers // 2:
         total = total + swap(total, "row", mask)
         mask *= 2
     other = swap(total, "row", 1)

time: 35.3 us -> 33.7 us (0.955)
  waiting for transfers between devices: 13.9 us -> 7.97 us
  Pallas kernels: 6.83 us -> 10.5 us
  starting transfers between devices: 12.2 us -> 13 us
    ppermute x9 -> x10, waiting for transfers between devices: 13.9 us -> 7.97 us  [swap(): return lax.ppermute(value, axis, [(i, i ^ mask) for i in range(peers)])]
    pallas_call x4, Pallas kernels: 6.83 us -> 10.5 us  [call(): pl.pallas_call(body, out_shape=out_shape, in_specs=specs or [vmem] * len(...]
    ppermute x9 -> x10, starting transfers between devices: 12.2 us -> 13 us  [swap(): return lax.ppermute(value, axis, [(i, i ^ mask) for i in range(peers)])]
  transfers between devices with their start and end apart: 9 -> 10, of which waited for: 8 -> 6; matrix products, arithmetic and copies ran while one was open for 2% -> 2% of each run, Pallas kernels for 6% -> 7%
where the time goes in v5:
time: 33.7 us; the launch traced here: 33.6 us
  starting transfers between devices  13 us (39%)
  Pallas kernels  10.5 us (31%)
  waiting for transfers between devices  7.97 us (24%)
  local copies, waits for them, and re-layouts  1.23 us (4%)
  between operations  0.73 us (2%)
    ppermute x10, starting transfers between devices, swap(): return lax.ppermute(value, axis, [(i, i ^ mask) for i in range(peers)])  13 us
    pallas_call x4, Pallas kernels, call(): pl.pallas_call(body, out_shape=out_shape, in_specs=specs or [vmem] * len(...  10.5 us
    ppermute x10, waiting for transfers between devices, swap(): return lax.ppermute(value, axis, [(i, i ^ mask) for i in range(peers)])  7.97 us
    reshape x1, local copies, waits for them, and re-layouts, per_device(): contact = call(contact_kernel, 'contact', shape((maps, spots), f32), (mix...  0.73 us
  transfers between devices with their start and end apart: 10, of which 6 were waited for; matrix products, arithmetic and copies ran while one was open for 2% of the time, Pallas kernels for 7%

profile of v5, /device:TPU:0, one launch (start us, length us, event | category | flops | bytes accessed | tf_op | source)
XLA Modules:
  0.0 33.6 jit_solution(6917175120687817113)
XLA Ops:
  0.6 3.0 %collective-permute-start = (bf16[64,128]{1,0:T(8,128)(2,1)}, bf16[64,128]{1,0:T(8,128)(2,1)S(1)}, u32[]{:S(2)}, u32[]{:S(2)}) collective-permute-start(bf16[64,128]{1,0:T(8,128)(2,1)} %embedding_hbm.1), channel_id=1, source_target_pairs={{0,1},{1,0},{2,3},{3,2},{4,5},{5,4},{6,7},{7,6},{8,9},{9,8},{10,11... | collective-permute-start | bytes 49160 | tf_op jit(solution)/shard_map/ppermute | solution.py:333
  3.7 1.5 %collective-permute-start.2 = (bf16[64,128]{1,0:T(8,128)(2,1)}, bf16[64,128]{1,0:T(8,128)(2,1)S(1)}, u32[]{:S(2)}, u32[]{:S(2)}) collective-permute-start(bf16[64,128]{1,0:T(8,128)(2,1)} %embedding_hbm.1), channel_id=1, source_target_pairs={{0,3},{1,2},{2,1},{3,0},{4,7},{5,6},{6,5},{7,4},{8,11},{9,10},{10,... | collective-permute-start | bytes 49160 | tf_op jit(solution)/shard_map/ppermute | solution.py:333
  5.2 0.0 collective-permute-start.1
  5.2 3.0 %collective-permute-start.3 = (bf16[5,32,64]{2,1,0:T(8,128)(2,1)}, bf16[5,32,64]{2,1,0:T(8,128)(2,1)S(1)}, u32[]{:S(2)}, u32[]{:S(2)}) collective-permute-start(bf16[5,32,64]{2,1,0:T(8,128)(2,1)} %cot_hbm.1), channel_id=1, source_target_pairs={{0,16},{4,20},{8,24},{12,28},{16,0},{20,4},{24,8},{28,12},{1,17},{... | collective-permute-start | bytes 61448 | tf_op jit(solution)/shard_map/ppermute | solution.py:333
  8.3 1.5 %prepare.1 = (bf16[64,128]{1,0:T(8,128)(2,1)S(1)}, s32[16,128]{1,0:T(8,128)S(1)}, bf16[2,256,384]{2,1,0:T(8,128)(2,1)S(1)}, bf16[384,768]{1,0:T(8,128)(2,1)S(1)}...) custom-call(bf16[64,128]{1,0:T(8,128)(2,1)} %embedding_hbm.1, s32[2]{0:T(128)} %dilation_hbm.1, ...), custom_call_target="tpu_custom_call" | custom-call | flops 4000000000 | bytes 1000 | tf_op jit(solution)/shard_map/prepare/pallas_call | solution.py:355
  9.8 0.0 collective-permute-done.refs_1_
  9.8 0.0 collective-permute-done.2.refs_3_
  9.8 0.0 collective-permute-done.1.refs_2_
  9.8 0.7 %collective-permute-done.3.refs_10_ = bf16[5,32,64]{2,1,0:T(8,128)(2,1)S(1)} collective-permute-done((bf16[5,32,64]{2,1,0:T(8,128)(2,1)}, bf16[5,32,64]{2,1,0:T(8,128)(2,1)S(1)}, u32[]{:S(2)}, u32[]{:S(2)}) %collective-permute-start.3) | collective-permute-done | bytes 20512 | tf_op jit(solution)/shard_map/ppermute | solution.py:333
  10.4 7.5 %contact_head.1 = (bf16[4096,128]{1,0:T(8,128)(2,1)S(1)}, bf16[352,128]{1,0:T(8,128)(2,1)S(1)}, bf16[352,128]{1,0:T(8,128)(2,1)S(1)}) custom-call(bf16[64,128]{1,0:T(8,128)(2,1)S(1)} %get-tuple-element.17.refs_0_, bf16[64,128]{1,0:T(8,128)(2,1)S(1)} %collective-permute-done.refs_1_, bf16[64,128]{1,0:T(8,128)(2,1)S(1)} %collective-permute-done.1.refs_2_, ...), custom_call_target="tpu_custom_call" | custom-call | flops 20000000000 | bytes 1000 | tf_op jit(solution)/shard_map/contact_head/pallas_call | solution.py:355
  18.0 0.1 collective-permute-start.4
  18.0 1.3 %collective-permute-done.4 = bf16[352,128]{1,0:T(8,128)(2,1)S(1)} collective-permute-done((bf16[352,128]{1,0:T(8,128)(2,1)S(1)}, bf16[352,128]{1,0:T(8,128)(2,1)S(1)}, u32[]{:S(2)}, u32[]{:S(2)}) %collective-permute-start.4) | collective-permute-done | bytes 90144 | tf_op jit(solution)/shard_map/ppermute | solution.py:333
  19.4 2.8 %collective-permute-start.7 = (bf16[256,128]{1,0:T(8,128)(2,1)S(1)}, bf16[256,128]{1,0:T(8,128)(2,1)S(1)}, u32[]{:S(2)}, u32[]{:S(2)}) collective-permute-start(bf16[256,128]{1,0:T(8,128)(2,1)S(1)} %concatenate.16), channel_id=1, source_target_pairs={{0,3},{1,2},{2,1},{3,0},{4,7},{5,6},{6,5},{7,4},{8,11},{9,10},{10,... | collective-permute-start | bytes 196616 | tf_op jit(solution)/shard_map/ppermute | solution.py:333
  22.2 0.6 %collective-permute-start.5 = (bf16[256,128]{1,0:T(8,128)(2,1)S(1)}, bf16[256,128]{1,0:T(8,128)(2,1)S(1)}, u32[]{:S(2)}, u32[]{:S(2)}) collective-permute-start(bf16[256,128]{1,0:T(8,128)(2,1)S(1)} %get-tuple-element.34), channel_id=1, source_target_pairs={{0,1},{1,0},{2,3},{3,2},{4,5},{5,4},{6,7},{7,6},{8,9},{9,8},{10,11... | collective-permute-start | bytes 196616 | tf_op jit(solution)/shard_map/ppermute | solution.py:333
  22.8 0.0 copy-start
  22.8 0.2 collective-permute-start.6
  23.0 0.5 %copy-done = f32[5]{0:T(128)S(1)} copy-done((f32[5]{0:T(128)S(1)}, f32[5]{0:T(128)}, u32[]{:S(2)}) %copy-start) | copy-done | bytes 44
  23.5 0.8 %contact.1 = f32[5,2048]{1,0:T(8,128)S(1)} custom-call(f32[5]{0:T(128)S(1)} %copy-done, f32[16,128]{1,0:T(8,128)S(1)} %get-tuple-element.22.refs_8_.mix_ref, bf16[4096,128]{1,0:T(8,128)(2,1)S(1)} %get-tuple-element.26.active_ref), custom_call_target="tpu_custom_call" | custom-call | flops 1000000000 | bytes 1000 | tf_op jit(solution)/shard_map/contact/pallas_call | solution.py:355
  24.3 0.7 %reshape.16 = f32[5,32,64]{2,1,0:T(8,128)} reshape(f32[5,2048]{1,0:T(8,128)S(1)} %contact.1) | data formatting | bytes 81920 | tf_op jit(solution)/shard_map/reshape | solution.py:446
  25.0 0.0 collective-permute-done.7
  25.0 1.5 %collective-permute-done.5 = bf16[256,128]{1,0:T(8,128)(2,1)S(1)} collective-permute-done((bf16[256,128]{1,0:T(8,128)(2,1)S(1)}, bf16[256,128]{1,0:T(8,128)(2,1)S(1)}, u32[]{:S(2)}, u32[]{:S(2)}) %collective-permute-start.5) | collective-permute-done | bytes 65568 | tf_op jit(solution)/shard_map/ppermute | solution.py:333
  26.6 0.6 %collective-permute-done.6 = bf16[256,128]{1,0:T(8,128)(2,1)S(1)} collective-permute-done((bf16[256,128]{1,0:T(8,128)(2,1)S(1)}, bf16[256,128]{1,0:T(8,128)(2,1)S(1)}, u32[]{:S(2)}, u32[]{:S(2)}) %collective-permute-start.6) | collective-permute-done | bytes 65568 | tf_op jit(solution)/shard_map/ppermute | solution.py:333
  27.2 1.6 %collective-permute-start.8 = (bf16[256,128]{1,0:T(8,128)(2,1)S(1)}, bf16[256,128]{1,0:T(8,128)(2,1)S(1)}, u32[]{:S(2)}, u32[]{:S(2)}) collective-permute-start(bf16[256,128]{1,0:T(8,128)(2,1)S(1)} %add_convert_fusion), channel_id=1, source_target_pairs={{0,8},{4,12},{8,0},{12,4},{16,24},{20,28},{24,16},{28,20},{1,9},{5... | collective-permute-start | bytes 196616 | tf_op jit(solution)/shard_map/ppermute | solution.py:333
  28.8 2.7 %collective-permute-done.8 = bf16[256,128]{1,0:T(8,128)(2,1)S(1)} collective-permute-done((bf16[256,128]{1,0:T(8,128)(2,1)S(1)}, bf16[256,128]{1,0:T(8,128)(2,1)S(1)}, u32[]{:S(2)}, u32[]{:S(2)}) %collective-permute-start.8) | collective-permute-done | bytes 65568 | tf_op jit(solution)/shard_map/ppermute | solution.py:333
  31.5 0.1 collective-permute-start.9
  31.6 1.2 %collective-permute-done.9.other_ref = bf16[256,128]{1,0:T(8,128)(2,1)S(1)} collective-permute-done((bf16[256,128]{1,0:T(8,128)(2,1)S(1)}, bf16[256,128]{1,0:T(8,128)(2,1)S(1)}, u32[]{:S(2)}, u32[]{:S(2)}) %collective-permute-start.9) | collective-permute-done | bytes 65568 | tf_op jit(solution)/shard_map/ppermute | solution.py:333
  32.8 0.7 %join.1 = (f32[64,128]{1,0:T(8,128)}, f32[432,128]{1,0:T(8,128)}) custom-call(bf16[256,128]{1,0:T(8,128)(2,1)S(1)} %add.19.mine_ref, bf16[256,128]{1,0:T(8,128)(2,1)S(1)} %collective-permute-done.9.other_ref), custom_call_target="tpu_custom_call" | custom-call | flops 1000 | bytes 1000 | tf_op jit(solution)/shard_map/join/pallas_call | solution.py:355
  (7 shorter events, 0.1 us)
Async XLA Ops:
  0.6 9.1 %collective-permute-start = (bf16[64,128]{1,0:T(8,128)(2,1)}, bf16[64,128]{1,0:T(8,128)(2,1)S(1)}, u32[]{:S(2)}, u32[]{:S(2)}) collective-permute-start(bf16[64,128]{1,0:T(8,128)(2,1)} %embedding_hbm.1), channel_id=1, source_target_pairs={{0,1},{1,0},{2,3},{3,2},{4,5},{5,4},{6,7},{7,6},{8,9},{9,8},{10,11... | collective-permute-start | bytes 49160 | tf_op jit(solution)/shard_map/ppermute | solution.py:333
  3.7 6.1 %collective-permute-start.2 = (bf16[64,128]{1,0:T(8,128)(2,1)}, bf16[64,128]{1,0:T(8,128)(2,1)S(1)}, u32[]{:S(2)}, u32[]{:S(2)}) collective-permute-start(bf16[64,128]{1,0:T(8,128)(2,1)} %embedding_hbm.1), channel_id=1, source_target_pairs={{0,3},{1,2},{2,1},{3,0},{4,7},{5,6},{6,5},{7,4},{8,11},{9,10},{10,... | collective-permute-start | bytes 49160 | tf_op jit(solution)/shard_map/ppermute | solution.py:333
  5.2 4.6 %collective-permute-start.1 = (bf16[64,128]{1,0:T(8,128)(2,1)}, bf16[64,128]{1,0:T(8,128)(2,1)S(1)}, u32[]{:S(2)}, u32[]{:S(2)}) collective-permute-start(bf16[64,128]{1,0:T(8,128)(2,1)} %embedding_hbm.1), channel_id=1, source_target_pairs={{0,2},{1,3},{2,0},{3,1},{4,6},{5,7},{6,4},{7,5},{8,10},{9,11},{10,... | collective-permute-start | bytes 49160 | tf_op jit(solution)/shard_map/ppermute | solution.py:333
  5.2 5.2 %collective-permute-start.3 = (bf16[5,32,64]{2,1,0:T(8,128)(2,1)}, bf16[5,32,64]{2,1,0:T(8,128)(2,1)S(1)}, u32[]{:S(2)}, u32[]{:S(2)}) collective-permute-start(bf16[5,32,64]{2,1,0:T(8,128)(2,1)} %cot_hbm.1), channel_id=1, source_target_pairs={{0,16},{4,20},{8,24},{12,28},{16,0},{20,4},{24,8},{28,12},{1,17},{... | collective-permute-start | bytes 61448 | tf_op jit(solution)/shard_map/ppermute | solution.py:333
  18.0 1.4 %collective-permute-start.4 = (bf16[352,128]{1,0:T(8,128)(2,1)S(1)}, bf16[352,128]{1,0:T(8,128)(2,1)S(1)}, u32[]{:S(2)}, u32[]{:S(2)}) collective-permute-start(bf16[352,128]{1,0:T(8,128)(2,1)S(1)} %get-tuple-element.25), channel_id=1, source_target_pairs={{0,4},{4,0},{8,12},{12,8},{16,20},{20,16},{24,28},{28,24},{1,5},{5... | collective-permute-start | bytes 270344 | tf_op jit(solution)/shard_map/ppermute | solution.py:333
  19.4 5.6 %collective-permute-start.7 = (bf16[256,128]{1,0:T(8,128)(2,1)S(1)}, bf16[256,128]{1,0:T(8,128)(2,1)S(1)}, u32[]{:S(2)}, u32[]{:S(2)}) collective-permute-start(bf16[256,128]{1,0:T(8,128)(2,1)S(1)} %concatenate.16), channel_id=1, source_target_pairs={{0,3},{1,2},{2,1},{3,0},{4,7},{5,6},{6,5},{7,4},{8,11},{9,10},{10,... | collective-permute-start | bytes 196616 | tf_op jit(solution)/shard_map/ppermute | solution.py:333
  22.2 4.3 %collective-permute-start.5 = (bf16[256,128]{1,0:T(8,128)(2,1)S(1)}, bf16[256,128]{1,0:T(8,128)(2,1)S(1)}, u32[]{:S(2)}, u32[]{:S(2)}) collective-permute-start(bf16[256,128]{1,0:T(8,128)(2,1)S(1)} %get-tuple-element.34), channel_id=1, source_target_pairs={{0,1},{1,0},{2,3},{3,2},{4,5},{5,4},{6,7},{7,6},{8,9},{9,8},{10,11... | collective-permute-start | bytes 196616 | tf_op jit(solution)/shard_map/ppermute | solution.py:333
  22.8 0.7 %copy-start = (f32[5]{0:T(128)S(1)}, f32[5]{0:T(128)}, u32[]{:S(2)}) copy-start(f32[5]{0:T(128)} %mix_bias_ref.1) | copy-start | bytes 64
  22.8 4.3 %collective-permute-start.6 = (bf16[256,128]{1,0:T(8,128)(2,1)S(1)}, bf16[256,128]{1,0:T(8,128)(2,1)S(1)}, u32[]{:S(2)}, u32[]{:S(2)}) collective-permute-start(bf16[256,128]{1,0:T(8,128)(2,1)S(1)} %get-tuple-element.35), channel_id=1, source_target_pairs={{0,2},{1,3},{2,0},{3,1},{4,6},{5,7},{6,4},{7,5},{8,10},{9,11},{10,... | collective-permute-start | bytes 196616 | tf_op jit(solution)/shard_map/ppermute | solution.py:333
  27.2 4.3 %collective-permute-start.8 = (bf16[256,128]{1,0:T(8,128)(2,1)S(1)}, bf16[256,128]{1,0:T(8,128)(2,1)S(1)}, u32[]{:S(2)}, u32[]{:S(2)}) collective-permute-start(bf16[256,128]{1,0:T(8,128)(2,1)S(1)} %add_convert_fusion), channel_id=1, source_target_pairs={{0,8},{4,12},{8,0},{12,4},{16,24},{20,28},{24,16},{28,20},{1,9},{5... | collective-permute-start | bytes 196616 | tf_op jit(solution)/shard_map/ppermute | solution.py:333
  31.5 1.3 %collective-permute-start.9 = (bf16[256,128]{1,0:T(8,128)(2,1)S(1)}, bf16[256,128]{1,0:T(8,128)(2,1)S(1)}, u32[]{:S(2)}, u32[]{:S(2)}) collective-permute-start(bf16[256,128]{1,0:T(8,128)(2,1)S(1)} %add.19.mine_ref), channel_id=1, source_target_pairs={{0,4},{4,0},{8,12},{12,8},{16,20},{20,16},{24,28},{28,24},{1,5},{5... | collective-permute-start | bytes 196616 | tf_op jit(solution)/shard_map/ppermute | solution.py:333

commit v6 on v5

--- a/solution.py
+++ b/solution.py
@@ -122,21 +122,71 @@
     contact_ref[...] = (mixed[0:8] + offset)[0:maps]
 
 
+def row_blocks(rows):
+    split = lax.axis_size("row") // 2
+    lower = lax.rem(lax.axis_index("row"), split)
+    return [lower * rows, (lower + split) * rows]
+
+
+def pairs_kernel(sizes, *refs):
+    peers, rows, cols, bins = sizes
+    block_refs = refs[:peers]
+    rate_ref, pair_ref, bins_ref, cols_ref, rows_ref = refs[peers:]
+    bf16 = jnp.bfloat16
+    f32 = jnp.float32
+    row_rate = jnp.max(rate_ref[0:8, :])
+    col_rate = jnp.max(rate_ref[8:16, :])
+    row_starts = row_blocks(rows)
+    col_index = lax.axis_index("col")
+    col_start = col_index * cols
+    extended = rows + 2 * DMAX
+    edge = 16
+    bins_ref[0:PAD, :] = jnp.zeros((PAD, LANES), f32)
+    bins_ref[bins + PAD : bins + 2 * PAD, :] = jnp.zeros((PAD, LANES), f32)
+    for step in range(peers):
+        place = pl.multiple_of(jnp.bitwise_xor(col_index, step) * cols + PAD, 8)
+        bins_ref[pl.ds(place, cols), :] = 0.5 * block_refs[step][...].astype(f32)
+    col_place = lax.broadcasted_iota(jnp.int32, (cols, LANES), 0) + col_start
+    for slot, shift in enumerate((0, -col_rate, col_rate, -row_rate, row_rate)):
+        place = col_place + shift
+        keep = ((place >= 0) & (place < bins)).astype(f32)
+        values = bins_ref[pl.ds(col_start + PAD + shift, cols), :]
+        cols_ref[slot] = values.astype(bf16)
+        cols_ref[5 + slot] = keep.astype(bf16)
+    for block in range(2):
+        for m in range(extended):
+            row = bins_ref[pl.ds(row_starts[block] - DMAX + m + PAD, 1), :]
+            rows_ref[block * extended + m] = jnp.broadcast_to(row, (edge, LANES)).astype(bf16)
+    for slot in range(5):
+        values = [cols_ref[slot, j : j + edge, :] for j in range(0, cols, edge)]
+        keeps = {j: cols_ref[5 + slot, j : j + edge, :] for j in (0, cols - edge)}
+        for block in range(2):
+            for m in range(extended):
+                place = row_starts[block] - DMAX + m
+                row = rows_ref[block * extended + m]
+                inside = ((place >= 0) & (place < bins)).astype(f32).astype(bf16)
+                first = (block * extended + m) * cols
+                for at, j in enumerate(range(0, cols, edge)):
+                    piece = row + values[at]
+                    if slot > 0 and j in keeps:
+                        piece = piece * keeps[j]
+                    if m < DMAX or m >= rows + DMAX:
+                        piece = piece * inside
+                    pair_ref[slot, first + j : first + j + edge, :] = piece
+
+
 def local_kernel(sizes, *refs):
     peers, rows, cols, bins, filters, half = sizes
-    block_refs = refs[:peers]
-    rate_ref, weight_ref, wide_ref, own_guide_ref, mix_ref, bias_ref, twin_cot_ref = refs[peers : peers + 7]
-    active_ref, send_ref, keep_ref = refs[peers + 7 : peers + 10]
-    bins_ref, pair_ref, conv_ref, center_ref, guide_ref, eights_ref = refs[peers + 10 : peers + 16]
-    grad_ref, turned_ref, acc_ref, taps_ref, flat_ref = refs[peers + 16 :]
+    pair_ref, rate_ref, weight_ref, wide_ref, own_guide_ref, mix_ref, bias_ref, twin_cot_ref = refs[:8]
+    active_ref, send_ref, keep_ref = refs[8:11]
+    conv_ref, center_ref, guide_ref, eights_ref = refs[11:15]
+    grad_ref, turned_ref, acc_ref, taps_ref, flat_ref, sums_ref = refs[15:]
     row_rate = jnp.max(rate_ref[0:8, :])
     col_rate = jnp.max(rate_ref[8:16, :])
     row_index = lax.axis_index("row")
     col_index = lax.axis_index("col")
-    split = lax.axis_size("row") // 2
-    upper = row_index // split
-    lower_index = lax.rem(row_index, split)
-    row_starts = [lower_index * rows, (lower_index + split) * rows]
+    row_starts = row_blocks(rows)
+    upper = row_index // (lax.axis_size("row") // 2)
     col_start = col_index * cols
     core = lax.rem(row_index, 2)
     count = len(TAPS)
@@ -145,50 +195,17 @@
     extended = rows + 2 * DMAX
     spots = rows * cols
     blocks = range(2)
-
-    bins_ref[0:PAD, :] = jnp.zeros((PAD, LANES), f32)
-    bins_ref[bins + PAD : bins + 2 * PAD, :] = jnp.zeros((PAD, LANES), f32)
-    for step in range(peers):
-        place = pl.multiple_of(jnp.bitwise_xor(col_index, step) * cols + PAD, 8)
-        bins_ref[pl.ds(place, cols), :] = 0.5 * block_refs[step][...].astype(f32)
-
     col_place = lax.broadcasted_iota(jnp.int32, (cols, LANES), 0) + col_start
-    edge = 16
-    values = []
-    keeps = []
-    for shift in (0, -col_rate, col_rate, -row_rate, row_rate):
-        values.append(bins_ref[pl.ds(col_start + PAD + shift, cols), :].astype(bf16))
-        place = col_place + shift
-        keeps.append(((place >= 0) & (place < bins)).astype(f32).astype(bf16))
-    for block in blocks:
-        for m in range(extended):
-            place = row_starts[block] - DMAX + m
-            row = bins_ref[pl.ds(place + PAD, 1), :]
-            row = jnp.broadcast_to(row, (edge, LANES)).astype(bf16)
-            inside = ((place >= 0) & (place < bins)).astype(f32).astype(bf16)
-            first = (block * extended + m) * cols
-            for slot in range(5):
-                for j in range(0, cols, edge):
-                    piece = row + values[slot][j : j + edge]
-                    if slot > 0 and (j == 0 or j + edge == cols):
-                        piece = piece * keeps[slot][j : j + edge]
-                    if m < DMAX or m >= rows + DMAX:
-                        piece = piece * inside
-                    pair_ref[slot, first + j : first + j + edge, :] = piece
-
-    own = pl.ds(pl.multiple_of(upper * spots, spots), spots)
-    guide_ref[own, :] = own_guide_ref[...]
-    twin = pl.ds(pl.multiple_of((1 - upper) * spots, spots), spots)
-    guide_ref[twin, :] = guide_of(twin_cot_ref, flat_ref, mix_ref[0 : twin_cot_ref.shape[0], :])
-
-    def shifted_columns(first, last, block=None):
-        at = slice(None) if block is None else slice(block * extended * cols, (block + 1) * extended * cols)
+
+    def shifted_columns(first, last, block):
+        at = slice(block * extended * cols, (block + 1) * extended * cols)
         return jnp.concatenate([pair_ref[first, at], pair_ref[0, at], pair_ref[last, at]], axis=1)
 
     lane = lax.broadcasted_iota(jnp.int32, (1, LANES), 1)
     is_mirror = lane >= HALF
     center = slice(DMAX * cols, (DMAX + rows) * cols)
-    for block in blocks:
+
+    def forward(block):
         here = slice(block * extended * cols, (block + 1) * extended * cols)
         direct = contract(shifted_columns(1, 2, block), weight_ref[0], ((1,), (1,)))
         conv_ref[0, here, :] = direct
@@ -203,9 +220,6 @@
         row_keeps.append(((place >= 0) & (place < bins)).astype(f32))
     margin = PAD * cols
     padded = 2 * margin + spots
-    for block in blocks:
-        for first in (block * padded, block * padded + margin + spots):
-            grad_ref[first : first + margin, :] = jnp.zeros((margin, LANES), bf16)
     last = cols - 8
 
     def row_step(block, i, col_total):
@@ -230,13 +244,60 @@
             eights_ref[q, pl.ds(pl.multiple_of((block * rows + i) * 8, 8), 8), :] = eight
         return col_total + grad
 
-    col_total = jnp.zeros((cols, LANES), f32)
+    def row_pass(block, col_total):
+        return lax.fori_loop(0, rows, functools.partial(row_step, block), col_total, unroll=4)
+
+    chunks = padded // LANES
+    first_chunk = margin // LANES
+    last_chunk = chunks - first_chunk
+    blank = jnp.zeros((LANES, LANES), bf16)
+
+    def clear_margins(block):
+        for first in (block * padded, block * padded + margin + spots):
+            grad_ref[first : first + margin, :] = jnp.zeros((margin, LANES), bf16)
+        for odd in range(2):
+            for chunk in range(chunks):
+                if not first_chunk <= chunk < last_chunk + odd:
+                    at = slice(block * padded + chunk * LANES, block * padded + (chunk + 1) * LANES)
+                    turned_ref[odd, :, at] = blank
+
+    def turn(block):
+        for odd in range(2):
+            for chunk in range(first_chunk, last_chunk + odd):
+                at = slice(block * padded + chunk * LANES, block * padded + (chunk + 1) * LANES)
+                begin = block * padded + chunk * LANES - odd * cols
+                turned_ref[odd, :, at] = grad_ref[begin : begin + LANES, :].T
+
+    def shifted_rows(first, rate, block):
+        pieces = []
+        for q in STEPS:
+            start = (DMAX - q * rate) * cols
+            odd = lax.rem(lax.rem(q * rate, 2) + 2, 2)
+            start = pl.multiple_of(start + odd * cols + block * padded, LANES)
+            pieces.append(turned_ref[odd, first : first + filters, pl.ds(start, extended * cols)])
+        return jnp.concatenate(pieces, axis=0)
+
+    def backward(block):
+        direct = contract(shifted_rows(0, row_rate, block), shifted_columns(1, 2, block), ((1,), (0,)))
+        mirror = contract(shifted_rows(HALF, col_rate, block), shifted_columns(3, 4, block), ((1,), (0,)))
+        return direct, mirror
+
+    forward(0)
+    own = pl.ds(pl.multiple_of(upper * spots, spots), spots)
+    guide_ref[own, :] = own_guide_ref[...]
+    twin = pl.ds(pl.multiple_of((1 - upper) * spots, spots), spots)
+    guide_ref[twin, :] = guide_of(twin_cot_ref, flat_ref, mix_ref[0 : twin_cot_ref.shape[0], :])
     for block in blocks:
-        col_total = lax.fori_loop(0, rows, functools.partial(row_step, block), col_total, unroll=4)
-    row_sums = []
-    col_sums = []
+        clear_margins(block)
+    col_total = row_pass(0, jnp.zeros((cols, LANES), f32))
+    forward(1)
+    turn(0)
+    col_total = row_pass(1, col_total)
+    turn(1)
+
     for q in range(3):
-        row_sums.append(jnp.sum(eights_ref[q].reshape(2 * rows, 8, LANES), axis=1))
+        totals = jnp.sum(eights_ref[q].reshape(2 * rows, 8, LANES), axis=1)
+        sums_ref[0 : 2 * rows, q * LANES : (q + 1) * LANES] = totals.astype(bf16)
         total = col_total
         for block in blocks:
             for i in [*range(DMAX), *range(rows - DMAX, rows)]:
@@ -245,52 +306,9 @@
                 drop = ((place < 0) | (place >= bins)).astype(f32)
                 first = block * padded + margin + i * cols
                 total = total - grad_ref[first : first + cols, :].astype(f32) * drop
-        col_sums.append(pltpu.roll(total, HALF, 1))
-
-    chunks = padded // LANES
-    first_chunk = margin // LANES
-    last_chunk = chunks - first_chunk
-    blank = jnp.zeros((LANES, LANES), bf16)
-    for block in blocks:
-        for odd in range(2):
-            for chunk in range(chunks):
-                at = slice(block * padded + chunk * LANES, block * padded + (chunk + 1) * LANES)
-                if first_chunk <= chunk < last_chunk + odd:
-                    begin = block * padded + chunk * LANES - odd * cols
-                    turned_ref[odd, :, at] = grad_ref[begin : begin + LANES, :].T
-                else:
-                    turned_ref[odd, :, at] = blank
-
-    def shifted_rows(first, rate):
-        pieces = []
-        for q in STEPS:
-            start = (DMAX - q * rate) * cols
-            odd = lax.rem(lax.rem(q * rate, 2) + 2, 2)
-            start = start + odd * cols
-            wide = [
-                turned_ref[
-                    odd,
-                    first : first + filters,
-                    pl.ds(pl.multiple_of(start + block * padded, LANES), extended * cols),
-                ]
-                for block in blocks
-            ]
-            pieces.append(jnp.concatenate(wide, axis=1))
-        return jnp.concatenate(pieces, axis=0)
-
-    direct = contract(shifted_rows(0, row_rate), shifted_columns(1, 2), ((1,), (0,)))
-    mirror = contract(shifted_rows(HALF, col_rate), shifted_columns(3, 4), ((1,), (0,)))
-    for at, (a, b) in enumerate(TAPS):
-        a, b = a + 1, b + 1
-        taps_ref[at * filters : (at + 1) * filters, :] = (
-            direct[a * filters : (a + 1) * filters, b * LANES : (b + 1) * LANES]
-            + mirror[b * filters : (b + 1) * filters, a * LANES : (a + 1) * LANES]
-        )
-
-    sums = jnp.concatenate(
-        [jnp.concatenate(row_sums, axis=1), jnp.concatenate(col_sums, axis=1)], axis=0
-    ).astype(bf16)
-    spread = contract(sums, wide_ref[...], ((1,), (0,)))
+        total = pltpu.roll(total, HALF, 1)
+        sums_ref[2 * rows : 2 * rows + cols, q * LANES : (q + 1) * LANES] = total.astype(bf16)
+    spread = contract(sums_ref[...], wide_ref[...], ((1,), (0,)))
     acc_ref[...] = jnp.zeros_like(acc_ref)
     for group in range(6):
         shift = STEPS[group % 3] * (row_rate if group < 3 else col_rate)
@@ -300,16 +318,27 @@
             acc_ref[where, :] = acc_ref[where, :] + piece[block * rows : (block + 1) * rows]
         where = pl.ds(col_start + PAD + shift, cols)
         acc_ref[where, :] = acc_ref[where, :] + piece[2 * rows : 2 * rows + cols]
-
-    total_rows = count * filters
+    part = cols // 2
     for target, which in ((keep_ref, core), (send_ref, 1 - core)):
-        part = cols // 2
         for slot, step in enumerate(slot_order(peers)):
-            block = jnp.bitwise_xor(col_index, step)
-            first = pl.multiple_of(block * cols + which * part + PAD, 8)
+            place = jnp.bitwise_xor(col_index, step)
+            first = pl.multiple_of(place * cols + which * part + PAD, 8)
             target[slot * part : (slot + 1) * part, :] = (
                 0.5 * acc_ref[pl.ds(first, part), :]
             ).astype(bf16)
+
+    lower = backward(0)
+    higher = backward(1)
+    direct = lower[0] + higher[0]
+    mirror = lower[1] + higher[1]
+    for at, (a, b) in enumerate(TAPS):
+        a, b = a + 1, b + 1
+        taps_ref[at * filters : (at + 1) * filters, :] = (
+            direct[a * filters : (a + 1) * filters, b * LANES : (b + 1) * LANES]
+            + mirror[b * filters : (b + 1) * filters, a * LANES : (a + 1) * LANES]
+        )
+    total_rows = count * filters
+    for target, which in ((keep_ref, core), (send_ref, 1 - core)):
         first = pl.multiple_of(which * (total_rows - half), 16)
         target[peers * part : peers * part + half, :] = taps_ref[pl.ds(first, half), :].astype(bf16)
 
@@ -396,14 +425,25 @@
     blocks = [own] + blocks[::-1]
     extended = (rows + 2 * DMAX) * cols
     padded = spots + 2 * PAD * cols
+    pairs = call(
+        functools.partial(pairs_kernel, (peers, rows, cols, bins)),
+        "pairs",
+        shape((5, 2 * extended, LANES), bf16),
+        (*blocks, rates),
+        scratch=(
+            pltpu.VMEM((bins + 2 * PAD, LANES), f32),
+            pltpu.VMEM((10, cols, LANES), bf16),
+            pltpu.VMEM((2 * (rows + 2 * DMAX), 16, LANES), bf16),
+        ),
+        limit=12,
+        flops=3_000_000_000,
+    )
     active, send, keep = call(
         functools.partial(local_kernel, (peers, rows, cols, bins, filters, half)),
         "contact_head",
         (shape((2 * spots, LANES), bf16), shape((packed, LANES), bf16), shape((packed, LANES), bf16)),
-        (*blocks, rates, weight, wide, guide, mix, bias, twin_cot),
+        (pairs, rates, weight, wide, guide, mix, bias, twin_cot),
         scratch=(
-            pltpu.VMEM((bins + 2 * PAD, LANES), f32),
-            pltpu.VMEM((5, 2 * extended, LANES), bf16),
             pltpu.VMEM((2, 2 * extended, 2 * LANES), f32),
             pltpu.VMEM((2 * spots, LANES), f32),
             pltpu.VMEM((2 * spots, LANES), bf16),
@@ -413,8 +453,9 @@
             pltpu.VMEM((bins + 2 * PAD, LANES), f32),
             pltpu.VMEM((taps_rows, LANES), f32),
             pltpu.VMEM((maps * rows, cols), f32),
+            pltpu.VMEM((2 * rows + cols, 3 * LANES), bf16),
         ),
-        limit=44,
+        limit=40,
         flops=20_000_000_000,
     )
 

time: 33.7 us -> 33.6 us (level)
  Pallas kernels: 10.5 us -> 11.4 us
  waiting for transfers between devices: 7.97 us -> 7.47 us
  local copies, waits for them, and re-layouts: 1.23 us -> 0.76 us
    pallas_call x4 -> x5, Pallas kernels: 10.5 us -> 11.4 us  [call(): pl.pallas_call(body, out_shape=out_shape, in_specs=specs or [vmem] * len(...]
    ppermute x10, waiting for transfers between devices: 7.97 us -> 7.47 us  [swap(): return lax.ppermute(value, axis, [(i, i ^ mask) for i in range(peers)])]
    unnamed x2, local copies, waits for them, and re-layouts: 0.48 us -> 0.01 us
  transfers between devices with their start and end apart: 10 -> 10, of which waited for: 6 -> 6; matrix products, arithmetic and copies ran while one was open for 2% -> 2% of each run, Pallas kernels for 7% -> 10%
where the time goes in v6:
time: 33.6 us; the launch traced here: 33.4 us
  starting transfers between devices  13 us (39%)
  Pallas kernels  11.4 us (34%)
  waiting for transfers between devices  7.47 us (22%)
  local copies, waits for them, and re-layouts  0.76 us (2%)
  between operations  0.75 us (2%)
    ppermute x10, starting transfers between devices, swap(): return lax.ppermute(value, axis, [(i, i ^ mask) for i in range(peers)])  13 us
    pallas_call x5, Pallas kernels, call(): pl.pallas_call(body, out_shape=out_shape, in_specs=specs or [vmem] * len(...  11.4 us
    ppermute x10, waiting for transfers between devices, swap(): return lax.ppermute(value, axis, [(i, i ^ mask) for i in range(peers)])  7.47 us
    reshape x1, local copies, waits for them, and re-layouts, per_device(): contact = call(contact_kernel, 'contact', shape((maps, spots), f32), (mix...  0.73 us
  transfers between devices with their start and end apart: 10, of which 6 were waited for; matrix products, arithmetic and copies ran while one was open for 2% of the time, Pallas kernels for 10%

profile of v6, /device:TPU:0, one launch (start us, length us, event | category | flops | bytes accessed | tf_op | source)
XLA Modules:
  0.0 33.4 jit_solution(17522536467077132054)
XLA Ops:
  0.6 3.0 %collective-permute-start = (bf16[64,128]{1,0:T(8,128)(2,1)}, bf16[64,128]{1,0:T(8,128)(2,1)S(1)}, u32[]{:S(2)}, u32[]{:S(2)}) collective-permute-start(bf16[64,128]{1,0:T(8,128)(2,1)} %embedding_hbm.1), channel_id=1, source_target_pairs={{0,1},{1,0},{2,3},{3,2},{4,5},{5,4},{6,7},{7,6},{8,9},{9,8},{10,11... | collective-permute-start | bytes 49160 | tf_op jit(solution)/shard_map/ppermute | solution.py:362
  3.7 1.5 %collective-permute-start.2 = (bf16[64,128]{1,0:T(8,128)(2,1)}, bf16[64,128]{1,0:T(8,128)(2,1)S(1)}, u32[]{:S(2)}, u32[]{:S(2)}) collective-permute-start(bf16[64,128]{1,0:T(8,128)(2,1)} %embedding_hbm.1), channel_id=1, source_target_pairs={{0,3},{1,2},{2,1},{3,0},{4,7},{5,6},{6,5},{7,4},{8,11},{9,10},{10,... | collective-permute-start | bytes 49160 | tf_op jit(solution)/shard_map/ppermute | solution.py:362
  5.2 0.0 collective-permute-start.1
  5.2 3.0 %collective-permute-start.3 = (bf16[5,32,64]{2,1,0:T(8,128)(2,1)}, bf16[5,32,64]{2,1,0:T(8,128)(2,1)S(1)}, u32[]{:S(2)}, u32[]{:S(2)}) collective-permute-start(bf16[5,32,64]{2,1,0:T(8,128)(2,1)} %cot_hbm.1), channel_id=1, source_target_pairs={{0,16},{4,20},{8,24},{12,28},{16,0},{20,4},{24,8},{28,12},{1,17},{... | collective-permute-start | bytes 61448 | tf_op jit(solution)/shard_map/ppermute | solution.py:362
  8.3 1.5 %prepare.1 = (bf16[64,128]{1,0:T(8,128)(2,1)S(1)}, s32[16,128]{1,0:T(8,128)S(1)}, bf16[2,256,384]{2,1,0:T(8,128)(2,1)S(1)}, bf16[384,768]{1,0:T(8,128)(2,1)S(1)}...) custom-call(bf16[64,128]{1,0:T(8,128)(2,1)} %embedding_hbm.1, s32[2]{0:T(128)} %dilation_hbm.1, ...), custom_call_target="tpu_custom_call" | custom-call | flops 4000000000 | bytes 1000 | tf_op jit(solution)/shard_map/prepare/pallas_call | solution.py:384
  9.8 0.0 collective-permute-done.refs_1_
  9.8 0.0 collective-permute-done.2.refs_3_
  9.8 0.0 collective-permute-done.1.refs_2_
  9.8 1.2 %pairs.1.refs_0_ = bf16[5,5120,128]{2,1,0:T(8,128)(2,1)S(1)} custom-call(bf16[64,128]{1,0:T(8,128)(2,1)S(1)} %get-tuple-element.17.refs_0_, bf16[64,128]{1,0:T(8,128)(2,1)S(1)} %collective-permute-done.refs_1_, bf16[64,128]{1,0:T(8,128)(2,1)S(1)} %collective-permute-done.1.refs_2_, bf16[64,128]{1,0:T(8,128)(2,1)S(1)} %collective-permute-done.2.refs_3_, ...), custom_call_target="tpu_custom_call" | custom-call | flops 3000000000 | bytes 1000 | tf_op jit(solution)/shard_map/pairs/pallas_call | solution.py:384
  10.9 0.0 collective-permute-done.3.refs_7_
  11.0 0.0 copy-start
  11.0 7.2 %contact_head.1 = (bf16[4096,128]{1,0:T(8,128)(2,1)S(1)}, bf16[352,128]{1,0:T(8,128)(2,1)S(1)}, bf16[352,128]{1,0:T(8,128)(2,1)S(1)}) custom-call(bf16[5,5120,128]{2,1,0:T(8,128)(2,1)S(1)} %pairs.1.refs_0_, s32[16,128]{1,0:T(8,128)S(1)} %get-tuple-element.18.refs_4_.refs_1_, bf16[2,256,384]{2,1,0:T(8,128)(2,1)S(1)} %get-tuple-element.19.refs_2_, ...), custom_call_target="tpu_custom_call" | custom-call | flops 20000000000 | bytes 1000 | tf_op jit(solution)/shard_map/contact_head/pallas_call | solution.py:384
  18.2 0.1 collective-permute-start.4
  18.3 1.3 %collective-permute-done.4 = bf16[352,128]{1,0:T(8,128)(2,1)S(1)} collective-permute-done((bf16[352,128]{1,0:T(8,128)(2,1)S(1)}, bf16[352,128]{1,0:T(8,128)(2,1)S(1)}, u32[]{:S(2)}, u32[]{:S(2)}) %collective-permute-start.4) | collective-permute-done | bytes 90144 | tf_op jit(solution)/shard_map/ppermute | solution.py:362
  19.6 2.5 %collective-permute-start.7 = (bf16[256,128]{1,0:T(8,128)(2,1)S(1)}, bf16[256,128]{1,0:T(8,128)(2,1)S(1)}, u32[]{:S(2)}, u32[]{:S(2)}) collective-permute-start(bf16[256,128]{1,0:T(8,128)(2,1)S(1)} %concatenate.16), channel_id=1, source_target_pairs={{0,3},{1,2},{2,1},{3,0},{4,7},{5,6},{6,5},{7,4},{8,11},{9,10},{10,... | collective-permute-start | bytes 196616 | tf_op jit(solution)/shard_map/ppermute | solution.py:362
  22.1 0.6 %collective-permute-start.5 = (bf16[256,128]{1,0:T(8,128)(2,1)S(1)}, bf16[256,128]{1,0:T(8,128)(2,1)S(1)}, u32[]{:S(2)}, u32[]{:S(2)}) collective-permute-start(bf16[256,128]{1,0:T(8,128)(2,1)S(1)} %get-tuple-element.34), channel_id=1, source_target_pairs={{0,1},{1,0},{2,3},{3,2},{4,5},{5,4},{6,7},{7,6},{8,9},{9,8},{10,11... | collective-permute-start | bytes 196616 | tf_op jit(solution)/shard_map/ppermute | solution.py:362
  22.7 0.5 %collective-permute-start.6 = (bf16[256,128]{1,0:T(8,128)(2,1)S(1)}, bf16[256,128]{1,0:T(8,128)(2,1)S(1)}, u32[]{:S(2)}, u32[]{:S(2)}) collective-permute-start(bf16[256,128]{1,0:T(8,128)(2,1)S(1)} %get-tuple-element.35), channel_id=1, source_target_pairs={{0,2},{1,3},{2,0},{3,1},{4,6},{5,7},{6,4},{7,5},{8,10},{9,11},{10,... | collective-permute-start | bytes 196616 | tf_op jit(solution)/shard_map/ppermute | solution.py:362
  23.2 0.0 copy-done
  23.2 0.8 %contact.1 = f32[5,2048]{1,0:T(8,128)S(1)} custom-call(f32[5]{0:T(128)S(1)} %copy-done, f32[16,128]{1,0:T(8,128)S(1)} %get-tuple-element.22.refs_5_.mix_ref, bf16[4096,128]{1,0:T(8,128)(2,1)S(1)} %get-tuple-element.26.active_ref), custom_call_target="tpu_custom_call" | custom-call | flops 1000000000 | bytes 1000 | tf_op jit(solution)/shard_map/contact/pallas_call | solution.py:384
  24.0 0.7 %reshape.16 = f32[5,32,64]{2,1,0:T(8,128)} reshape(f32[5,2048]{1,0:T(8,128)S(1)} %contact.1) | data formatting | bytes 81920 | tf_op jit(solution)/shard_map/reshape | solution.py:487
  24.8 0.3 collective-permute-done.7
  25.1 1.4 %collective-permute-done.5 = bf16[256,128]{1,0:T(8,128)(2,1)S(1)} collective-permute-done((bf16[256,128]{1,0:T(8,128)(2,1)S(1)}, bf16[256,128]{1,0:T(8,128)(2,1)S(1)}, u32[]{:S(2)}, u32[]{:S(2)}) %collective-permute-start.5) | collective-permute-done | bytes 65568 | tf_op jit(solution)/shard_map/ppermute | solution.py:362
  26.5 0.5 %collective-permute-done.6 = bf16[256,128]{1,0:T(8,128)(2,1)S(1)} collective-permute-done((bf16[256,128]{1,0:T(8,128)(2,1)S(1)}, bf16[256,128]{1,0:T(8,128)(2,1)S(1)}, u32[]{:S(2)}, u32[]{:S(2)}) %collective-permute-start.6) | collective-permute-done | bytes 65568 | tf_op jit(solution)/shard_map/ppermute | solution.py:362
  27.1 1.6 %collective-permute-start.8 = (bf16[256,128]{1,0:T(8,128)(2,1)S(1)}, bf16[256,128]{1,0:T(8,128)(2,1)S(1)}, u32[]{:S(2)}, u32[]{:S(2)}) collective-permute-start(bf16[256,128]{1,0:T(8,128)(2,1)S(1)} %add_convert_fusion), channel_id=1, source_target_pairs={{0,8},{4,12},{8,0},{12,4},{16,24},{20,28},{24,16},{28,20},{1,9},{5... | collective-permute-start | bytes 196616 | tf_op jit(solution)/shard_map/ppermute | solution.py:362
  28.7 2.7 %collective-permute-done.8 = bf16[256,128]{1,0:T(8,128)(2,1)S(1)} collective-permute-done((bf16[256,128]{1,0:T(8,128)(2,1)S(1)}, bf16[256,128]{1,0:T(8,128)(2,1)S(1)}, u32[]{:S(2)}, u32[]{:S(2)}) %collective-permute-start.8) | collective-permute-done | bytes 65568 | tf_op jit(solution)/shard_map/ppermute | solution.py:362
  31.4 0.1 collective-permute-start.9
  31.5 1.2 %collective-permute-done.9.other_ref = bf16[256,128]{1,0:T(8,128)(2,1)S(1)} collective-permute-done((bf16[256,128]{1,0:T(8,128)(2,1)S(1)}, bf16[256,128]{1,0:T(8,128)(2,1)S(1)}, u32[]{:S(2)}, u32[]{:S(2)}) %collective-permute-start.9) | collective-permute-done | bytes 65568 | tf_op jit(solution)/shard_map/ppermute | solution.py:362
  32.7 0.7 %join.1 = (f32[64,128]{1,0:T(8,128)}, f32[432,128]{1,0:T(8,128)}) custom-call(bf16[256,128]{1,0:T(8,128)(2,1)S(1)} %add.19.mine_ref, bf16[256,128]{1,0:T(8,128)(2,1)S(1)} %collective-permute-done.9.other_ref), custom_call_target="tpu_custom_call" | custom-call | flops 1000 | bytes 1000 | tf_op jit(solution)/shard_map/join/pallas_call | solution.py:384
  (7 shorter events, 0.1 us)
Async XLA Ops:
  0.6 9.1 %collective-permute-start = (bf16[64,128]{1,0:T(8,128)(2,1)}, bf16[64,128]{1,0:T(8,128)(2,1)S(1)}, u32[]{:S(2)}, u32[]{:S(2)}) collective-permute-start(bf16[64,128]{1,0:T(8,128)(2,1)} %embedding_hbm.1), channel_id=1, source_target_pairs={{0,1},{1,0},{2,3},{3,2},{4,5},{5,4},{6,7},{7,6},{8,9},{9,8},{10,11... | collective-permute-start | bytes 49160 | tf_op jit(solution)/shard_map/ppermute | solution.py:362
  3.7 6.1 %collective-permute-start.2 = (bf16[64,128]{1,0:T(8,128)(2,1)}, bf16[64,128]{1,0:T(8,128)(2,1)S(1)}, u32[]{:S(2)}, u32[]{:S(2)}) collective-permute-start(bf16[64,128]{1,0:T(8,128)(2,1)} %embedding_hbm.1), channel_id=1, source_target_pairs={{0,3},{1,2},{2,1},{3,0},{4,7},{5,6},{6,5},{7,4},{8,11},{9,10},{10,... | collective-permute-start | bytes 49160 | tf_op jit(solution)/shard_map/ppermute | solution.py:362
  5.2 4.6 %collective-permute-start.1 = (bf16[64,128]{1,0:T(8,128)(2,1)}, bf16[64,128]{1,0:T(8,128)(2,1)S(1)}, u32[]{:S(2)}, u32[]{:S(2)}) collective-permute-start(bf16[64,128]{1,0:T(8,128)(2,1)} %embedding_hbm.1), channel_id=1, source_target_pairs={{0,2},{1,3},{2,0},{3,1},{4,6},{5,7},{6,4},{7,5},{8,10},{9,11},{10,... | collective-permute-start | bytes 49160 | tf_op jit(solution)/shard_map/ppermute | solution.py:362
  5.2 5.7 %collective-permute-start.3 = (bf16[5,32,64]{2,1,0:T(8,128)(2,1)}, bf16[5,32,64]{2,1,0:T(8,128)(2,1)S(1)}, u32[]{:S(2)}, u32[]{:S(2)}) collective-permute-start(bf16[5,32,64]{2,1,0:T(8,128)(2,1)} %cot_hbm.1), channel_id=1, source_target_pairs={{0,16},{4,20},{8,24},{12,28},{16,0},{20,4},{24,8},{28,12},{1,17},{... | collective-permute-start | bytes 61448 | tf_op jit(solution)/shard_map/ppermute | solution.py:362
  11.0 12.3 %copy-start = (f32[5]{0:T(128)S(1)}, f32[5]{0:T(128)}, u32[]{:S(2)}) copy-start(f32[5]{0:T(128)} %mix_bias_ref.1) | copy-start | bytes 64
  18.2 1.4 %collective-permute-start.4 = (bf16[352,128]{1,0:T(8,128)(2,1)S(1)}, bf16[352,128]{1,0:T(8,128)(2,1)S(1)}, u32[]{:S(2)}, u32[]{:S(2)}) collective-permute-start(bf16[352,128]{1,0:T(8,128)(2,1)S(1)} %get-tuple-element.25), channel_id=1, source_target_pairs={{0,4},{4,0},{8,12},{12,8},{16,20},{20,16},{24,28},{28,24},{1,5},{5... | collective-permute-start | bytes 270344 | tf_op jit(solution)/shard_map/ppermute | solution.py:362
  19.6 5.4 %collective-permute-start.7 = (bf16[256,128]{1,0:T(8,128)(2,1)S(1)}, bf16[256,128]{1,0:T(8,128)(2,1)S(1)}, u32[]{:S(2)}, u32[]{:S(2)}) collective-permute-start(bf16[256,128]{1,0:T(8,128)(2,1)S(1)} %concatenate.16), channel_id=1, source_target_pairs={{0,3},{1,2},{2,1},{3,0},{4,7},{5,6},{6,5},{7,4},{8,11},{9,10},{10,... | collective-permute-start | bytes 196616 | tf_op jit(solution)/shard_map/ppermute | solution.py:362
  22.1 4.3 %collective-permute-start.5 = (bf16[256,128]{1,0:T(8,128)(2,1)S(1)}, bf16[256,128]{1,0:T(8,128)(2,1)S(1)}, u32[]{:S(2)}, u32[]{:S(2)}) collective-permute-start(bf16[256,128]{1,0:T(8,128)(2,1)S(1)} %get-tuple-element.34), channel_id=1, source_target_pairs={{0,1},{1,0},{2,3},{3,2},{4,5},{5,4},{6,7},{7,6},{8,9},{9,8},{10,11... | collective-permute-start | bytes 196616 | tf_op jit(solution)/shard_map/ppermute | solution.py:362
  22.7 4.3 %collective-permute-start.6 = (bf16[256,128]{1,0:T(8,128)(2,1)S(1)}, bf16[256,128]{1,0:T(8,128)(2,1)S(1)}, u32[]{:S(2)}, u32[]{:S(2)}) collective-permute-start(bf16[256,128]{1,0:T(8,128)(2,1)S(1)} %get-tuple-element.35), channel_id=1, source_target_pairs={{0,2},{1,3},{2,0},{3,1},{4,6},{5,7},{6,4},{7,5},{8,10},{9,11},{10,... | collective-permute-start | bytes 196616 | tf_op jit(solution)/shard_map/ppermute | solution.py:362
  27.1 4.3 %collective-permute-start.8 = (bf16[256,128]{1,0:T(8,128)(2,1)S(1)}, bf16[256,128]{1,0:T(8,128)(2,1)S(1)}, u32[]{:S(2)}, u32[]{:S(2)}) collective-permute-start(bf16[256,128]{1,0:T(8,128)(2,1)S(1)} %add_convert_fusion), channel_id=1, source_target_pairs={{0,8},{4,12},{8,0},{12,4},{16,24},{20,28},{24,16},{28,20},{1,9},{5... | collective-permute-start | bytes 196616 | tf_op jit(solution)/shard_map/ppermute | solution.py:362
  31.4 1.3 %collective-permute-start.9 = (bf16[256,128]{1,0:T(8,128)(2,1)S(1)}, bf16[256,128]{1,0:T(8,128)(2,1)S(1)}, u32[]{:S(2)}, u32[]{:S(2)}) collective-permute-start(bf16[256,128]{1,0:T(8,128)(2,1)S(1)} %add.19.mine_ref), channel_id=1, source_target_pairs={{0,4},{4,0},{8,12},{12,8},{16,20},{20,16},{24,28},{28,24},{1,5},{5... | collective-permute-start | bytes 196616 | tf_op jit(solution)/shard_map/ppermute | solution.py:362

commit v7 on v6

--- a/solution.py
+++ b/solution.py
@@ -9,6 +9,7 @@
 
 DMAX = 4
 PAD = 8
+TWIN = 2
 STEPS = (-1, 0, 1)
 TAPS = [(a, b) for a in STEPS for b in STEPS]
 LANES = 128
@@ -112,7 +113,7 @@
 def contact_kernel(mix_bias_ref, mix_ref, active_ref, contact_ref):
     mix = mix_ref[...].astype(jnp.bfloat16)
     maps, spots = contact_ref.shape
-    upper = lax.axis_index("row") // (lax.axis_size("row") // 2)
+    upper = upper_twin()
     mine = pl.ds(pl.multiple_of(upper * spots, spots), spots)
     mixed = contract(mix, active_ref[mine, :], ((1,), (1,)))
     which = lax.broadcasted_iota(jnp.int32, (8, 1), 0)
@@ -122,10 +123,14 @@
     contact_ref[...] = (mixed[0:8] + offset)[0:maps]
 
 
+def upper_twin():
+    return lax.rem(lax.axis_index("row") // TWIN, 2)
+
+
 def row_blocks(rows):
-    split = lax.axis_size("row") // 2
-    lower = lax.rem(lax.axis_index("row"), split)
-    return [lower * rows, (lower + split) * rows]
+    row_index = lax.axis_index("row")
+    lower = row_index - TWIN * upper_twin()
+    return [lower * rows, (lower + TWIN) * rows]
 
 
 def pairs_kernel(sizes, *refs):
@@ -186,7 +191,7 @@
     row_index = lax.axis_index("row")
     col_index = lax.axis_index("col")
     row_starts = row_blocks(rows)
-    upper = row_index // (lax.axis_size("row") // 2)
+    upper = upper_twin()
     col_start = col_index * cols
     core = lax.rem(row_index, 2)
     count = len(TAPS)
@@ -370,7 +375,7 @@
     peers = lax.axis_size("col")
     row_peers = lax.axis_size("row")
     bins = cols * peers
-    twin_cot = swap(cotangent, "row", row_peers // 2)
+    twin_cot = swap(cotangent, "row", TWIN)
     blocks = [swap(embedding, "col", mask) for mask in range(peers - 1, 0, -1)]
     taps = len(TAPS)
     taps_rows = taps * filters
@@ -486,8 +491,8 @@
         flops=1_000_000_000,
     ).reshape(maps, rows, cols)
     total, contact = lax.optimization_barrier((total, contact))
-    mask = 2
-    while mask < row_peers // 2:
+    mask = 2 * TWIN
+    while mask < row_peers:
         total = total + swap(total, "row", mask)
         mask *= 2
     other = swap(total, "row", 1)

time: 33.6 us -> 33.5 us (level)
  transfers between devices with their start and end apart: 10 -> 10, of which waited for: 6 -> 7; matrix products, arithmetic and copies ran while one was open for 2% -> 2% of each run, Pallas kernels for 10% -> 10%
where the time goes in v7:
time: 33.5 us; the launch traced here: 33.3 us
  starting transfers between devices  13 us (39%)
  Pallas kernels  11.3 us (34%)
  waiting for transfers between devices  7.33 us (22%)
  local copies, waits for them, and re-layouts  0.76 us (2%)
  between operations  0.74 us (2%)
    ppermute x10, starting transfers between devices, swap(): return lax.ppermute(value, axis, [(i, i ^ mask) for i in range(peers)])  13 us
    pallas_call x5, Pallas kernels, call(): pl.pallas_call(body, out_shape=out_shape, in_specs=specs or [vmem] * len(...  11.3 us
    ppermute x10, waiting for transfers between devices, swap(): return lax.ppermute(value, axis, [(i, i ^ mask) for i in range(peers)])  7.33 us
    reshape x1, local copies, waits for them, and re-layouts, per_device(): contact = call(contact_kernel, 'contact', shape((maps, spots), f32), (mix...  0.73 us
  transfers between devices with their start and end apart: 10, of which 7 were waited for; matrix products, arithmetic and copies ran while one was open for 2% of the time, Pallas kernels for 10%

profile of v7, /device:TPU:0, one launch (start us, length us, event | category | flops | bytes accessed | tf_op | source)
XLA Modules:
  0.0 33.3 jit_solution(16149927753919635812)
XLA Ops:
  0.6 3.0 %collective-permute-start = (bf16[64,128]{1,0:T(8,128)(2,1)}, bf16[64,128]{1,0:T(8,128)(2,1)S(1)}, u32[]{:S(2)}, u32[]{:S(2)}) collective-permute-start(bf16[64,128]{1,0:T(8,128)(2,1)} %embedding_hbm.1), channel_id=1, source_target_pairs={{0,1},{1,0},{2,3},{3,2},{4,5},{5,4},{6,7},{7,6},{8,9},{9,8},{10,11... | collective-permute-start | bytes 49160 | tf_op jit(solution)/shard_map/ppermute | solution.py:367
  3.7 1.5 %collective-permute-start.2 = (bf16[64,128]{1,0:T(8,128)(2,1)}, bf16[64,128]{1,0:T(8,128)(2,1)S(1)}, u32[]{:S(2)}, u32[]{:S(2)}) collective-permute-start(bf16[64,128]{1,0:T(8,128)(2,1)} %embedding_hbm.1), channel_id=1, source_target_pairs={{0,3},{1,2},{2,1},{3,0},{4,7},{5,6},{6,5},{7,4},{8,11},{9,10},{10,... | collective-permute-start | bytes 49160 | tf_op jit(solution)/shard_map/ppermute | solution.py:367
  5.2 0.0 collective-permute-start.1
  5.2 2.0 %collective-permute-start.3 = (bf16[5,32,64]{2,1,0:T(8,128)(2,1)}, bf16[5,32,64]{2,1,0:T(8,128)(2,1)S(1)}, u32[]{:S(2)}, u32[]{:S(2)}) collective-permute-start(bf16[5,32,64]{2,1,0:T(8,128)(2,1)} %cot_hbm.1), channel_id=1, source_target_pairs={{0,8},{4,12},{8,0},{12,4},{16,24},{20,28},{24,16},{28,20},{1,9},{5... | collective-permute-start | bytes 61448 | tf_op jit(solution)/shard_map/ppermute | solution.py:367
  7.2 1.5 %prepare.1 = (bf16[64,128]{1,0:T(8,128)(2,1)S(1)}, s32[16,128]{1,0:T(8,128)S(1)}, bf16[2,256,384]{2,1,0:T(8,128)(2,1)S(1)}, bf16[384,768]{1,0:T(8,128)(2,1)S(1)}...) custom-call(bf16[64,128]{1,0:T(8,128)(2,1)} %embedding_hbm.1, s32[2]{0:T(128)} %dilation_hbm.1, ...), custom_call_target="tpu_custom_call" | custom-call | flops 4000000000 | bytes 1000 | tf_op jit(solution)/shard_map/prepare/pallas_call | solution.py:389
  8.7 0.0 collective-permute-done.refs_1_
  8.8 0.0 collective-permute-done.2.refs_3_
  8.8 0.3 %collective-permute-done.1.refs_2_ = bf16[64,128]{1,0:T(8,128)(2,1)S(1)} collective-permute-done((bf16[64,128]{1,0:T(8,128)(2,1)}, bf16[64,128]{1,0:T(8,128)(2,1)S(1)}, u32[]{:S(2)}, u32[]{:S(2)}) %collective-permute-start.1) | collective-permute-done | bytes 16416 | tf_op jit(solution)/shard_map/ppermute | solution.py:367
  9.1 1.1 %pairs.1.refs_0_ = bf16[5,5120,128]{2,1,0:T(8,128)(2,1)S(1)} custom-call(bf16[64,128]{1,0:T(8,128)(2,1)S(1)} %get-tuple-element.17.refs_0_, bf16[64,128]{1,0:T(8,128)(2,1)S(1)} %collective-permute-done.refs_1_, bf16[64,128]{1,0:T(8,128)(2,1)S(1)} %collective-permute-done.1.refs_2_, bf16[64,128]{1,0:T(8,128)(2,1)S(1)} %collective-permute-done.2.refs_3_, ...), custom_call_target="tpu_custom_call" | custom-call | flops 3000000000 | bytes 1000 | tf_op jit(solution)/shard_map/pairs/pallas_call | solution.py:389
  10.3 0.0 collective-permute-done.3.refs_7_
  10.3 0.0 copy-start
  10.3 7.2 %contact_head.1 = (bf16[4096,128]{1,0:T(8,128)(2,1)S(1)}, bf16[352,128]{1,0:T(8,128)(2,1)S(1)}, bf16[352,128]{1,0:T(8,128)(2,1)S(1)}) custom-call(bf16[5,5120,128]{2,1,0:T(8,128)(2,1)S(1)} %pairs.1.refs_0_, s32[16,128]{1,0:T(8,128)S(1)} %get-tuple-element.18.refs_4_.refs_1_, bf16[2,256,384]{2,1,0:T(8,128)(2,1)S(1)} %get-tuple-element.19.refs_2_, ...), custom_call_target="tpu_custom_call" | custom-call | flops 20000000000 | bytes 1000 | tf_op jit(solution)/shard_map/contact_head/pallas_call | solution.py:389
  17.5 0.1 collective-permute-start.4
  17.6 1.3 %collective-permute-done.4 = bf16[352,128]{1,0:T(8,128)(2,1)S(1)} collective-permute-done((bf16[352,128]{1,0:T(8,128)(2,1)S(1)}, bf16[352,128]{1,0:T(8,128)(2,1)S(1)}, u32[]{:S(2)}, u32[]{:S(2)}) %collective-permute-start.4) | collective-permute-done | bytes 90144 | tf_op jit(solution)/shard_map/ppermute | solution.py:367
  18.9 2.2 %collective-permute-start.7 = (bf16[256,128]{1,0:T(8,128)(2,1)S(1)}, bf16[256,128]{1,0:T(8,128)(2,1)S(1)}, u32[]{:S(2)}, u32[]{:S(2)}) collective-permute-start(bf16[256,128]{1,0:T(8,128)(2,1)S(1)} %concatenate.16), channel_id=1, source_target_pairs={{0,3},{1,2},{2,1},{3,0},{4,7},{5,6},{6,5},{7,4},{8,11},{9,10},{10,... | collective-permute-start | bytes 196616 | tf_op jit(solution)/shard_map/ppermute | solution.py:367
  21.1 0.6 %collective-permute-start.5 = (bf16[256,128]{1,0:T(8,128)(2,1)S(1)}, bf16[256,128]{1,0:T(8,128)(2,1)S(1)}, u32[]{:S(2)}, u32[]{:S(2)}) collective-permute-start(bf16[256,128]{1,0:T(8,128)(2,1)S(1)} %get-tuple-element.34), channel_id=1, source_target_pairs={{0,1},{1,0},{2,3},{3,2},{4,5},{5,4},{6,7},{7,6},{8,9},{9,8},{10,11... | collective-permute-start | bytes 196616 | tf_op jit(solution)/shard_map/ppermute | solution.py:367
  21.7 0.8 %collective-permute-start.6 = (bf16[256,128]{1,0:T(8,128)(2,1)S(1)}, bf16[256,128]{1,0:T(8,128)(2,1)S(1)}, u32[]{:S(2)}, u32[]{:S(2)}) collective-permute-start(bf16[256,128]{1,0:T(8,128)(2,1)S(1)} %get-tuple-element.35), channel_id=1, source_target_pairs={{0,2},{1,3},{2,0},{3,1},{4,6},{5,7},{6,4},{7,5},{8,10},{9,11},{10,... | collective-permute-start | bytes 196616 | tf_op jit(solution)/shard_map/ppermute | solution.py:367
  22.5 0.0 copy-done
  22.5 0.8 %contact.1 = f32[5,2048]{1,0:T(8,128)S(1)} custom-call(f32[5]{0:T(128)S(1)} %copy-done, f32[16,128]{1,0:T(8,128)S(1)} %get-tuple-element.22.refs_5_.mix_ref, bf16[4096,128]{1,0:T(8,128)(2,1)S(1)} %get-tuple-element.26.active_ref), custom_call_target="tpu_custom_call" | custom-call | flops 1000000000 | bytes 1000 | tf_op jit(solution)/shard_map/contact/pallas_call | solution.py:389
  23.3 0.7 %reshape.16 = f32[5,32,64]{2,1,0:T(8,128)} reshape(f32[5,2048]{1,0:T(8,128)S(1)} %contact.1) | data formatting | bytes 81920 | tf_op jit(solution)/shard_map/reshape | solution.py:492
  24.1 0.3 collective-permute-done.7
  24.4 1.1 %collective-permute-done.5 = bf16[256,128]{1,0:T(8,128)(2,1)S(1)} collective-permute-done((bf16[256,128]{1,0:T(8,128)(2,1)S(1)}, bf16[256,128]{1,0:T(8,128)(2,1)S(1)}, u32[]{:S(2)}, u32[]{:S(2)}) %collective-permute-start.5) | collective-permute-done | bytes 65568 | tf_op jit(solution)/shard_map/ppermute | solution.py:367
  25.4 0.5 %collective-permute-done.6 = bf16[256,128]{1,0:T(8,128)(2,1)S(1)} collective-permute-done((bf16[256,128]{1,0:T(8,128)(2,1)S(1)}, bf16[256,128]{1,0:T(8,128)(2,1)S(1)}, u32[]{:S(2)}, u32[]{:S(2)}) %collective-permute-start.6) | collective-permute-done | bytes 65568 | tf_op jit(solution)/shard_map/ppermute | solution.py:367
  26.0 2.7 %collective-permute-start.8 = (bf16[256,128]{1,0:T(8,128)(2,1)S(1)}, bf16[256,128]{1,0:T(8,128)(2,1)S(1)}, u32[]{:S(2)}, u32[]{:S(2)}) collective-permute-start(bf16[256,128]{1,0:T(8,128)(2,1)S(1)} %add_convert_fusion), channel_id=1, source_target_pairs={{0,16},{4,20},{8,24},{12,28},{16,0},{20,4},{24,8},{28,12},{1,17},{... | collective-permute-start | bytes 196616 | tf_op jit(solution)/shard_map/ppermute | solution.py:367
  28.7 2.6 %collective-permute-done.8 = bf16[256,128]{1,0:T(8,128)(2,1)S(1)} collective-permute-done((bf16[256,128]{1,0:T(8,128)(2,1)S(1)}, bf16[256,128]{1,0:T(8,128)(2,1)S(1)}, u32[]{:S(2)}, u32[]{:S(2)}) %collective-permute-start.8) | collective-permute-done | bytes 65568 | tf_op jit(solution)/shard_map/ppermute | solution.py:367
  31.3 0.1 collective-permute-start.9
  31.3 1.2 %collective-permute-done.9.other_ref = bf16[256,128]{1,0:T(8,128)(2,1)S(1)} collective-permute-done((bf16[256,128]{1,0:T(8,128)(2,1)S(1)}, bf16[256,128]{1,0:T(8,128)(2,1)S(1)}, u32[]{:S(2)}, u32[]{:S(2)}) %collective-permute-start.9) | collective-permute-done | bytes 65568 | tf_op jit(solution)/shard_map/ppermute | solution.py:367
  32.6 0.7 %join.1 = (f32[64,128]{1,0:T(8,128)}, f32[432,128]{1,0:T(8,128)}) custom-call(bf16[256,128]{1,0:T(8,128)(2,1)S(1)} %add.19.mine_ref, bf16[256,128]{1,0:T(8,128)(2,1)S(1)} %collective-permute-done.9.other_ref), custom_call_target="tpu_custom_call" | custom-call | flops 1000 | bytes 1000 | tf_op jit(solution)/shard_map/join/pallas_call | solution.py:389
  (7 shorter events, 0.1 us)
Async XLA Ops:
  0.6 8.1 %collective-permute-start = (bf16[64,128]{1,0:T(8,128)(2,1)}, bf16[64,128]{1,0:T(8,128)(2,1)S(1)}, u32[]{:S(2)}, u32[]{:S(2)}) collective-permute-start(bf16[64,128]{1,0:T(8,128)(2,1)} %embedding_hbm.1), channel_id=1, source_target_pairs={{0,1},{1,0},{2,3},{3,2},{4,5},{5,4},{6,7},{7,6},{8,9},{9,8},{10,11... | collective-permute-start | bytes 49160 | tf_op jit(solution)/shard_map/ppermute | solution.py:367
  3.7 5.1 %collective-permute-start.2 = (bf16[64,128]{1,0:T(8,128)(2,1)}, bf16[64,128]{1,0:T(8,128)(2,1)S(1)}, u32[]{:S(2)}, u32[]{:S(2)}) collective-permute-start(bf16[64,128]{1,0:T(8,128)(2,1)} %embedding_hbm.1), channel_id=1, source_target_pairs={{0,3},{1,2},{2,1},{3,0},{4,7},{5,6},{6,5},{7,4},{8,11},{9,10},{10,... | collective-permute-start | bytes 49160 | tf_op jit(solution)/shard_map/ppermute | solution.py:367
  5.2 3.9 %collective-permute-start.1 = (bf16[64,128]{1,0:T(8,128)(2,1)}, bf16[64,128]{1,0:T(8,128)(2,1)S(1)}, u32[]{:S(2)}, u32[]{:S(2)}) collective-permute-start(bf16[64,128]{1,0:T(8,128)(2,1)} %embedding_hbm.1), channel_id=1, source_target_pairs={{0,2},{1,3},{2,0},{3,1},{4,6},{5,7},{6,4},{7,5},{8,10},{9,11},{10,... | collective-permute-start | bytes 49160 | tf_op jit(solution)/shard_map/ppermute | solution.py:367
  5.2 5.1 %collective-permute-start.3 = (bf16[5,32,64]{2,1,0:T(8,128)(2,1)}, bf16[5,32,64]{2,1,0:T(8,128)(2,1)S(1)}, u32[]{:S(2)}, u32[]{:S(2)}) collective-permute-start(bf16[5,32,64]{2,1,0:T(8,128)(2,1)} %cot_hbm.1), channel_id=1, source_target_pairs={{0,8},{4,12},{8,0},{12,4},{16,24},{20,28},{24,16},{28,20},{1,9},{5... | collective-permute-start | bytes 61448 | tf_op jit(solution)/shard_map/ppermute | solution.py:367
  10.3 12.3 %copy-start = (f32[5]{0:T(128)S(1)}, f32[5]{0:T(128)}, u32[]{:S(2)}) copy-start(f32[5]{0:T(128)} %mix_bias_ref.1) | copy-start | bytes 64
  17.5 1.4 %collective-permute-start.4 = (bf16[352,128]{1,0:T(8,128)(2,1)S(1)}, bf16[352,128]{1,0:T(8,128)(2,1)S(1)}, u32[]{:S(2)}, u32[]{:S(2)}) collective-permute-start(bf16[352,128]{1,0:T(8,128)(2,1)S(1)} %get-tuple-element.25), channel_id=1, source_target_pairs={{0,4},{4,0},{8,12},{12,8},{16,20},{20,16},{24,28},{28,24},{1,5},{5... | collective-permute-start | bytes 270344 | tf_op jit(solution)/shard_map/ppermute | solution.py:367
  18.9 5.4 %collective-permute-start.7 = (bf16[256,128]{1,0:T(8,128)(2,1)S(1)}, bf16[256,128]{1,0:T(8,128)(2,1)S(1)}, u32[]{:S(2)}, u32[]{:S(2)}) collective-permute-start(bf16[256,128]{1,0:T(8,128)(2,1)S(1)} %concatenate.16), channel_id=1, source_target_pairs={{0,3},{1,2},{2,1},{3,0},{4,7},{5,6},{6,5},{7,4},{8,11},{9,10},{10,... | collective-permute-start | bytes 196616 | tf_op jit(solution)/shard_map/ppermute | solution.py:367
  21.1 4.3 %collective-permute-start.5 = (bf16[256,128]{1,0:T(8,128)(2,1)S(1)}, bf16[256,128]{1,0:T(8,128)(2,1)S(1)}, u32[]{:S(2)}, u32[]{:S(2)}) collective-permute-start(bf16[256,128]{1,0:T(8,128)(2,1)S(1)} %get-tuple-element.34), channel_id=1, source_target_pairs={{0,1},{1,0},{2,3},{3,2},{4,5},{5,4},{6,7},{7,6},{8,9},{9,8},{10,11... | collective-permute-start | bytes 196616 | tf_op jit(solution)/shard_map/ppermute | solution.py:367
  21.7 4.3 %collective-permute-start.6 = (bf16[256,128]{1,0:T(8,128)(2,1)S(1)}, bf16[256,128]{1,0:T(8,128)(2,1)S(1)}, u32[]{:S(2)}, u32[]{:S(2)}) collective-permute-start(bf16[256,128]{1,0:T(8,128)(2,1)S(1)} %get-tuple-element.35), channel_id=1, source_target_pairs={{0,2},{1,3},{2,0},{3,1},{4,6},{5,7},{6,4},{7,5},{8,10},{9,11},{10,... | collective-permute-start | bytes 196616 | tf_op jit(solution)/shard_map/ppermute | solution.py:367
  26.0 5.2 %collective-permute-start.8 = (bf16[256,128]{1,0:T(8,128)(2,1)S(1)}, bf16[256,128]{1,0:T(8,128)(2,1)S(1)}, u32[]{:S(2)}, u32[]{:S(2)}) collective-permute-start(bf16[256,128]{1,0:T(8,128)(2,1)S(1)} %add_convert_fusion), channel_id=1, source_target_pairs={{0,16},{4,20},{8,24},{12,28},{16,0},{20,4},{24,8},{28,12},{1,17},{... | collective-permute-start | bytes 196616 | tf_op jit(solution)/shard_map/ppermute | solution.py:367
  31.3 1.3 %collective-permute-start.9 = (bf16[256,128]{1,0:T(8,128)(2,1)S(1)}, bf16[256,128]{1,0:T(8,128)(2,1)S(1)}, u32[]{:S(2)}, u32[]{:S(2)}) collective-permute-start(bf16[256,128]{1,0:T(8,128)(2,1)S(1)} %add.19.mine_ref), channel_id=1, source_target_pairs={{0,4},{4,0},{8,12},{12,8},{16,20},{20,16},{24,28},{28,24},{1,5},{5... | collective-permute-start | bytes 196616 | tf_op jit(solution)/shard_map/ppermute | solution.py:367
